TPU v7x, 32 devices: a whole 2x2x4 slice. The times are simulated.
32 devices in a mesh: ctx: 16 (over z, y, x), work: 2 (over core).
Axes of the slice: x: 2, y: 2, z: 4, core: 2. Of those that a mesh axis runs over, the one named last changes fastest.
Arguments:
- inputs: bfloat16 [2, 4096, 2880], P('work', 'ctx'), may hold values from -6 to 6
- queries: bfloat16 [2, 4096, 2048], P('work', 'ctx')
- keys: bfloat16 [2, 4096, 256], P('work', 'ctx')
- out_grad: bfloat16 [2, 4096, 2048], P('work', 'ctx'), may hold values from -6 to 6
- positions: int32 [2, 4096], P('work', 'ctx'), may hold values from 0 to 4095, as said below
- bands: int32 [32], replicated, may hold values from 32 to 128, as said below
- step: int32 [1], replicated, may hold values from 1 to 16
- value_weight: float32 [2, 2880, 256], P('work', 'ctx'), may hold values from -0.109375 to 0.109375
- moment_one: float32 [2, 2880, 256], P('work', 'ctx'), may hold values from -0.0078125 to 0.0078125
- moment_two: float32 [2, 2880, 256], P('work', 'ctx'), may hold values from 1e-08 to 1e-06
Outputs:
- attn_out: bfloat16 [2, 4096, 2048], P('work', 'ctx')
- mean_weight: float32 [2880, 256], P('ctx')
- mean_one: float32 [2880, 256], P('ctx')
- mean_two: float32 [2880, 256], P('ctx')
Inputs may be any that keep to these rules, and one draw needn't show every extreme that they name: `positions`: in each worker's sequence a token's position is 0 at the first token and at each document start, else one more than the previous token's. One worker's sequence is a single document. `bands`: one head has exactly 128.
All inputs are finite; a program needn't handle non-finite values.
Results may differ from a plain program's by a relative error of at most 0.0015.
The roundings to bfloat16 on the way count: a program that leaves them out, or rounds other values in their place, can miss the bound.
Values may be sent and summed in bfloat16 or wider, within the bound.
No kernel may reach another device: no remote copies, remote signals or barrier semaphores. Data moves between devices by JAX's collectives and lax.ppermute only.
A program may use at most 64 MiB of HBM per device.

v0:
```python
import jax
import jax.numpy as jnp
from jax import lax
from jax.sharding import PartitionSpec as P

HD = 64
QH = 32
KH = 4
LOOKBACK_SPAN = 128


beta_one = 0.9
beta_two = 0.95
adam_eps = 1e-08
learn_rate = 0.01
clip_norm = 0.5


def shifted(array, axis, by):
    devices = lax.axis_size(axis)
    pairs = [(i, i + by) for i in range(devices) if 0 <= i + by < devices]
    return lax.ppermute(array, axis, pairs)


def attend(qrows, krows, vrows, grows, bands, pos):
    count = qrows.shape[0]
    span = krows.shape[0]
    halo = span - count
    group = QH // KH
    dist = (
        lax.broadcasted_iota(jnp.int32, (count, span), 0)
        + halo
        - lax.broadcasted_iota(jnp.int32, (count, span), 1)
    )
    near = (dist >= 0) & (dist <= pos[:, None])
    outputs = []
    grads = []
    for head in range(KH):
        lo = head * group * HD
        hi = (head + 1) * group * HD
        query = qrows[:, lo:hi].reshape(count, group, HD)
        keyed = krows[:, head * HD : (head + 1) * HD]
        valued = vrows[:, head * HD : (head + 1) * HD]
        cotan = grows[:, lo:hi].reshape(count, group, HD)
        limit = bands[head * group : (head + 1) * group]
        allowed = near[None] & (dist[None] <= limit[:, None, None])
        scores = jnp.einsum(
            "qgd,kd->gqk", query, keyed, preferred_element_type=jnp.float32
        ) * HD ** (-0.5)
        scores = jnp.where(allowed, scores, -1e30)
        top = jnp.max(scores, axis=2, keepdims=True)
        expo = jnp.exp(scores - top)
        probs = (expo / jnp.sum(expo, axis=2, keepdims=True)).astype(jnp.bfloat16)
        outputs.append(
            jnp.einsum("gqk,kd->qgd", probs, valued, preferred_element_type=jnp.float32).reshape(
                count, group * HD
            )
        )
        grads.append(jnp.einsum("gqk,qgd->kd", probs, cotan, preferred_element_type=jnp.float32))
    return (jnp.concatenate(outputs, 1).astype(jnp.bfloat16), jnp.concatenate(grads, 1))


def per_device(
    inputs, queries, keys, out_grad, positions, bands, step, value_weight, moment_one, moment_two
):
    acts = inputs[0]
    rows = acts.shape[0]
    shard_rows = value_weight.shape[1]
    tokens_all = rows * lax.axis_size("ctx")
    weight = value_weight[0]
    columns = acts
    value_vectors = jnp.dot(
        columns,
        lax.all_gather(weight.astype(jnp.bfloat16), "ctx", axis=0, tiled=True),
        preferred_element_type=jnp.float32,
    ).astype(jnp.bfloat16)
    keyed = keys[0]
    prev_keys, prev_values = shifted(
        (keyed[rows - LOOKBACK_SPAN :], value_vectors[rows - LOOKBACK_SPAN :]), "ctx", 1
    )
    all_keys = jnp.concatenate([prev_keys, keyed], 0)
    all_values = jnp.concatenate([prev_values, value_vectors], 0)
    out, grad_rows = attend(queries[0], all_keys, all_values, out_grad[0], bands, positions[0])
    returned = shifted(grad_rows[:LOOKBACK_SPAN], "ctx", -1)
    own = grad_rows[LOOKBACK_SPAN:]
    own = jnp.concatenate([own[: rows - LOOKBACK_SPAN], own[rows - LOOKBACK_SPAN :] + returned], 0)
    value_grad = own.astype(jnp.bfloat16)
    columns = acts
    summed = (
        lax.psum(
            lax.dot_general(
                columns, value_grad, (((0,), (0,)), ((), ())), preferred_element_type=jnp.float32
            ),
            "ctx",
        )
        / tokens_all
    )
    norm = jnp.sqrt(jnp.sum(summed * summed))
    grad = lax.dynamic_slice_in_dim(summed, lax.axis_index("ctx") * shard_rows, shard_rows, 0)
    grad = grad * jnp.minimum(1.0, clip_norm / (norm + 1e-06))
    first = beta_one * moment_one[0] + (1.0 - beta_one) * grad
    second = beta_two * moment_two[0] + (1.0 - beta_two) * grad * grad
    count = step[0].astype(jnp.float32)
    fix_one = 1.0 - jnp.power(jnp.float32(beta_one), count)
    fix_two = 1.0 - jnp.power(jnp.float32(beta_two), count)
    updated = weight - learn_rate * (first / fix_one) / (jnp.sqrt(second / fix_two) + adam_eps)
    workers = lax.axis_size("work")
    mean_weight, mean_one, mean_two = lax.psum((updated, first, second), "work")
    return (out[None], mean_weight / workers, mean_one / workers, mean_two / workers)


def solution(mesh):
    in_specs = (
        P("work", "ctx", None),
        P("work", "ctx", None),
        P("work", "ctx", None),
        P("work", "ctx", None),
        P("work", "ctx"),
        P(),
        P(),
        P("work", "ctx", None),
        P("work", "ctx", None),
        P("work", "ctx", None),
    )
    out_specs = (P("work", "ctx", None), P("ctx", None), P("ctx", None), P("ctx", None))
    return jax.shard_map(
        per_device, mesh=mesh, in_specs=in_specs, out_specs=out_specs, check_vma=False
    )
```

profile of v0, /device:TPU:0, one launch (start us, length us, event | category | flops | bytes accessed | tf_op | source)
XLA Modules:
  0.0 256.4 jit_solution(12954597880343346058)
XLA Ops:
  7.2 1.7 copy.127
  9.0 1.0 copy.70
  10.1 0.7 slice_bitcast_fusion
  10.7 5.5 %collective-permute-start.1 = (bf16[128,256]{0,1:T(8,128)(2,1)}, bf16[128,256]{0,1:T(8,128)(2,1)}, u32[]{:S(2)}, u32[]{:S(2)}) collective-permute-start(bf16[128,256]{0,1:T(8,128)(2,1)} %slice_bitcast_fusion), channel_id=1, source_target_pairs={{0,2},{2,4},{4,6},{6,8},{8,10},{10,12},{12,14},{14,16},{16,18},{18... | collective-permute-start | bytes 196616 | tf_op jit(solution)/shard_map/ppermute | solution.py:22
  16.2 0.8 iota_subtract_fusion
  17.0 0.8 compare_and_fusion
  17.8 2.2 fusion.109
  20.0 0.9 fusion.108
  21.0 1.8 copy.72
  22.8 1.1 copy.81
  23.9 1.8 copy.78
  25.7 0.9 copy.75
  26.6 1.1 copy.89
  27.7 1.8 copy.95
  29.8 4.0 %fusion.115 = (f32[8,256]{1,0:T(8,128)S(1)}, f32[8,256,384]{1,2,0:T(8,128)}) fusion(s32[256,384]{0,1:T(8,128)S(1)} %copy-done.6, s32[8]{0:T(128)S(1)} %get-tuple-element.21, pred[256,384]{0,1:T(8,128)(4,1)S(1)} %compare_and_fusion, bf16[256,8,64]{0,2,1:T(8,128)(2,1)} %bitcast.165, bf16[256,256]{0,1:T(8,128)(2,1)S(1)} %bitcast.158, ...), kind=kOutput, calls=%fused_computation.139 | convolution fusion | flops 105480576 | bytes 4104224 | tf_op jit(solution)/shard_map/sub | solution.py:52
  33.8 2.2 divide_convert_fusion.2
  36.0 1.2 copy-done.2
  37.2 0.6 convolution_bitcast_fusion.3
  37.8 3.8 %fusion.112 = (f32[8,256]{1,0:T(8,128)S(1)}, f32[8,256,384]{1,2,0:T(8,128)}) fusion(s32[256,384]{0,1:T(8,128)S(1)} %copy-done.6, s32[8]{0:T(128)S(1)} %get-tuple-element.23, pred[256,384]{0,1:T(8,128)(4,1)S(1)} %copy-done.12, bf16[256,8,64]{0,2,1:T(8,128)(2,1)S(1)} %bitcast.164, bf16[256,256]{0,1:T(8,128)(2,1)S(1)} %bitcast.159, ...), kind=kOutput, calls=%fused_computation.138 | convolution fusion | flops 105480576 | bytes 4104224 | tf_op jit(solution)/shard_map/sub | solution.py:52
  41.6 2.2 divide_convert_fusion.1
  43.8 1.2 copy-done.3
  45.6 3.8 %fusion.111 = (f32[8,256]{1,0:T(8,128)S(1)}, f32[8,256,384]{1,2,0:T(8,128)}) fusion(s32[256,384]{0,1:T(8,128)S(1)} %copy-done.6, s32[8]{0:T(128)S(1)} %get-tuple-element.22, pred[256,384]{0,1:T(8,128)(4,1)S(1)} %copy-done.13, bf16[256,8,64]{0,2,1:T(8,128)(2,1)S(1)} %bitcast.163, bf16[256,256]{0,1:T(8,128)(2,1)S(1)} %bitcast.161, ...), kind=kOutput, calls=%fused_computation.137 | convolution fusion | flops 105480576 | bytes 4104224 | tf_op jit(solution)/shard_map/sub | solution.py:52
  49.3 2.2 divide_convert_fusion
  51.5 1.2 convolution_bitcast_fusion.1
  52.8 4.1 %fusion.118 = (f32[8,256]{1,0:T(8,128)S(1)}, f32[8,256,384]{1,2,0:T(8,128)}) fusion(s32[256,384]{0,1:T(8,128)} %iota_subtract_fusion, s32[8]{0:T(128)S(1)} %get-tuple-element.20, pred[256,384]{0,1:T(8,128)(4,1)} %copy-done.11, bf16[256,8,64]{0,2,1:T(8,128)(2,1)} %bitcast.162, bf16[256,256]{0,1:T(8,128)(2,1)} %bitcast.160, ...), kind=kOutput, calls=%fused_computation.140 | convolution fusion | flops 105480576 | bytes 4104224 | tf_op jit(solution)/shard_map/sub | solution.py:52
  56.9 2.2 divide_convert_fusion.3
  59.1 1.2 copy-done.1
  61.0 1.3 collective-permute-start.2
  62.3 5.5 %collective-permute-done.2 = f32[128,256]{0,1:T(8,128)S(1)} collective-permute-done((f32[128,256]{0,1:T(8,128)S(1)}, f32[128,256]{0,1:T(8,128)S(1)}, u32[]{:S(2)}, u32[]{:S(2)}) %collective-permute-start.2) | collective-permute-done | bytes 131104 | tf_op jit(solution)/shard_map/ppermute | solution.py:22
  67.9 2.2 convolution_bitcast_fusion
  70.2 1.4 all-gather.3.cloned.1.call-done
  71.6 3.3 %reshape.174 = bf16[2880,256]{1,0:T(8,128)(2,1)} reshape(bf16[16,180,256]{2,1,0:T(8,128)(2,1)} %all-gather.3.cloned.1.call-done) | data formatting | bytes 2949120
  74.9 2.0 fusion.31
  76.9 3.0 %collective-permute-start = (bf16[128,256]{1,0:T(8,128)(2,1)S(1)}, bf16[128,256]{1,0:T(8,128)(2,1)S(1)}, u32[]{:S(2)}, u32[]{:S(2)}) collective-permute-start(bf16[128,256]{1,0:T(8,128)(2,1)S(1)} %slice.108), channel_id=1, source_target_pairs={{0,2},{2,4},{4,6},{6,8},{8,10},{10,12},{12,14},{14,16},{16,18},{18... | collective-permute-start | bytes 196616 | tf_op jit(solution)/shard_map/ppermute | solution.py:22
  80.7 1.8 collective-permute-done
  82.4 1.9 convolution_convert_fusion.2
  84.3 2.5 convolution_convert_fusion.1
  86.8 133.7 %all-reduce.4.cloned.1.call-done = f32[2880,256]{1,0:T(8,128)} async-done(((f32[2880,256]{1,0:T(8,128)}), f32[2880,256]{1,0:T(8,128)}) %all-reduce.4.cloned.1.call-update) | async-done | bytes 2949136 | tf_op jit(solution)/shard_map/psum | solution.py:90
  220.6 4.8 %broadcast_multiply_fusion = (f32[2880,256]{1,0:T(8,128)}, f32[]{:T(128)}) fusion(f32[2880,256]{1,0:T(8,128)} %all-reduce.4.cloned.1.call-done), kind=kLoop, calls=%fused_computation.45 | loop fusion | flops 2211839 | bytes 5898244 | tf_op jit(solution)/shard_map/div | solution.py:90
  226.1 2.1 bitcast_subtract_fusion
  228.2 1.2 convolution_convert_fusion
  229.5 1.1 copy.86
  230.6 1.1 copy.87
  231.7 1.8 convolution_convert_fusion.3
  233.7 1.1 pad_maximum_fusion
  234.8 11.6 %all-reduce.6.cloned.1.call-done = (f32[180,256]{1,0:T(8,128)}, f32[180,256]{1,0:T(8,128)}, f32[180,256]{1,0:T(8,128)}) async-done(((f32[180,256]{1,0:T(8,128)}, f32[180,256]{1,0:T(8,128)}, f32[180,256]{1,0:T(8,128)}), (f32[180,256]{1,0:T(8,128)}, f32[180,256]{1,0:T(8,128)}, f32[180,256]{1,0:T(8,128)})) %all-reduce.6.cloned.1.call-update) | async-done | bytes 552976 | tf_op jit(solution)/shard_map/psum | solution.py:108
  246.5 1.6 broadcast_multiply_fusion.3
  248.1 1.8 broadcast_multiply_fusion.1
  (47 shorter events, 2.1 us)
Async XLA Ops:
  7.2 60.7 %copy-start = (bf16[1,256,2880]{1,2,0:T(8,128)(2,1)S(1)}, bf16[1,256,2880]{1,2,0:T(8,128)(2,1)}, u32[]{:S(2)}) copy-start(bf16[1,256,2880]{1,2,0:T(8,128)(2,1)} %param.10) | copy-start | bytes 4423684
  7.2 12.8 %copy-start.4 = (bf16[1,256,2048]{2,1,0:T(8,128)(2,1)S(1)}, bf16[1,256,2048]{2,1,0:T(8,128)(2,1)}, u32[]{:S(2)}) copy-start(bf16[1,256,2048]{2,1,0:T(8,128)(2,1)} %param.13) | copy-start | bytes 3145732
  7.2 13.7 %copy-start.14 = (s32[32]{0:T(128)S(1)}, s32[32]{0:T(128)}, u32[]{:S(2)}) copy-start(s32[32]{0:T(128)} %param.15) | copy-start | bytes 388
  7.2 64.4 %all-gather.3.cloned.1.call-start = ((), (), s32[]{:S(2)}) async-start(), calls=%async_computation.1 | async-start | bytes 1601536 | tf_op jit(solution)/shard_map/all_gather | solution.py:74
  9.0 211.6 %all-reduce.4.cloned.1.call-start = ((), (), s32[]{:S(2)}) async-start(), calls=%async_computation | async-start | bytes 5898240 | tf_op jit(solution)/shard_map/psum | solution.py:90
  10.1 27.7 %copy-start.8 = (bf16[1,256,256]{1,2,0:T(8,128)(2,1)}, bf16[1,256,256]{1,2,0:T(8,128)(2,1)S(1)}, u32[]{:S(2)}) copy-start(bf16[1,256,256]{1,2,0:T(8,128)(2,1)S(1)} %copy.70) | copy-start | bytes 393220
  10.7 19.0 %collective-permute-start.1 = (bf16[128,256]{0,1:T(8,128)(2,1)}, bf16[128,256]{0,1:T(8,128)(2,1)}, u32[]{:S(2)}, u32[]{:S(2)}) collective-permute-start(bf16[128,256]{0,1:T(8,128)(2,1)} %slice_bitcast_fusion), channel_id=1, source_target_pairs={{0,2},{2,4},{4,6},{6,8},{8,10},{10,12},{12,14},{14,16},{16,18},{18... | collective-permute-start | bytes 196616 | tf_op jit(solution)/shard_map/ppermute | solution.py:22
  17.8 12.0 %copy-start.11 = (pred[256,384]{0,1:T(8,128)(4,1)}, pred[256,384]{0,1:T(8,128)(4,1)S(1)}, u32[]{:S(2)}) copy-start(pred[256,384]{0,1:T(8,128)(4,1)S(1)} %compare_and_fusion) | copy-start | bytes 294916
  20.9 8.9 %copy-start.6 = (s32[256,384]{0,1:T(8,128)S(1)}, s32[256,384]{0,1:T(8,128)}, u32[]{:S(2)}) copy-start(s32[256,384]{0,1:T(8,128)} %iota_subtract_fusion) | copy-start | bytes 1179652
  33.8 4.0 %copy-start.10 = (bf16[256,512]{0,1:T(8,128)(2,1)S(1)}, bf16[256,512]{0,1:T(8,128)(2,1)}, u32[]{:S(2)}) copy-start(bf16[256,512]{0,1:T(8,128)(2,1)} %copy.78) | copy-start | bytes 786436
  33.8 4.0 %copy-start.12 = (pred[256,384]{0,1:T(8,128)(4,1)S(1)}, pred[256,384]{0,1:T(8,128)(4,1)}, u32[]{:S(2)}) copy-start(pred[256,384]{0,1:T(8,128)(4,1)} %copy-done.11) | copy-start | bytes 294916
  36.0 1.2 copy-start.2
  41.6 4.0 %copy-start.9 = (bf16[1,256,256]{1,2,0:T(8,128)(2,1)S(1)}, bf16[1,256,256]{1,2,0:T(8,128)(2,1)}, u32[]{:S(2)}) copy-start(bf16[1,256,256]{1,2,0:T(8,128)(2,1)} %copy-done.8) | copy-start | bytes 393220
  41.6 4.0 %copy-start.13 = (pred[256,384]{0,1:T(8,128)(4,1)S(1)}, pred[256,384]{0,1:T(8,128)(4,1)}, u32[]{:S(2)}) copy-start(pred[256,384]{0,1:T(8,128)(4,1)} %copy-done.11) | copy-start | bytes 294916
  43.8 1.2 copy-start.3
  49.3 2.2 copy-start.5
  56.9 4.0 %copy-start.7 = (f32[384,64]{0,1:T(8,128)S(1)}, f32[384,64]{0,1:T(8,128)}, u32[]{:S(2)}) copy-start(f32[384,64]{0,1:T(8,128)} %convolution_bitcast_fusion.1) | copy-start | bytes 294916
  59.1 1.2 copy-start.1
  61.0 6.9 %collective-permute-start.2 = (f32[128,256]{0,1:T(8,128)S(1)}, f32[128,256]{0,1:T(8,128)S(1)}, u32[]{:S(2)}, u32[]{:S(2)}) collective-permute-start(f32[128,256]{0,1:T(8,128)S(1)} %slice.132), channel_id=1, source_target_pairs={{2,0},{4,2},{6,4},{8,6},{10,8},{12,10},{14,12},{16,14},{18,16},{20... | collective-permute-start | bytes 393224 | tf_op jit(solution)/shard_map/ppermute | solution.py:22
  70.1 176.3 %all-reduce.6.cloned.1.call-start = ((), (), s32[]{:S(2)}) async-start(), calls=%async_computation.2 | async-start | bytes 1130496 | tf_op jit(solution)/shard_map/psum | solution.py:108
  76.9 5.5 %collective-permute-start = (bf16[128,256]{1,0:T(8,128)(2,1)S(1)}, bf16[128,256]{1,0:T(8,128)(2,1)S(1)}, u32[]{:S(2)}, u32[]{:S(2)}) collective-permute-start(bf16[128,256]{1,0:T(8,128)(2,1)S(1)} %slice.108), channel_id=1, source_target_pairs={{0,2},{2,4},{4,6},{6,8},{8,10},{10,12},{12,14},{14,16},{16,18},{18... | collective-permute-start | bytes 196616 | tf_op jit(solution)/shard_map/ppermute | solution.py:22
Sparse Core Ops, SparseCore 0:
  10.8 60.8 all-gather.2
  77.3 143.2 all-reduce.3
  228.3 18.0 all-reduce.5
where the time goes:
time: 257 us; the launch traced here: 256 us
  waiting for transfers between devices  154 us (60%)
  matrix products  30.3 us (12%)
  local copies, waits for them, and re-layouts  24.7 us (10%)
  other arithmetic  21.8 us (8%)
  between operations  15.6 us (6%)
  starting transfers between devices  9.88 us (4%)
    psum x1, waiting for transfers between devices, per_device(): lax.psum(lax.dot_general(columns, value_grad, (((0,), (0,)), ((), ())), p...  134 us
    sub x4, matrix products, attend(): expo = jnp.exp(scores - top)  15.7 us
    psum x1, waiting for transfers between devices, per_device(): mean_weight, mean_one, mean_two = lax.psum((updated, first, second), 'work')  11.6 us
    ppermute x3, starting transfers between devices, shifted(): return lax.ppermute(array, axis, pairs)  9.76 us
    unnamed x33, local copies, waits for them, and re-layouts  9.64 us
    convert_element_type x4, other arithmetic, attend(): probs = (expo / jnp.sum(expo, axis=2, keepdims=True)).astype(jnp.bfloat16)  8.78 us
    slice x5, local copies, waits for them, and re-layouts, attend(): query = qrows[:, lo:hi].reshape(count, group, HD)  7.76 us
    dot_general x4, matrix products, attend(): jnp.einsum('gqk,kd->qgd', probs, valued, preferred_element_type=jnp.float32)  7.42 us
  transfers between devices with their start and end apart: 6, of which 5 were waited for; matrix products, arithmetic and copies ran while one was open for 24% of the time, Pallas kernels for 0%

commit v1 on v0

v1 whole, which is shorter than its diff:
```python
import functools

import jax
import jax.numpy as jnp
from jax import lax
from jax.experimental import pallas as pl
from jax.experimental.pallas import tpu as pltpu
from jax.sharding import PartitionSpec as P


HD = 64
QH = 32
KH = 4
LOOKBACK_SPAN = 128
LANES = 128

beta_one = 0.9
beta_two = 0.95
adam_eps = 1e-08
learn_rate = 0.01
clip_norm = 0.5

bf16 = jnp.bfloat16
f32 = jnp.float32


def swapped(array, axis, mask):
    pairs = [(i, i ^ mask) for i in range(lax.axis_size(axis))]
    return lax.ppermute(array, axis, pairs)


def shifted(array, axis, by):
    devices = lax.axis_size(axis)
    pairs = [(i, i + by) for i in range(devices) if 0 <= i + by < devices]
    return lax.ppermute(array, axis, pairs)


VMEM = pl.BlockSpec(memory_space=pltpu.VMEM)
SMEM = pl.BlockSpec(memory_space=pltpu.SMEM)


def params(mib):
    return pltpu.CompilerParams(vmem_limit_bytes=mib << 20)


def full(shape, dtype):
    return jax.ShapeDtypeStruct(shape, dtype)


def probs_body(bands, pos, query, cotan, klo, khi, probs_out, grad_out):
    block = LOOKBACK_SPAN
    group = QH // KH
    pairs = group // 2
    step = pl.program_id(0)
    span = 2 * block
    left = lax.broadcasted_iota(jnp.int32, (span, LANES), 1) < HD
    keyed = jnp.concatenate([klo[...], khi[...]], 0).astype(f32) * HD ** (-0.5)
    rolled = pltpu.roll(keyed, HD, 1)
    dist = (
        lax.broadcasted_iota(jnp.int32, (span, block), 1)
        + block
        - lax.broadcasted_iota(jnp.int32, (span, block), 0)
    )
    dist = jnp.where(dist < 0, 2 * span, dist)
    row = pos[...]
    sums = []
    for half in range(2):
        one, two = (keyed, rolled) if half == 0 else (rolled, keyed)
        sides = (
            jnp.where(left, one, 0.0).astype(bf16),
            jnp.where(left, 0.0, two).astype(bf16),
        )
        base = half * group * HD
        cols = [slice(base + p * LANES, base + (p + 1) * LANES) for p in range(pairs)]
        queries = jnp.concatenate([query[:, c] for c in cols], 0)
        cotans = jnp.concatenate([cotan[:, c] for c in cols], 0)
        for odd, side in enumerate(sides):
            scores = lax.dot_general(
                side, queries, (((1,), (1,)), ((), ())), preferred_element_type=f32
            )
            rows = []
            for p in range(pairs):
                head = half * group + 2 * p + odd
                limit = jnp.minimum(row, bands[step * 2 * group + head])
                seen = jnp.where(
                    dist <= limit, scores[:, p * block : (p + 1) * block], -1e30
                )
                expo = jnp.exp(seen - jnp.max(seen, axis=0, keepdims=True))
                prob = (expo * (1.0 / jnp.sum(expo, axis=0, keepdims=True))).astype(bf16)
                probs_out[head] = prob
                rows.append(prob)
            sums.append(
                lax.dot_general(
                    jnp.concatenate(rows, 1),
                    cotans,
                    (((1,), (0,)), ((), ())),
                    preferred_element_type=f32,
                )
            )
    grad_out[...] = jnp.where(
        left,
        sums[0] + pltpu.roll(sums[1], HD, 1),
        sums[3] + pltpu.roll(sums[2], HD, 1),
    )


def probs_call(bands, positions, queries, out_grad, keys_lo, lo, keys_hi, hi, block_index):
    block = LOOKBACK_SPAN
    wide = 2 * (QH // KH) * HD
    heads = 2 * (QH // KH)
    steps = KH // 2
    return pl.pallas_call(
        probs_body,
        grid=(steps,),
        in_specs=[
            pl.BlockSpec(memory_space=pltpu.SMEM),
            pl.BlockSpec((1, block), lambda s: (0, block_index)),
            pl.BlockSpec((block, wide), lambda s: (block_index, s)),
            pl.BlockSpec((block, wide), lambda s: (block_index, s)),
            pl.BlockSpec((block, LANES), lambda s: (lo, s)),
            pl.BlockSpec((block, LANES), lambda s: (hi, s)),
        ],
        out_specs=[
            pl.BlockSpec((heads, 2 * block, block), lambda s: (s, 0, 0)),
            pl.BlockSpec((2 * block, LANES), lambda s: (0, s)),
        ],
        out_shape=[
            full((QH, 2 * block, block), bf16),
            full((2 * block, KH * HD), f32),
        ],
        compiler_params=params(16),
    )(bands, positions, queries, out_grad, keys_lo, keys_hi)


def mix_body(probs, vlo, vhi, *refs):
    out = refs[-1]
    group = QH // KH
    pairs = group // 2
    block = LOOKBACK_SPAN
    valued = jnp.concatenate([vlo[...], vhi[...]], 0).astype(f32)
    turned = valued.T.astype(bf16)
    for half in range(2):
        left = turned[half * HD : (half + 1) * HD]
        for p in range(pairs):
            head = half * group + 2 * p
            both = jnp.concatenate([probs[head], probs[head + 1]], 1)
            res = lax.dot_general(
                left, both, (((1,), (0,)), ((), ())), preferred_element_type=f32
            )
            stacked = jnp.concatenate([res[:, :block], res[:, block:]], 0)
            base = half * group * HD + p * LANES
            out[:, base : base + LANES] = stacked.T.astype(bf16)


def mix_call(probs, vlo, vhi, tokens, block_index, into):
    block = LOOKBACK_SPAN
    wide = 2 * (QH // KH) * HD
    heads = 2 * (QH // KH)
    extra = [] if into is None else [into]
    return pl.pallas_call(
        mix_body,
        grid=(KH // 2,),
        in_specs=[
            pl.BlockSpec((heads, 2 * block, block), lambda s: (s, 0, 0)),
            pl.BlockSpec((block, LANES), lambda s: (0, s)),
            pl.BlockSpec((block, LANES), lambda s: (0, s)),
        ]
        + [pl.BlockSpec(memory_space=pl.ANY)] * len(extra),
        out_specs=pl.BlockSpec((block, wide), lambda s: (block_index, s)),
        out_shape=full((tokens, QH * HD), bf16),
        input_output_aliases={3: 0} if extra else {},
        compiler_params=params(12),
    )(probs, vlo, vhi, *extra)


def cut_body(quad, near, acts, *refs):
    outs, shards = refs[:quad], refs[quad]
    devices, rows = shards.shape[:2]
    for j in range(devices):
        shards[j] = acts[j * rows : (j + 1) * rows, :]
    mine = near[0]
    for m in range(quad):
        for z in range(devices // quad):
            outs[m][z] = shards[z * quad + (mine ^ m)]


def cut_call(near, turned, devices, quad):
    width, tokens = turned.shape
    rows = width // devices
    return pl.pallas_call(
        functools.partial(cut_body, quad),
        in_specs=[SMEM, VMEM],
        out_specs=[VMEM] * quad,
        out_shape=[full((devices // quad, rows, tokens), bf16)] * quad,
        scratch_shapes=[pltpu.VMEM((devices, rows, tokens), bf16)],
        compiler_params=params(8),
        name="cut",
    )(near, turned)


def outer_body(quad, far_size, far, *refs):
    turned, grads, outs = refs[:quad], refs[quad : 2 * quad], refs[2 * quad :]
    mine = far[0]
    for k in range(far_size):
        z = mine ^ k
        total = None
        for m in range(quad):
            term = lax.dot_general(
                turned[m][z], grads[m][...], (((1,), (0,)), ((), ())), preferred_element_type=f32
            )
            total = term if total is None else total + term
        outs[k][...] = total.astype(outs[k].dtype)


def outer_call(far, turned, grads):
    quad = len(turned)
    far_size, rows, _ = turned[0].shape
    wide = grads[0].shape[1]
    return pl.pallas_call(
        functools.partial(outer_body, quad, far_size),
        in_specs=[SMEM] + [VMEM] * (2 * quad),
        out_specs=[VMEM] * far_size,
        out_shape=[full((rows, wide), f32 if k == 0 else bf16) for k in range(far_size)],
        compiler_params=params(8),
        name="outer",
    )(far, *turned, *grads)


def value_body(quad, far_size, far, *refs):
    turned, weights, outs = refs[:quad], refs[quad : quad + far_size], refs[quad + far_size :]
    mine = far[0]
    for m in range(quad):
        total = None
        for k in range(far_size):
            term = lax.dot_general(
                turned[m][mine ^ k],
                weights[k][...],
                (((0,), (0,)), ((), ())),
                preferred_element_type=f32,
            )
            total = term if total is None else total + term
        outs[m][...] = total


def value_call(far, turned, weights):
    quad = len(turned)
    far_size, _, tokens = turned[0].shape
    wide = weights[0].shape[1]
    return pl.pallas_call(
        functools.partial(value_body, quad, far_size),
        in_specs=[SMEM] + [VMEM] * (quad + far_size),
        out_specs=[VMEM] * quad,
        out_shape=[full((tokens, wide), f32)] * quad,
        compiler_params=params(8),
        name="value",
    )(far, *turned, *weights)


def join_body(count, *refs):
    parts, outs = refs[:count], refs[count:]
    for b, out in enumerate(outs):
        rows = slice(b * out.shape[0], (b + 1) * out.shape[0])
        total = parts[0][rows, :]
        for part in parts[1:]:
            total = total + part[rows, :]
        out[...] = total.astype(bf16)


def join_call(parts, blocks):
    tokens, wide = parts[0].shape
    return pl.pallas_call(
        functools.partial(join_body, len(parts)),
        in_specs=[VMEM] * len(parts),
        out_specs=[VMEM] * blocks,
        out_shape=[full((tokens // blocks, wide), bf16)] * blocks,
        compiler_params=params(4),
        name="join",
    )(*parts)


def reduce_body(scale, slot, own, *refs):
    others, total, square = refs[:-2], refs[-2], refs[-1]
    grad = own[...]
    for other in others:
        grad = grad + other[...].astype(f32)
    grad = grad * scale
    total[...] = grad
    lane = lax.broadcasted_iota(jnp.int32, square.shape, 1)
    square[...] = jnp.where(lane == slot[0], jnp.sum(grad * grad), 0.0)


def reduce_call(slot, own, others, scale):
    return pl.pallas_call(
        functools.partial(reduce_body, scale),
        in_specs=[SMEM] + [VMEM] * (1 + len(others)),
        out_specs=[VMEM] * 2,
        out_shape=[full(own.shape, f32), full((1, LANES), f32)],
        compiler_params=params(4),
        name="reduce",
    )(slot, own, *others)


def tree_sum(values):
    while len(values) > 1:
        values = [a + b for a, b in zip(values[::2], values[1::2])]
    return values[0]


def adam_body(workers, slot, fixes, squares, *refs):
    ins, outs = refs[: 4 * workers], refs[4 * workers :]
    fix_one, fix_two = fixes[0], fixes[1]
    results = []
    for w in range(workers):
        grad, weight, first, second = (r[...] for r in ins[4 * w : 4 * w + 4])
        norm = jnp.sqrt(jnp.full((8, grad.shape[1]), squares[0, slot[0] ^ w]))
        factor = jnp.minimum(1.0, clip_norm / (norm + 1e-06))
        grad = grad * factor[:1]
        first = beta_one * first + (1.0 - beta_one) * grad
        second = beta_two * second + (1.0 - beta_two) * grad * grad
        weight = weight - learn_rate * (first / fix_one) / (
            jnp.sqrt(second / fix_two) + adam_eps
        )
        results.append((weight, first, second))
    for out, values in zip(outs, zip(*results)):
        out[...] = tree_sum(list(values)) / workers


def adam_call(slot, fixes, squares, states):
    workers = len(states)
    shape = states[0][0].shape
    return pl.pallas_call(
        functools.partial(adam_body, workers),
        in_specs=[SMEM] * 3 + [VMEM] * (4 * workers),
        out_specs=[VMEM] * 3,
        out_shape=[full(shape, f32)] * 3,
        compiler_params=params(8),
        name="adam",
    )(slot, fixes, squares, *[a for state in states for a in state])


def scalar(value):
    return value.astype(jnp.int32).reshape(1)


def per_device(
    inputs, queries, keys, out_grad, positions, bands, step, value_weight, moment_one, moment_two
):
    acts = inputs[0]
    tokens = acts.shape[0]
    block = LOOKBACK_SPAN
    blocks = tokens // block
    devices = lax.axis_size("ctx")
    workers = lax.axis_size("work")
    quad = min(4, devices)
    far_size = devices // quad
    index = lax.axis_index("ctx")
    slot = scalar(lax.axis_index("work"))
    near = scalar(index & (quad - 1))
    far = scalar(index >> (quad.bit_length() - 1))
    keyed = keys[0]
    query, cotan = queries[0], out_grad[0]
    weight, first, second = value_weight[0], moment_one[0], moment_two[0]
    narrow = weight.astype(bf16)

    prev_keys = shifted(keyed, "ctx", 1)
    turned = cut_call(near, acts.T, devices, quad)
    turned = [turned[0]] + [swapped(turned[m], "ctx", m) for m in range(1, quad)]
    column = [narrow] + [swapped(narrow, "ctx", k * quad) for k in range(1, far_size)]

    probs = [None] * blocks
    grads = [None] * blocks
    for b in range(blocks - 1, -1, -1):
        lower, lo = (keyed, b - 1) if b else (prev_keys, blocks - 1)
        probs[b], grads[b] = probs_call(
            bands, positions, query, cotan, lower, lo, keyed, b, b
        )
    returned = shifted(grads[0][:block], "ctx", -1)
    rows = []
    for b in range(blocks):
        after = grads[b + 1][:block] if b + 1 < blocks else returned
        rows.append((grads[b][block:] + after).astype(bf16))
    value_grad = jnp.concatenate(rows, 0)
    value_grads = [value_grad] + [swapped(value_grad, "ctx", m) for m in range(1, quad)]

    parts = outer_call(far, turned, value_grads)
    others = [swapped(parts[k], "ctx", k * quad) for k in range(1, far_size)]

    pieces = value_call(far, turned, column)
    pieces = [pieces[0]] + [swapped(pieces[m], "ctx", m) for m in range(1, quad)]
    values = join_call(pieces, blocks)
    prev_values = shifted(values[-1], "ctx", 1)
    out = None
    for b in range(blocks - 1, -1, -1):
        lower = values[b - 1] if b else prev_values
        out = mix_call(probs[b], lower, values[b], tokens, b, out)

    grad, squares = reduce_call(slot, parts[0], others, 1.0 / (tokens * devices))
    states = [(grad, weight, first, second)]
    for w in range(1, workers):
        states.append(tuple(swapped(a, "work", w) for a in states[0]))
    for axis, size in (("work", workers), ("ctx", devices)):
        bit = 1
        while bit < size:
            squares = squares + swapped(squares, axis, bit)
            bit *= 2
    count = step[0].astype(f32)
    fixes = jnp.stack(
        [1.0 - jnp.power(f32(beta_one), count), 1.0 - jnp.power(f32(beta_two), count)]
    )
    mean_weight, mean_one, mean_two = adam_call(slot, fixes, squares, states)
    return (out[None], mean_weight, mean_one, mean_two)


def solution(mesh):
    in_specs = (
        P("work", "ctx", None),
        P("work", "ctx", None),
        P("work", "ctx", None),
        P("work", "ctx", None),
        P("work", "ctx"),
        P(),
        P(),
        P("work", "ctx", None),
        P("work", "ctx", None),
        P("work", "ctx", None),
    )
    out_specs = (P("work", "ctx", None), P("ctx", None), P("ctx", None), P("ctx", None))
    return jax.shard_map(
        per_device, mesh=mesh, in_specs=in_specs, out_specs=out_specs, check_vma=False
    )
```

time: 257 us -> 103 us (0.40)
  waiting for transfers between devices: 154 us -> 31.3 us
  matrix products: 30.3 us -> 0 us
  starting transfers between devices: 9.88 us -> 31.8 us
  other arithmetic: 21.8 us -> 1.73 us
  Pallas kernels: 0 us -> 19.6 us
  between operations: 15.6 us -> 1.61 us
  local copies, waits for them, and re-layouts: 24.7 us -> 16.6 us
    psum x2 -> x0, waiting for transfers between devices: 145 us -> none  [the longest x1 134 us: per_device(): lax.psum(lax.dot_general(columns, value_grad, (((0,), (0,)), ((), ())), p...]
    ppermute x0 -> x24, waiting for transfers between devices: none -> 31.3 us  [swapped(): return lax.ppermute(array, axis, pairs)]
    ppermute x0 -> x24, starting transfers between devices: none -> 22 us  [swapped(): return lax.ppermute(array, axis, pairs)]
    pallas_call x0 -> x10, Pallas kernels: none -> 19.6 us  [the longest x2 7.29 us: probs_call(): pl.pallas_call(probs_body, grid=(steps,), in_specs=[pl.BlockSpec(memory_s...]
    sub x4 -> x0, matrix products: 15.7 us -> none  [attend(): expo = jnp.exp(scores - top)]
    dot_general x10 -> x0, matrix products: 14.6 us -> none  [the longest x4 7.42 us: attend(): jnp.einsum('gqk,kd->qgd', probs, valued, preferred_element_type=jnp.float32)]
    slice x15 -> x0, local copies, waits for them, and re-layouts: 12.6 us -> none  [the longest x5 7.76 us: attend(): query = qrows[:, lo:hi].reshape(count, group, HD)]
    div x3 -> x0, other arithmetic: 8.17 us -> none  [the longest x1 4.79 us: per_device(): lax.psum(lax.dot_general(columns, value_grad, (((0,), (0,)), ((), ())), p...]
  transfers between devices with their start and end apart: 6 -> 27, of which waited for: 5 -> 10; matrix products, arithmetic and copies ran while one was open for 24% -> 4% of each run, Pallas kernels for 0% -> 14%
where the time goes in v1:
time: 103 us
  starting transfers between devices  31.8 us (31%)
  waiting for transfers between devices  31.3 us (30%)
  Pallas kernels  19.6 us (19%)
  local copies, waits for them, and re-layouts  16.6 us (16%)
  other arithmetic  1.73 us (2%)
  between operations  1.61 us (2%)
    ppermute x24, waiting for transfers between devices, swapped(): return lax.ppermute(array, axis, pairs)  31.3 us
    ppermute x24, starting transfers between devices, swapped(): return lax.ppermute(array, axis, pairs)  22 us
    unnamed x44, local copies, waits for them, and re-layouts  16.6 us
    ppermute x3, starting transfers between devices, shifted(): return lax.ppermute(array, axis, pairs)  9.79 us
    pallas_call x2, Pallas kernels, probs_call(): pl.pallas_call(probs_body, grid=(steps,), in_specs=[pl.BlockSpec(memory_s...  7.29 us
    pallas_call x2, Pallas kernels, mix_call(): pl.pallas_call(mix_body, grid=(KH // 2,), in_specs=[pl.BlockSpec((heads,...  3.26 us
    pallas_call x1, Pallas kernels, value_call(): pl.pallas_call(functools.partial(value_body, quad, far_size), in_specs=[S...  2.54 us
    pallas_call x1, Pallas kernels, outer_call(): pl.pallas_call(functools.partial(outer_body, quad, far_size), in_specs=[S...  2.39 us
  transfers between devices with their start and end apart: 27, of which 10 were waited for; matrix products, arithmetic and copies ran while one was open for 4% of the time, Pallas kernels for 14%

profile of v1, /device:TPU:0, one launch (start us, length us, event | category | flops | bytes accessed | tf_op | source)
XLA Modules:
  0.0 102.5 jit_solution(6864985035994910227)
XLA Ops:
  0.6 4.9 %collective-permute-start = (bf16[256,256]{1,0:T(8,128)(2,1)}, bf16[256,256]{1,0:T(8,128)(2,1)S(1)}, u32[]{:S(2)}, u32[]{:S(2)}) collective-permute-start(bf16[256,256]{1,0:T(8,128)(2,1)} %bitcast.27), channel_id=1, source_target_pairs={{0,2},{2,4},{4,6},{6,8},{8,10},{10,12},{12,14},{14,16},{16,18},{18... | collective-permute-start | bytes 393224 | tf_op jit(solution)/shard_map/ppermute | solution.py:35
  5.5 1.2 %copy-done = bf16[1,256,2048]{2,1,0:T(8,128)(2,1)S(1)} copy-done((bf16[1,256,2048]{2,1,0:T(8,128)(2,1)S(1)}, bf16[1,256,2048]{2,1,0:T(8,128)(2,1)}, u32[]{:S(2)}) %copy-start) | copy-done | bytes 1048600
  6.7 1.2 %copy-done.1 = bf16[1,256,2048]{2,1,0:T(8,128)(2,1)S(1)} copy-done((bf16[1,256,2048]{2,1,0:T(8,128)(2,1)S(1)}, bf16[1,256,2048]{2,1,0:T(8,128)(2,1)}, u32[]{:S(2)}) %copy-start.1) | copy-done | bytes 1048600
  8.0 0.9 copy-done.5
  10.2 3.6 %shard_map.130 = (bf16[32,256,128]{2,1,0:T(8,128)(2,1)S(1)}, f32[256,256]{1,0:T(8,128)S(1)}) custom-call(s32[32]{0:T(128)S(1)} %copy-done.17, s32[1,256]{1,0:T(1,128)S(1)} %copy-done.16, bf16[256,2048]{1,0:T(8,128)(2,1)S(1)} %bitcast.22, bf16[256,2048]{1,0:T(8,128)(2,1)S(1)} %bitcast.24, bf16[256,256]{1,0:T(8,128)(2,1)S(1)} %bitcast.28, ...), custom_call_target="tpu_custom_call" | custom-call | tf_op jit(solution)/shard_map/pallas_call | solution.py:112
  13.9 1.3 %copy-done.2 = bf16[32,256,128]{2,1,0:T(8,128)(2,1)} copy-done((bf16[32,256,128]{2,1,0:T(8,128)(2,1)}, bf16[32,256,128]{2,1,0:T(8,128)(2,1)S(1)}, u32[]{:S(2)}) %copy-start.2) | copy-done | bytes 2097176
  15.2 3.7 %shard_map.129 = (bf16[32,256,128]{2,1,0:T(8,128)(2,1)S(1)}, f32[256,256]{1,0:T(8,128)S(1)}) custom-call(s32[32]{0:T(128)S(1)} %copy-done.17, s32[1,256]{1,0:T(1,128)S(1)} %copy-done.16, bf16[256,2048]{1,0:T(8,128)(2,1)S(1)} %bitcast.23, bf16[256,2048]{1,0:T(8,128)(2,1)S(1)} %bitcast.25, bf16[256,256]{1,0:T(8,128)(2,1)S(1)} %collective-permute-done.klo, ...), custom_call_target="tpu_custom_call" | custom-call | tf_op jit(solution)/shard_map/pallas_call | solution.py:112
  18.9 0.7 add_convert_fusion.1
  19.6 1.3 %collective-permute-start.11 = (f32[128,256]{1,0:T(8,128)}, f32[128,256]{1,0:T(8,128)S(1)}, u32[]{:S(2)}, u32[]{:S(2)}) collective-permute-start(f32[128,256]{1,0:T(8,128)} %get-tuple-element.51), channel_id=1, source_target_pairs={{2,0},{4,2},{6,4},{8,6},{10,8},{12,10},{14,12},{16,14},{18,16},{20... | collective-permute-start | bytes 393224 | tf_op jit(solution)/shard_map/ppermute | solution.py:35
  20.9 1.4 %copy-done.4 = bf16[1,256,2880]{1,2,0:T(8,128)(2,1)S(1)} copy-done((bf16[1,256,2880]{1,2,0:T(8,128)(2,1)S(1)}, bf16[1,256,2880]{1,2,0:T(8,128)(2,1)}, u32[]{:S(2)}) %copy-start.4) | copy-done | bytes 1474584
  22.2 1.1 %cut.1 = (bf16[4,180,256]{2,1,0:T(8,128)(2,1)S(1)}, bf16[4,180,256]{2,1,0:T(8,128)(2,1)S(1)}, bf16[4,180,256]{2,1,0:T(8,128)(2,1)}, bf16[4,180,256]{2,1,0:T(8,128)(2,1)}) custom-call(s32[1]{0:T(128)} %bitcast.4.near, bf16[2880,256]{1,0:T(8,128)(2,1)S(1)} %bitcast.26), custom_call_target="tpu_custom_call" | custom-call | tf_op jit(solution)/shard_map/cut/pallas_call | solution.py:190
  23.3 2.6 %collective-permute-start.1 = (bf16[4,180,256]{2,1,0:T(8,128)(2,1)S(1)}, bf16[4,180,256]{2,1,0:T(8,128)(2,1)S(1)}, u32[]{:S(2)}, u32[]{:S(2)}) collective-permute-start(bf16[4,180,256]{2,1,0:T(8,128)(2,1)S(1)} %get-tuple-element.29), channel_id=1, source_target_pairs={{0,2},{2,0},{4,6},{6,4},{8,10},{10,8},{12,14},{14,12},{16,18},{18,... | collective-permute-start | bytes 1105928 | tf_op jit(solution)/shard_map/ppermute | solution.py:29
  26.0 1.9 %collective-permute-start.4 = (bf16[180,256]{1,0:T(8,128)(2,1)S(1)}, bf16[180,256]{1,0:T(8,128)(2,1)S(1)}, u32[]{:S(2)}, u32[]{:S(2)}) collective-permute-start(bf16[180,256]{1,0:T(8,128)(2,1)S(1)} %bitcast.37), channel_id=1, source_target_pairs={{0,8},{2,10},{4,12},{6,14},{8,0},{10,2},{12,4},{14,6},{16,24},{18,... | collective-permute-start | bytes 276488 | tf_op jit(solution)/shard_map/ppermute | solution.py:29
  27.9 2.6 %collective-permute-start.5 = (bf16[180,256]{1,0:T(8,128)(2,1)S(1)}, bf16[180,256]{1,0:T(8,128)(2,1)S(1)}, u32[]{:S(2)}, u32[]{:S(2)}) collective-permute-start(bf16[180,256]{1,0:T(8,128)(2,1)S(1)} %bitcast.38), channel_id=1, source_target_pairs={{0,16},{2,18},{4,20},{6,22},{8,24},{10,26},{12,28},{14,30},{16,0},... | collective-permute-start | bytes 276488 | tf_op jit(solution)/shard_map/ppermute | solution.py:29
  30.5 1.2 %collective-permute-start.2 = (bf16[4,180,256]{2,1,0:T(8,128)(2,1)}, bf16[4,180,256]{2,1,0:T(8,128)(2,1)S(1)}, u32[]{:S(2)}, u32[]{:S(2)}) collective-permute-start(bf16[4,180,256]{2,1,0:T(8,128)(2,1)} %get-tuple-element.30), channel_id=1, source_target_pairs={{0,4},{2,6},{4,0},{6,2},{8,12},{10,14},{12,8},{14,10},{16,20},{18,... | collective-permute-start | bytes 1105928 | tf_op jit(solution)/shard_map/ppermute | solution.py:29
  31.7 2.3 %collective-permute-start.3 = (bf16[4,180,256]{2,1,0:T(8,128)(2,1)}, bf16[4,180,256]{2,1,0:T(8,128)(2,1)}, u32[]{:S(2)}, u32[]{:S(2)}) collective-permute-start(bf16[4,180,256]{2,1,0:T(8,128)(2,1)} %get-tuple-element.31), channel_id=1, source_target_pairs={{0,6},{2,4},{4,2},{6,0},{8,14},{10,12},{12,10},{14,8},{16,22},{18,... | collective-permute-start | bytes 1105928 | tf_op jit(solution)/shard_map/ppermute | solution.py:29
  34.0 0.9 add_convert_fusion
  35.7 1.6 %collective-permute-start.12 = (bf16[256,256]{1,0:T(8,128)(2,1)S(1)}, bf16[256,256]{1,0:T(8,128)(2,1)}, u32[]{:S(2)}, u32[]{:S(2)}) collective-permute-start(bf16[256,256]{1,0:T(8,128)(2,1)S(1)} %pad_maximum_fusion.refs_4_), channel_id=1, source_target_pairs={{0,2},{2,0},{4,6},{6,4},{8,10},{10,8},{12,14},{14,12},{16,18},{18,... | collective-permute-start | bytes 393224 | tf_op jit(solution)/shard_map/ppermute | solution.py:29
  37.4 4.0 %collective-permute-done.6.refs_7_ = bf16[180,256]{1,0:T(8,128)(2,1)S(1)} collective-permute-done((bf16[180,256]{1,0:T(8,128)(2,1)S(1)}, bf16[180,256]{1,0:T(8,128)(2,1)S(1)}, u32[]{:S(2)}, u32[]{:S(2)}) %collective-permute-start.6) | collective-permute-done | bytes 92192 | tf_op jit(solution)/shard_map/ppermute | solution.py:29
  42.6 0.8 collective-permute-start.14
  43.5 8.9 %collective-permute-done.2.refs_2_ = bf16[4,180,256]{2,1,0:T(8,128)(2,1)S(1)} collective-permute-done((bf16[4,180,256]{2,1,0:T(8,128)(2,1)}, bf16[4,180,256]{2,1,0:T(8,128)(2,1)S(1)}, u32[]{:S(2)}, u32[]{:S(2)}) %collective-permute-start.2) | collective-permute-done | bytes 368672 | tf_op jit(solution)/shard_map/ppermute | solution.py:29
  52.4 0.9 copy-done.13
  53.3 0.9 copy-done.15
  54.2 2.5 %value.1 = (f32[256,256]{1,0:T(8,128)S(1)}, f32[256,256]{1,0:T(8,128)}, f32[256,256]{1,0:T(8,128)}, f32[256,256]{1,0:T(8,128)}) custom-call(s32[1]{0:T(128)} %bitcast.3.far, bf16[4,180,256]{2,1,0:T(8,128)(2,1)S(1)} %get-tuple-element.28.refs_0_, bf16[4,180,256]{2,1,0:T(8,128)(2,1)S(1)} %collective-permute-done.1.refs_1_, ...), custom_call_target="tpu_custom_call" | custom-call | tf_op jit(solution)/shard_map/value/pallas_call | solution.py:249
  56.7 0.7 copy-done.8
  57.5 1.7 %collective-permute-start.7 = (f32[256,256]{1,0:T(8,128)}, f32[256,256]{1,0:T(8,128)}, u32[]{:S(2)}, u32[]{:S(2)}) collective-permute-start(f32[256,256]{1,0:T(8,128)} %get-tuple-element.33), channel_id=1, source_target_pairs={{0,2},{2,0},{4,6},{6,4},{8,10},{10,8},{12,14},{14,12},{16,18},{18,... | collective-permute-start | bytes 786440 | tf_op jit(solution)/shard_map/ppermute | solution.py:29
  59.8 1.1 %collective-permute-start.9 = (f32[256,256]{1,0:T(8,128)}, f32[256,256]{1,0:T(8,128)}, u32[]{:S(2)}, u32[]{:S(2)}) collective-permute-start(f32[256,256]{1,0:T(8,128)} %get-tuple-element.35), channel_id=1, source_target_pairs={{0,6},{2,4},{4,2},{6,0},{8,14},{10,12},{12,10},{14,8},{16,22},{18,... | collective-permute-start | bytes 786440 | tf_op jit(solution)/shard_map/ppermute | solution.py:29
  61.0 2.4 %outer.1 = (f32[180,256]{1,0:T(8,128)S(1)}, bf16[180,256]{1,0:T(8,128)(2,1)S(1)}, bf16[180,256]{1,0:T(8,128)(2,1)}, bf16[180,256]{1,0:T(8,128)(2,1)S(1)}) custom-call(s32[1]{0:T(128)} %bitcast.3.far, bf16[4,180,256]{2,1,0:T(8,128)(2,1)S(1)} %get-tuple-element.28.refs_0_, bf16[4,180,256]{2,1,0:T(8,128)(2,1)S(1)} %collective-permute-done.1.refs_1_, ...), custom_call_target="tpu_custom_call" | custom-call | tf_op jit(solution)/shard_map/outer/pallas_call | solution.py:219
  64.5 4.1 %collective-permute-done.15.refs_0_ = bf16[180,256]{1,0:T(8,128)(2,1)S(1)} collective-permute-done((bf16[180,256]{1,0:T(8,128)(2,1)S(1)}, bf16[180,256]{1,0:T(8,128)(2,1)S(1)}, u32[]{:S(2)}, u32[]{:S(2)}) %collective-permute-start.15) | collective-permute-done | bytes 92192 | tf_op jit(solution)/shard_map/ppermute | solution.py:29
  68.8 1.4 %collective-permute-done.16.refs_1_ = bf16[180,256]{1,0:T(8,128)(2,1)S(1)} collective-permute-done((bf16[180,256]{1,0:T(8,128)(2,1)}, bf16[180,256]{1,0:T(8,128)(2,1)S(1)}, u32[]{:S(2)}, u32[]{:S(2)}) %collective-permute-start.16) | collective-permute-done | bytes 92192 | tf_op jit(solution)/shard_map/ppermute | solution.py:29
  70.2 4.8 %collective-permute-done.17.refs_2_ = bf16[180,256]{1,0:T(8,128)(2,1)S(1)} collective-permute-done((bf16[180,256]{1,0:T(8,128)(2,1)S(1)}, bf16[180,256]{1,0:T(8,128)(2,1)S(1)}, u32[]{:S(2)}, u32[]{:S(2)}) %collective-permute-start.17) | collective-permute-done | bytes 92192 | tf_op jit(solution)/shard_map/ppermute | solution.py:29
  75.0 0.9 copy-done.11
  76.2 1.1 %collective-permute-done.18 = f32[1,128]{1,0:T(1,128)S(1)} collective-permute-done((f32[1,128]{1,0:T(1,128)S(1)}, f32[1,128]{1,0:T(1,128)S(1)}, u32[]{:S(2)}, u32[]{:S(2)}) %collective-permute-start.18) | collective-permute-done | bytes 544 | tf_op jit(solution)/shard_map/ppermute | solution.py:29
  77.4 1.7 %collective-permute-start.19 = (f32[1,128]{1,0:T(1,128)S(1)}, f32[1,128]{1,0:T(1,128)S(1)}, u32[]{:S(2)}, u32[]{:S(2)}) collective-permute-start(f32[1,128]{1,0:T(1,128)S(1)} %add.23), channel_id=1, source_target_pairs={{0,2},{2,0},{4,6},{6,4},{8,10},{10,8},{12,14},{14,12},{16,18},{18,... | collective-permute-start | bytes 1544 | tf_op jit(solution)/shard_map/ppermute | solution.py:29
  79.1 1.8 %collective-permute-done.19 = f32[1,128]{1,0:T(1,128)S(1)} collective-permute-done((f32[1,128]{1,0:T(1,128)S(1)}, f32[1,128]{1,0:T(1,128)S(1)}, u32[]{:S(2)}, u32[]{:S(2)}) %collective-permute-start.19) | collective-permute-done | bytes 544 | tf_op jit(solution)/shard_map/ppermute | solution.py:29
  80.9 0.9 collective-permute-start.20
  81.9 2.6 %collective-permute-done.20 = f32[1,128]{1,0:T(1,128)S(1)} collective-permute-done((f32[1,128]{1,0:T(1,128)S(1)}, f32[1,128]{1,0:T(1,128)S(1)}, u32[]{:S(2)}, u32[]{:S(2)}) %collective-permute-start.20) | collective-permute-done | bytes 544 | tf_op jit(solution)/shard_map/ppermute | solution.py:29
  84.5 0.9 copy.25
  85.5 0.9 copy.24
  86.5 0.9 copy.23
  89.3 0.7 collective-permute-start.22
  90.2 0.9 copy-done.9
  91.1 1.2 %join.1 = (bf16[128,256]{1,0:T(8,128)(2,1)S(1)}, bf16[128,256]{1,0:T(8,128)(2,1)S(1)}) custom-call(f32[256,256]{1,0:T(8,128)S(1)} %copy-done.9, f32[256,256]{1,0:T(8,128)} %collective-permute-done.7.refs_1_, f32[256,256]{1,0:T(8,128)} %collective-permute-done.8.refs_2_, f32[256,256]{1,0:T(8,128)} %collective-permute-done.9.refs_3_), custom_call_target="tpu_custom_call" | custom-call | tf_op jit(solution)/shard_map/join/pallas_call | solution.py:271
  92.3 1.6 %collective-permute-done.22 = f32[1,128]{1,0:T(1,128)S(1)} collective-permute-done((f32[1,128]{1,0:T(1,128)S(1)}, f32[1,128]{1,0:T(1,128)S(1)}, u32[]{:S(2)}, u32[]{:S(2)}) %collective-permute-start.22) | collective-permute-done | bytes 544 | tf_op jit(solution)/shard_map/ppermute | solution.py:29
  93.9 3.6 %collective-permute-start.10 = (bf16[128,256]{1,0:T(8,128)(2,1)S(1)}, bf16[128,256]{1,0:T(8,128)(2,1)S(1)}, u32[]{:S(2)}, u32[]{:S(2)}) collective-permute-start(bf16[128,256]{1,0:T(8,128)(2,1)S(1)} %get-tuple-element.36.vhi), channel_id=1, source_target_pairs={{0,2},{2,4},{4,6},{6,8},{8,10},{10,12},{12,14},{14,16},{16,18},{18... | collective-permute-start | bytes 196616 | tf_op jit(solution)/shard_map/ppermute | solution.py:35
  97.6 1.6 %shard_map.131.refs_0_ = bf16[256,2048]{1,0:T(8,128)(2,1)} custom-call(bf16[32,256,128]{2,1,0:T(8,128)(2,1)S(1)} %copy-done.3, bf16[128,256]{1,0:T(8,128)(2,1)S(1)} %get-tuple-element.37.vlo.vhi, bf16[128,256]{1,0:T(8,128)(2,1)S(1)} %get-tuple-element.36.vhi), custom_call_target="tpu_custom_call" | custom-call | tf_op jit(solution)/shard_map/pallas_call | solution.py:160
  99.3 1.6 %adam.1 = (f32[180,256]{1,0:T(8,128)}, f32[180,256]{1,0:T(8,128)}, f32[180,256]{1,0:T(8,128)}) custom-call(s32[1]{0:T(128)} %bitcast.8.slot, f32[2]{0:T(128)S(1)} %pad_maximum_fusion.1.fixes, f32[1,128]{1,0:T(1,128)S(1)} %add.27.squares, f32[180,256]{1,0:T(8,128)S(1)} %get-tuple-element.46.refs_0_, f32[180,256]{1,0:T(8,128)S(1)} %bitcast.32, ...), custom_call_target="tpu_custom_call" | custom-call | tf_op jit(solution)/shard_map/adam/pallas_call | solution.py:331
  100.9 1.6 %shard_map.132 = bf16[256,2048]{1,0:T(8,128)(2,1)} custom-call(bf16[32,256,128]{2,1,0:T(8,128)(2,1)S(1)} %get-tuple-element.27.probs, bf16[128,256]{1,0:T(8,128)(2,1)S(1)} %collective-permute-done.10.vlo, bf16[128,256]{1,0:T(8,128)(2,1)S(1)} %get-tuple-element.37.vlo.vhi, bf16[256,2048]{1,0:T(8,128)(2,1)} %shard_map.131.refs_0_), custom_call_target="tpu_custom_call", output_to_operand_aliasing={{}: (3, {})} | custom-call | tf_op jit(solution)/shard_map/pallas_call | solution.py:160
  (69 shorter events, 7.0 us)
Async XLA Ops:
  0.6 14.6 %collective-permute-start = (bf16[256,256]{1,0:T(8,128)(2,1)}, bf16[256,256]{1,0:T(8,128)(2,1)S(1)}, u32[]{:S(2)}, u32[]{:S(2)}) collective-permute-start(bf16[256,256]{1,0:T(8,128)(2,1)} %bitcast.27), channel_id=1, source_target_pairs={{0,2},{2,4},{4,6},{6,8},{8,10},{10,12},{12,14},{14,16},{16,18},{18... | collective-permute-start | bytes 393224 | tf_op jit(solution)/shard_map/ppermute | solution.py:35
  5.5 1.2 %copy-start = (bf16[1,256,2048]{2,1,0:T(8,128)(2,1)S(1)}, bf16[1,256,2048]{2,1,0:T(8,128)(2,1)}, u32[]{:S(2)}) copy-start(bf16[1,256,2048]{2,1,0:T(8,128)(2,1)} %param.11) | copy-start | bytes 3145732
  6.7 1.2 %copy-start.1 = (bf16[1,256,2048]{2,1,0:T(8,128)(2,1)S(1)}, bf16[1,256,2048]{2,1,0:T(8,128)(2,1)}, u32[]{:S(2)}) copy-start(bf16[1,256,2048]{2,1,0:T(8,128)(2,1)} %param.13) | copy-start | bytes 3145732
  8.0 0.9 copy-start.5
  8.9 0.7 copy-start.16
  9.6 0.7 copy-start.17
  10.2 5.0 %copy-start.6 = (bf16[1,256,256]{2,1,0:T(8,128)(2,1)S(1)}, bf16[1,256,256]{2,1,0:T(8,128)(2,1)}, u32[]{:S(2)}) copy-start(bf16[1,256,256]{2,1,0:T(8,128)(2,1)} %param.12) | copy-start | bytes 393220
  13.9 1.3 %copy-start.2 = (bf16[32,256,128]{2,1,0:T(8,128)(2,1)}, bf16[32,256,128]{2,1,0:T(8,128)(2,1)S(1)}, u32[]{:S(2)}) copy-start(bf16[32,256,128]{2,1,0:T(8,128)(2,1)S(1)} %get-tuple-element.38.probs) | copy-start | bytes 6291460
  15.2 4.4 %copy-start.7 = (f32[256,256]{1,0:T(8,128)}, f32[256,256]{1,0:T(8,128)S(1)}, u32[]{:S(2)}) copy-start(f32[256,256]{1,0:T(8,128)S(1)} %get-tuple-element.40) | copy-start | bytes 786436
  15.2 10.8 %copy-start.18 = (f32[1,180,256]{2,0,1:T(1,128)S(1)}, f32[1,180,256]{2,0,1:T(1,128)}, u32[]{:S(2)}) copy-start(f32[1,180,256]{2,0,1:T(1,128)} %param.17) | copy-start | bytes 552964
  19.6 12.2 %collective-permute-start.11 = (f32[128,256]{1,0:T(8,128)}, f32[128,256]{1,0:T(8,128)S(1)}, u32[]{:S(2)}, u32[]{:S(2)}) collective-permute-start(f32[128,256]{1,0:T(8,128)} %get-tuple-element.51), channel_id=1, source_target_pairs={{2,0},{4,2},{6,4},{8,6},{10,8},{12,10},{14,12},{16,14},{18,16},{20... | collective-permute-start | bytes 393224 | tf_op jit(solution)/shard_map/ppermute | solution.py:35
  20.9 1.4 %copy-start.4 = (bf16[1,256,2880]{1,2,0:T(8,128)(2,1)S(1)}, bf16[1,256,2880]{1,2,0:T(8,128)(2,1)}, u32[]{:S(2)}) copy-start(bf16[1,256,2880]{1,2,0:T(8,128)(2,1)} %param.10) | copy-start | bytes 4423684
  22.2 12.8 %copy-start.19 = (bf16[128,256]{1,0:T(8,128)(2,1)S(1)}, bf16[128,256]{1,0:T(8,128)(2,1)}, u32[]{:S(2)}) copy-start(bf16[128,256]{1,0:T(8,128)(2,1)} %get-tuple-element.50) | copy-start | bytes 196612
  23.3 19.3 %collective-permute-start.1 = (bf16[4,180,256]{2,1,0:T(8,128)(2,1)S(1)}, bf16[4,180,256]{2,1,0:T(8,128)(2,1)S(1)}, u32[]{:S(2)}, u32[]{:S(2)}) collective-permute-start(bf16[4,180,256]{2,1,0:T(8,128)(2,1)S(1)} %get-tuple-element.29), channel_id=1, source_target_pairs={{0,2},{2,0},{4,6},{6,4},{8,10},{10,8},{12,14},{14,12},{16,18},{18,... | collective-permute-start | bytes 1105928 | tf_op jit(solution)/shard_map/ppermute | solution.py:29
  26.0 8.9 %collective-permute-start.4 = (bf16[180,256]{1,0:T(8,128)(2,1)S(1)}, bf16[180,256]{1,0:T(8,128)(2,1)S(1)}, u32[]{:S(2)}, u32[]{:S(2)}) collective-permute-start(bf16[180,256]{1,0:T(8,128)(2,1)S(1)} %bitcast.37), channel_id=1, source_target_pairs={{0,8},{2,10},{4,12},{6,14},{8,0},{10,2},{12,4},{14,6},{16,24},{18,... | collective-permute-start | bytes 276488 | tf_op jit(solution)/shard_map/ppermute | solution.py:29
  27.9 7.1 %collective-permute-start.5 = (bf16[180,256]{1,0:T(8,128)(2,1)S(1)}, bf16[180,256]{1,0:T(8,128)(2,1)S(1)}, u32[]{:S(2)}, u32[]{:S(2)}) collective-permute-start(bf16[180,256]{1,0:T(8,128)(2,1)S(1)} %bitcast.38), channel_id=1, source_target_pairs={{0,16},{2,18},{4,20},{6,22},{8,24},{10,26},{12,28},{14,30},{16,0},... | collective-permute-start | bytes 276488 | tf_op jit(solution)/shard_map/ppermute | solution.py:29
  30.5 21.9 %collective-permute-start.2 = (bf16[4,180,256]{2,1,0:T(8,128)(2,1)}, bf16[4,180,256]{2,1,0:T(8,128)(2,1)S(1)}, u32[]{:S(2)}, u32[]{:S(2)}) collective-permute-start(bf16[4,180,256]{2,1,0:T(8,128)(2,1)} %get-tuple-element.30), channel_id=1, source_target_pairs={{0,4},{2,6},{4,0},{6,2},{8,12},{10,14},{12,8},{14,10},{16,20},{18,... | collective-permute-start | bytes 1105928 | tf_op jit(solution)/shard_map/ppermute | solution.py:29
  31.7 20.7 %collective-permute-start.3 = (bf16[4,180,256]{2,1,0:T(8,128)(2,1)}, bf16[4,180,256]{2,1,0:T(8,128)(2,1)}, u32[]{:S(2)}, u32[]{:S(2)}) collective-permute-start(bf16[4,180,256]{2,1,0:T(8,128)(2,1)} %get-tuple-element.31), channel_id=1, source_target_pairs={{0,6},{2,4},{4,2},{6,0},{8,14},{10,12},{12,10},{14,8},{16,22},{18,... | collective-permute-start | bytes 1105928 | tf_op jit(solution)/shard_map/ppermute | solution.py:29
  34.9 6.4 %collective-permute-start.6 = (bf16[180,256]{1,0:T(8,128)(2,1)S(1)}, bf16[180,256]{1,0:T(8,128)(2,1)S(1)}, u32[]{:S(2)}, u32[]{:S(2)}) collective-permute-start(bf16[180,256]{1,0:T(8,128)(2,1)S(1)} %bitcast.39), channel_id=1, source_target_pairs={{0,24},{2,26},{4,28},{6,30},{8,16},{10,18},{12,20},{14,22},{16,8},... | collective-permute-start | bytes 276488 | tf_op jit(solution)/shard_map/ppermute | solution.py:29
  35.1 0.6 copy-start.12
  35.7 24.1 %collective-permute-start.12 = (bf16[256,256]{1,0:T(8,128)(2,1)S(1)}, bf16[256,256]{1,0:T(8,128)(2,1)}, u32[]{:S(2)}, u32[]{:S(2)}) collective-permute-start(bf16[256,256]{1,0:T(8,128)(2,1)S(1)} %pad_maximum_fusion.refs_4_), channel_id=1, source_target_pairs={{0,2},{2,0},{4,6},{6,4},{8,10},{10,8},{12,14},{14,12},{16,18},{18,... | collective-permute-start | bytes 393224 | tf_op jit(solution)/shard_map/ppermute | solution.py:29
  41.4 0.6 copy-start.14
  42.0 18.9 %collective-permute-start.13 = (bf16[256,256]{1,0:T(8,128)(2,1)S(1)}, bf16[256,256]{1,0:T(8,128)(2,1)}, u32[]{:S(2)}, u32[]{:S(2)}) collective-permute-start(bf16[256,256]{1,0:T(8,128)(2,1)S(1)} %pad_maximum_fusion.refs_4_), channel_id=1, source_target_pairs={{0,4},{2,6},{4,0},{6,2},{8,12},{10,14},{12,8},{14,10},{16,20},{18,... | collective-permute-start | bytes 393224 | tf_op jit(solution)/shard_map/ppermute | solution.py:29
  42.6 18.3 %collective-permute-start.14 = (bf16[256,256]{1,0:T(8,128)(2,1)S(1)}, bf16[256,256]{1,0:T(8,128)(2,1)}, u32[]{:S(2)}, u32[]{:S(2)}) collective-permute-start(bf16[256,256]{1,0:T(8,128)(2,1)S(1)} %pad_maximum_fusion.refs_4_), channel_id=1, source_target_pairs={{0,6},{2,4},{4,2},{6,0},{8,14},{10,12},{12,10},{14,8},{16,22},{18,... | collective-permute-start | bytes 393224 | tf_op jit(solution)/shard_map/ppermute | solution.py:29
  52.4 0.9 copy-start.13
  53.3 0.9 copy-start.15
  56.7 0.7 copy-start.8
  57.5 30.6 %collective-permute-start.7 = (f32[256,256]{1,0:T(8,128)}, f32[256,256]{1,0:T(8,128)}, u32[]{:S(2)}, u32[]{:S(2)}) collective-permute-start(f32[256,256]{1,0:T(8,128)} %get-tuple-element.33), channel_id=1, source_target_pairs={{0,2},{2,0},{4,6},{6,4},{8,10},{10,8},{12,14},{14,12},{16,18},{18,... | collective-permute-start | bytes 786440 | tf_op jit(solution)/shard_map/ppermute | solution.py:29
  59.2 29.4 %collective-permute-start.8 = (f32[256,256]{1,0:T(8,128)}, f32[256,256]{1,0:T(8,128)}, u32[]{:S(2)}, u32[]{:S(2)}) collective-permute-start(f32[256,256]{1,0:T(8,128)} %get-tuple-element.34), channel_id=1, source_target_pairs={{0,4},{2,6},{4,0},{6,2},{8,12},{10,14},{12,8},{14,10},{16,20},{18,... | collective-permute-start | bytes 786440 | tf_op jit(solution)/shard_map/ppermute | solution.py:29
  59.8 29.5 %collective-permute-start.9 = (f32[256,256]{1,0:T(8,128)}, f32[256,256]{1,0:T(8,128)}, u32[]{:S(2)}, u32[]{:S(2)}) collective-permute-start(f32[256,256]{1,0:T(8,128)} %get-tuple-element.35), channel_id=1, source_target_pairs={{0,6},{2,4},{4,2},{6,0},{8,14},{10,12},{12,10},{14,8},{16,22},{18,... | collective-permute-start | bytes 786440 | tf_op jit(solution)/shard_map/ppermute | solution.py:29
  63.4 0.7 copy-start.10
  64.0 4.6 %collective-permute-start.15 = (bf16[180,256]{1,0:T(8,128)(2,1)S(1)}, bf16[180,256]{1,0:T(8,128)(2,1)S(1)}, u32[]{:S(2)}, u32[]{:S(2)}) collective-permute-start(bf16[180,256]{1,0:T(8,128)(2,1)S(1)} %get-tuple-element.42), channel_id=1, source_target_pairs={{0,8},{2,10},{4,12},{6,14},{8,0},{10,2},{12,4},{14,6},{16,24},{18,... | collective-permute-start | bytes 276488 | tf_op jit(solution)/shard_map/ppermute | solution.py:29
  64.5 5.7 %collective-permute-start.16 = (bf16[180,256]{1,0:T(8,128)(2,1)}, bf16[180,256]{1,0:T(8,128)(2,1)S(1)}, u32[]{:S(2)}, u32[]{:S(2)}) collective-permute-start(bf16[180,256]{1,0:T(8,128)(2,1)} %get-tuple-element.43), channel_id=1, source_target_pairs={{0,16},{2,18},{4,20},{6,22},{8,24},{10,26},{12,28},{14,30},{16,0},... | collective-permute-start | bytes 276488 | tf_op jit(solution)/shard_map/ppermute | solution.py:29
  68.6 6.4 %collective-permute-start.17 = (bf16[180,256]{1,0:T(8,128)(2,1)S(1)}, bf16[180,256]{1,0:T(8,128)(2,1)S(1)}, u32[]{:S(2)}, u32[]{:S(2)}) collective-permute-start(bf16[180,256]{1,0:T(8,128)(2,1)S(1)} %get-tuple-element.44), channel_id=1, source_target_pairs={{0,24},{2,26},{4,28},{6,30},{8,16},{10,18},{12,20},{14,22},{16,8},... | collective-permute-start | bytes 276488 | tf_op jit(solution)/shard_map/ppermute | solution.py:29
  68.8 28.8 %copy-start.3 = (bf16[32,256,128]{2,1,0:T(8,128)(2,1)S(1)}, bf16[32,256,128]{2,1,0:T(8,128)(2,1)}, u32[]{:S(2)}) copy-start(bf16[32,256,128]{2,1,0:T(8,128)(2,1)} %copy-done.2) | copy-start | bytes 6291460
  75.0 0.9 copy-start.11
  76.1 1.2 %collective-permute-start.18 = (f32[1,128]{1,0:T(1,128)S(1)}, f32[1,128]{1,0:T(1,128)S(1)}, u32[]{:S(2)}, u32[]{:S(2)}) collective-permute-start(f32[1,128]{1,0:T(1,128)S(1)} %get-tuple-element.45), channel_id=1, source_target_pairs={{0,1},{1,0},{2,3},{3,2},{4,5},{5,4},{6,7},{7,6},{8,9},{9,8},{10,11... | collective-permute-start | bytes 1544 | tf_op jit(solution)/shard_map/ppermute | solution.py:29
  77.4 3.6 %collective-permute-start.19 = (f32[1,128]{1,0:T(1,128)S(1)}, f32[1,128]{1,0:T(1,128)S(1)}, u32[]{:S(2)}, u32[]{:S(2)}) collective-permute-start(f32[1,128]{1,0:T(1,128)S(1)} %add.23), channel_id=1, source_target_pairs={{0,2},{2,0},{4,6},{6,4},{8,10},{10,8},{12,14},{14,12},{16,18},{18,... | collective-permute-start | bytes 1544 | tf_op jit(solution)/shard_map/ppermute | solution.py:29
  80.9 3.6 %collective-permute-start.20 = (f32[1,128]{1,0:T(1,128)S(1)}, f32[1,128]{1,0:T(1,128)S(1)}, u32[]{:S(2)}, u32[]{:S(2)}) collective-permute-start(f32[1,128]{1,0:T(1,128)S(1)} %add.24), channel_id=1, source_target_pairs={{0,4},{2,6},{4,0},{6,2},{8,12},{10,14},{12,8},{14,10},{16,20},{18,... | collective-permute-start | bytes 1544 | tf_op jit(solution)/shard_map/ppermute | solution.py:29
  84.5 3.6 %collective-permute-start.21 = (f32[1,128]{1,0:T(1,128)S(1)}, f32[1,128]{1,0:T(1,128)S(1)}, u32[]{:S(2)}, u32[]{:S(2)}) collective-permute-start(f32[1,128]{1,0:T(1,128)S(1)} %add.25), channel_id=1, source_target_pairs={{0,8},{2,10},{4,12},{6,14},{8,0},{10,2},{12,4},{14,6},{16,24},{18,... | collective-permute-start | bytes 1544 | tf_op jit(solution)/shard_map/ppermute | solution.py:29
  85.5 13.8 %collective-permute-start.24 = (f32[180,256]{1,0:T(8,128)S(1)}, f32[180,256]{1,0:T(8,128)S(1)}, u32[]{:S(2)}, u32[]{:S(2)}) collective-permute-start(f32[180,256]{1,0:T(8,128)S(1)} %bitcast.31), channel_id=1, source_target_pairs={{0,1},{1,0},{2,3},{3,2},{4,5},{5,4},{6,7},{7,6},{8,9},{9,8},{10,11... | collective-permute-start | bytes 552968 | tf_op jit(solution)/shard_map/ppermute | solution.py:29
  88.1 11.2 %collective-permute-start.25 = (f32[180,256]{1,0:T(8,128)S(1)}, f32[180,256]{1,0:T(8,128)S(1)}, u32[]{:S(2)}, u32[]{:S(2)}) collective-permute-start(f32[180,256]{1,0:T(8,128)S(1)} %bitcast.33), channel_id=1, source_target_pairs={{0,1},{1,0},{2,3},{3,2},{4,5},{5,4},{6,7},{7,6},{8,9},{9,8},{10,11... | collective-permute-start | bytes 552968 | tf_op jit(solution)/shard_map/ppermute | solution.py:29
  88.1 11.2 %collective-permute-start.26 = (f32[180,256]{1,0:T(8,128)S(1)}, f32[180,256]{1,0:T(8,128)S(1)}, u32[]{:S(2)}, u32[]{:S(2)}) collective-permute-start(f32[180,256]{1,0:T(8,128)S(1)} %bitcast.35), channel_id=1, source_target_pairs={{0,1},{1,0},{2,3},{3,2},{4,5},{5,4},{6,7},{7,6},{8,9},{9,8},{10,11... | collective-permute-start | bytes 552968 | tf_op jit(solution)/shard_map/ppermute | solution.py:29
  88.6 10.6 %collective-permute-start.23 = (f32[180,256]{1,0:T(8,128)S(1)}, f32[180,256]{1,0:T(8,128)S(1)}, u32[]{:S(2)}, u32[]{:S(2)}) collective-permute-start(f32[180,256]{1,0:T(8,128)S(1)} %get-tuple-element.46.refs_0_), channel_id=1, source_target_pairs={{0,1},{1,0},{2,3},{3,2},{4,5},{5,4},{6,7},{7,6},{8,9},{9,8},{10,11... | collective-permute-start | bytes 552968 | tf_op jit(solution)/shard_map/ppermute | solution.py:29
  89.3 4.5 %collective-permute-start.22 = (f32[1,128]{1,0:T(1,128)S(1)}, f32[1,128]{1,0:T(1,128)S(1)}, u32[]{:S(2)}, u32[]{:S(2)}) collective-permute-start(f32[1,128]{1,0:T(1,128)S(1)} %add.26), channel_id=1, source_target_pairs={{0,16},{2,18},{4,20},{6,22},{8,24},{10,26},{12,28},{14,30},{16,0},... | collective-permute-start | bytes 1544 | tf_op jit(solution)/shard_map/ppermute | solution.py:29
  90.1 1.0 copy-start.9
  93.9 7.0 %collective-permute-start.10 = (bf16[128,256]{1,0:T(8,128)(2,1)S(1)}, bf16[128,256]{1,0:T(8,128)(2,1)S(1)}, u32[]{:S(2)}, u32[]{:S(2)}) collective-permute-start(bf16[128,256]{1,0:T(8,128)(2,1)S(1)} %get-tuple-element.36.vhi), channel_id=1, source_target_pairs={{0,2},{2,4},{4,6},{6,8},{8,10},{10,12},{12,14},{14,16},{16,18},{18... | collective-permute-start | bytes 196616 | tf_op jit(solution)/shard_map/ppermute | solution.py:35

commit v2 on v1

v2 whole, which is shorter than its diff:
```python
import functools

import jax
import jax.numpy as jnp
from jax import lax
from jax.experimental import pallas as pl
from jax.experimental.pallas import tpu as pltpu
from jax.sharding import PartitionSpec as P


HD = 64
QH = 32
KH = 4
LOOKBACK_SPAN = 128
LANES = 128

beta_one = 0.9
beta_two = 0.95
adam_eps = 1e-08
learn_rate = 0.01
clip_norm = 0.5

bf16 = jnp.bfloat16
f32 = jnp.float32


def swapped(array, axis, mask):
    pairs = [(i, i ^ mask) for i in range(lax.axis_size(axis))]
    return lax.ppermute(array, axis, pairs)


def shifted(array, axis, by):
    devices = lax.axis_size(axis)
    pairs = [(i, i + by) for i in range(devices) if 0 <= i + by < devices]
    return lax.ppermute(array, axis, pairs)


VMEM = pl.BlockSpec(memory_space=pltpu.VMEM)
SMEM = pl.BlockSpec(memory_space=pltpu.SMEM)


def in_hbm(*arrays):
    return [pltpu.with_memory_space_constraint(a, pltpu.HBM) for a in arrays]


def params(mib):
    return pltpu.CompilerParams(vmem_limit_bytes=mib << 20)


def full(shape, dtype):
    return jax.ShapeDtypeStruct(shape, dtype)


def probs_body(bands, pos, query, cotan, prev, klo, khi, probs_out, send, mine):
    block = LOOKBACK_SPAN
    group = QH // KH
    pairs = group // 2
    index, step = pl.program_id(0), pl.program_id(1)
    span = 2 * block
    left = lax.broadcasted_iota(jnp.int32, (span, LANES), 1) < HD
    lower = jnp.where(index == 0, prev[...].astype(f32), klo[...].astype(f32))
    keyed = jnp.concatenate([lower, khi[...].astype(f32)], 0) * HD ** (-0.5)
    rolled = pltpu.roll(keyed, HD, 1)
    dist = (
        lax.broadcasted_iota(jnp.int32, (span, block), 1)
        + block
        - lax.broadcasted_iota(jnp.int32, (span, block), 0)
    )
    dist = jnp.where(dist < 0, 2 * span, dist)
    row = pos[...]
    sums = []
    for half in range(2):
        one, two = (keyed, rolled) if half == 0 else (rolled, keyed)
        sides = (
            jnp.where(left, one, 0.0).astype(bf16),
            jnp.where(left, 0.0, two).astype(bf16),
        )
        base = half * group * HD
        cols = [slice(base + p * LANES, base + (p + 1) * LANES) for p in range(pairs)]
        queries = jnp.concatenate([query[:, c] for c in cols], 0)
        cotans = jnp.concatenate([cotan[:, c] for c in cols], 0)
        for odd, side in enumerate(sides):
            scores = lax.dot_general(
                side, queries, (((1,), (1,)), ((), ())), preferred_element_type=f32
            )
            rows = []
            for p in range(pairs):
                head = half * group + 2 * p + odd
                limit = jnp.minimum(row, bands[step * 2 * group + head])
                seen = jnp.where(
                    dist <= limit, scores[:, p * block : (p + 1) * block], -1e30
                )
                expo = jnp.exp(seen - jnp.max(seen, axis=0, keepdims=True))
                prob = (expo * (1.0 / jnp.sum(expo, axis=0, keepdims=True))).astype(bf16)
                probs_out[0, head] = prob
                rows.append(prob)
            sums.append(
                lax.dot_general(
                    jnp.concatenate(rows, 1),
                    cotans,
                    (((1,), (0,)), ((), ())),
                    preferred_element_type=f32,
                )
            )
    grad = jnp.where(
        left,
        sums[0] + pltpu.roll(sums[1], HD, 1),
        sums[3] + pltpu.roll(sums[2], HD, 1),
    )
    for b in range(mine.shape[0] // block):
        for s in range(mine.shape[1] // LANES):
            here = slice(b * block, (b + 1) * block)
            cols = slice(s * LANES, (s + 1) * LANES)

            @pl.when((index == b) & (step == s))
            def _():
                mine[here, cols] = grad[block:]
                if b:
                    before = slice((b - 1) * block, b * block)
                    mine[before, cols] = mine[before, cols] + grad[:block]
                else:
                    send[:, cols] = grad[:block]


def probs_call(bands, positions, queries, out_grad, prev_keys, keys):
    block = LOOKBACK_SPAN
    tokens = queries.shape[0]
    blocks = tokens // block
    wide = 2 * (QH // KH) * HD
    heads = 2 * (QH // KH)
    bands, positions, queries, out_grad, keys = in_hbm(
        bands, positions, queries, out_grad, keys
    )
    return pl.pallas_call(
        probs_body,
        grid=(blocks, KH // 2),
        in_specs=[
            SMEM,
            pl.BlockSpec((1, block), lambda b, s: (0, b)),
            pl.BlockSpec((block, wide), lambda b, s: (b, s)),
            pl.BlockSpec((block, wide), lambda b, s: (b, s)),
            pl.BlockSpec((block, LANES), lambda b, s: (blocks - 1, s)),
            pl.BlockSpec((block, LANES), lambda b, s: (jnp.maximum(b - 1, 0), s)),
            pl.BlockSpec((block, LANES), lambda b, s: (b, s)),
        ],
        out_specs=[
            pl.BlockSpec((1, heads, 2 * block, block), lambda b, s: (b, s, 0, 0)),
            pl.BlockSpec((block, KH * HD), lambda b, s: (0, 0)),
            pl.BlockSpec((tokens, KH * HD), lambda b, s: (0, 0)),
        ],
        out_shape=[
            pltpu.HBM((blocks, QH, 2 * block, block), bf16),
            full((block, KH * HD), f32),
            full((tokens, KH * HD), f32),
        ],
        compiler_params=params(12),
        name="probs",
    )(bands, positions, queries, out_grad, prev_keys, keys, keys)


def mix_body(probs, vlo, vhi, *refs):
    out = refs[-1]
    group = QH // KH
    pairs = group // 2
    block = LOOKBACK_SPAN
    valued = jnp.concatenate([vlo[...], vhi[...]], 0).astype(f32)
    turned = valued.T.astype(bf16)
    for half in range(2):
        left = turned[half * HD : (half + 1) * HD]
        for p in range(pairs):
            head = half * group + 2 * p
            both = jnp.concatenate([probs[0, head], probs[0, head + 1]], 1)
            res = lax.dot_general(
                left, both, (((1,), (0,)), ((), ())), preferred_element_type=f32
            )
            stacked = jnp.concatenate([res[:, :block], res[:, block:]], 0)
            base = half * group * HD + p * LANES
            out[:, base : base + LANES] = stacked.T.astype(bf16)


def mix_call(probs, lower, lo, values, first, count, into):
    block = LOOKBACK_SPAN
    tokens = values.shape[0]
    wide = 2 * (QH // KH) * HD
    heads = 2 * (QH // KH)
    extra = [] if into is None else [into]
    return pl.pallas_call(
        mix_body,
        grid=(count, KH // 2),
        in_specs=[
            pl.BlockSpec((1, heads, 2 * block, block), lambda b, s: (b + first, s, 0, 0)),
            pl.BlockSpec((block, LANES), lambda b, s: (b + lo, s)),
            pl.BlockSpec((block, LANES), lambda b, s: (b + first, s)),
        ]
        + [pl.BlockSpec(memory_space=pltpu.HBM)] * len(extra),
        out_specs=pl.BlockSpec((block, wide), lambda b, s: (b + first, s)),
        out_shape=pltpu.HBM((tokens, QH * HD), bf16),
        input_output_aliases={3: 0} if extra else {},
        compiler_params=params(8),
    )(*in_hbm(probs), lower, values, *extra)


def cut_body(quad, acts, weight, *refs):
    outs, narrow = refs[:quad], refs[quad]
    whole, shards, sems = refs[quad + 1 :]
    devices, rows = shards.shape[:2]
    far_size = devices // quad
    part = whole.shape[0] // sems.shape[0]
    copies = []
    for c in range(sems.shape[0]):
        copy = pltpu.make_async_copy(
            acts.at[pl.ds(c * part, part), :], whole.at[pl.ds(c * part, part), :], sems.at[c]
        )
        copy.start()
        copies.append(copy)
    narrow[...] = weight[...].reshape(narrow.shape).astype(bf16)
    per = devices // sems.shape[0]
    for c, copy in enumerate(copies):
        copy.wait()
        for j in range(c * per, (c + 1) * per):
            shards[j] = whole[j * rows : (j + 1) * rows, :]
    mine = lax.axis_index("ctx") & (quad - 1)
    for m in range(quad):
        for z in range(far_size):
            outs[m][z] = shards[z * quad + (mine ^ m)]


def cut_call(turned, weight, devices, quad):
    width, tokens = turned.shape
    rows = width // devices
    turned, weight = in_hbm(turned, weight)
    return pl.pallas_call(
        functools.partial(cut_body, quad),
        in_specs=[pl.BlockSpec(memory_space=pltpu.HBM), VMEM],
        out_specs=[VMEM] * (quad + 1),
        out_shape=[full((devices // quad, rows, tokens), bf16)] * quad
        + [full((rows, weight.shape[2]), bf16)],
        scratch_shapes=[
            pltpu.VMEM((width, tokens), bf16),
            pltpu.VMEM((devices, rows, tokens), bf16),
            pltpu.SemaphoreType.DMA((4,)),
        ],
        compiler_params=params(8),
        name="cut",
    )(turned, weight)


def far_index(quad):
    return lax.axis_index("ctx") >> (quad.bit_length() - 1)


def outer_body(quad, far_size, *refs):
    turned, grads, outs = refs[:quad], refs[quad : 2 * quad], refs[2 * quad :]
    mine = far_index(quad)
    for k in range(far_size):
        z = mine ^ k
        total = None
        for m in range(quad):
            term = lax.dot_general(
                turned[m][z], grads[m][...], (((1,), (0,)), ((), ())), preferred_element_type=f32
            )
            total = term if total is None else total + term
        outs[k][...] = total.astype(outs[k].dtype)


def outer_call(turned, grads):
    quad = len(turned)
    far_size, rows, _ = turned[0].shape
    wide = grads[0].shape[1]
    return pl.pallas_call(
        functools.partial(outer_body, quad, far_size),
        in_specs=[VMEM] * (2 * quad),
        out_specs=[VMEM] * far_size,
        out_shape=[full((rows, wide), f32 if k == 0 else bf16) for k in range(far_size)],
        compiler_params=params(8),
        name="outer",
    )(*turned, *grads)


def value_body(quad, far_size, *refs):
    turned, weights, outs = refs[:quad], refs[quad : quad + far_size], refs[quad + far_size :]
    mine = far_index(quad)
    for m in range(quad):
        total = None
        for k in range(far_size):
            term = lax.dot_general(
                turned[m][mine ^ k],
                weights[k][...],
                (((0,), (0,)), ((), ())),
                preferred_element_type=f32,
            )
            total = term if total is None else total + term
        outs[m][...] = total


def value_call(turned, weights):
    quad = len(turned)
    far_size, _, tokens = turned[0].shape
    wide = weights[0].shape[1]
    return pl.pallas_call(
        functools.partial(value_body, quad, far_size),
        in_specs=[VMEM] * (quad + far_size),
        out_specs=[VMEM] * quad,
        out_shape=[full((tokens, wide), f32)] * quad,
        compiler_params=params(8),
        name="value",
    )(*turned, *weights)


def join_body(count, *refs):
    parts, whole, tail = refs[:count], refs[count], refs[count + 1]
    total = parts[0][...]
    for part in parts[1:]:
        total = total + part[...]
    value = total.astype(bf16)
    whole[...] = value
    tail[...] = value[whole.shape[0] - tail.shape[0] :]


def join_call(parts):
    tokens, wide = parts[0].shape
    return pl.pallas_call(
        functools.partial(join_body, len(parts)),
        in_specs=[VMEM] * len(parts),
        out_specs=[VMEM] * 2,
        out_shape=[full((tokens, wide), bf16), full((LOOKBACK_SPAN, wide), bf16)],
        compiler_params=params(4),
        name="join",
    )(*parts)


def reduce_body(scale, own, *refs):
    others, total, square = refs[:-2], refs[-2], refs[-1]
    grad = own[...]
    for other in others:
        grad = grad + other[...].astype(f32)
    grad = grad * scale
    total[...] = grad
    lane = lax.broadcasted_iota(jnp.int32, square.shape, 1)
    square[...] = jnp.where(lane == lax.axis_index("work"), jnp.sum(grad * grad), 0.0)


def reduce_call(own, others, scale):
    return pl.pallas_call(
        functools.partial(reduce_body, scale),
        in_specs=[VMEM] * (1 + len(others)),
        out_specs=[VMEM] * 2,
        out_shape=[full(own.shape, f32), full((1, LANES), f32)],
        compiler_params=params(4),
        name="reduce",
    )(own, *others)


def pack_body(weight, first, second, out):
    for n, ref in enumerate((weight, first, second)):
        out[n] = ref[...].reshape(out.shape[1:])


def pack_call(weight, first, second):
    rows, _, wide = weight.shape
    return pl.pallas_call(
        pack_body,
        in_specs=[VMEM] * 3,
        out_specs=VMEM,
        out_shape=full((3, rows, wide), f32),
        compiler_params=params(4),
        name="pack",
    )(*in_hbm(weight, first, second))


def tree_sum(values):
    while len(values) > 1:
        values = [a + b for a, b in zip(values[::2], values[1::2])]
    return values[0]


def adam_body(workers, step, squares, *refs):
    grads, states, outs = refs[:workers], refs[workers : 2 * workers], refs[2 * workers :]
    shape = grads[0].shape
    count = jnp.full((8, shape[1]), step[0].astype(f32))
    fix_one = (1.0 - jnp.power(f32(beta_one), count))[:1]
    fix_two = (1.0 - jnp.power(f32(beta_two), count))[:1]
    slot = lax.axis_index("work")
    results = []
    for w in range(workers):
        norm = jnp.sqrt(jnp.full((8, shape[1]), squares[0, slot ^ w]))
        factor = jnp.minimum(1.0, clip_norm / (norm + 1e-06))
        grad = grads[w][...] * factor[:1]
        weight, first, second = states[w][0], states[w][1], states[w][2]
        first = beta_one * first + (1.0 - beta_one) * grad
        second = beta_two * second + (1.0 - beta_two) * grad * grad
        weight = weight - learn_rate * (first / fix_one) / (
            jnp.sqrt(second / fix_two) + adam_eps
        )
        results.append((weight, first, second))
    for out, values in zip(outs, zip(*results)):
        out[...] = tree_sum(list(values)) / workers


def adam_call(step, squares, grads, states):
    workers = len(states)
    shape = grads[0].shape
    return pl.pallas_call(
        functools.partial(adam_body, workers),
        in_specs=[SMEM] * 2 + [VMEM] * (2 * workers),
        out_specs=[VMEM] * 3,
        out_shape=[full(shape, f32)] * 3,
        compiler_params=params(8),
        name="adam",
    )(step, squares, *grads, *states)


def per_device(
    inputs, queries, keys, out_grad, positions, bands, step, value_weight, moment_one, moment_two
):
    tokens = inputs.shape[1]
    block = LOOKBACK_SPAN
    devices = lax.axis_size("ctx")
    workers = lax.axis_size("work")
    quad = min(4, devices)
    far_size = devices // quad
    weight, first, second = (
        jnp.transpose(a, (1, 0, 2)) for a in (value_weight, moment_one, moment_two)
    )

    *turned, narrow = cut_call(inputs[0].T, weight, devices, quad)
    turned = [turned[0]] + [swapped(turned[m], "ctx", m) for m in range(1, quad)]
    prev_keys = shifted(keys[0], "ctx", 1)
    column = [narrow] + [swapped(narrow, "ctx", k * quad) for k in range(1, far_size)]

    probs, send, mine = probs_call(bands, positions, queries[0], out_grad[0], prev_keys, keys[0])
    returned = shifted(send, "ctx", -1)
    last = tokens - block
    value_grad = jnp.concatenate([mine[:last], mine[last:] + returned], 0).astype(bf16)
    value_grads = [value_grad] + [swapped(value_grad, "ctx", m) for m in range(1, quad)]

    pieces = value_call(turned, column)
    parts = outer_call(turned, value_grads)
    others = [swapped(parts[k], "ctx", k * quad) for k in range(1, far_size)]

    pieces = [pieces[0]] + [swapped(pieces[m], "ctx", m) for m in range(1, quad)]
    values, tail = join_call(pieces)
    prev_values = shifted(tail, "ctx", 1)
    blocks = tokens // block
    out = None
    if blocks > 1:
        out = mix_call(probs, values, 0, values, 1, blocks - 1, None)
    out = mix_call(probs, prev_values, 0, values, 0, 1, out)

    state = pack_call(weight, first, second)
    states = [state] + [swapped(state, "work", w) for w in range(1, workers)]
    grad, squares = reduce_call(parts[0], others, 1.0 / (tokens * devices))
    grads = [grad] + [swapped(grad, "work", w) for w in range(1, workers)]
    for axis, size in (("work", workers), ("ctx", devices)):
        bit = size // 2
        while bit:
            squares = squares + swapped(squares, axis, bit)
            bit //= 2
    mean_weight, mean_one, mean_two = adam_call(step, squares, grads, states)
    return (out[None], mean_weight, mean_one, mean_two)


def solution(mesh):
    in_specs = (
        P("work", "ctx", None),
        P("work", "ctx", None),
        P("work", "ctx", None),
        P("work", "ctx", None),
        P("work", "ctx"),
        P(),
        P(),
        P("work", "ctx", None),
        P("work", "ctx", None),
        P("work", "ctx", None),
    )
    out_specs = (P("work", "ctx", None), P("ctx", None), P("ctx", None), P("ctx", None))
    return jax.shard_map(
        per_device, mesh=mesh, in_specs=in_specs, out_specs=out_specs, check_vma=False
    )
```

time: 103 us -> 96.8 us (0.940)
  local copies, waits for them, and re-layouts: 16.6 us -> 0.01 us
  starting transfers between devices: 31.8 us -> 44.8 us
  waiting for transfers between devices: 31.3 us -> 29.3 us
  other arithmetic: 1.73 us -> 0.04 us
  Pallas kernels: 19.6 us -> 21 us
    unnamed x44 -> x0, local copies, waits for them, and re-layouts: 16.6 us -> none
    ppermute x24 -> x22, starting transfers between devices: 22 us -> 35.7 us  [swapped(): return lax.ppermute(array, axis, pairs)]
    ppermute x24 -> x22, waiting for transfers between devices: 31.3 us -> 26.2 us  [swapped(): return lax.ppermute(array, axis, pairs)]
    ppermute x3, waiting for transfers between devices: 0.01 us -> 3.05 us  [shifted(): return lax.ppermute(array, axis, pairs)]
    pallas_call x9, Pallas kernels: 18.4 us -> 20.9 us  [the longest x1 8.35 us: probs_call(): pl.pallas_call(probs_body, grid=(blocks, KH // 2), in_specs=[SMEM, pl.Blo...]
    convert_element_type x2 -> x0, other arithmetic: 1.62 us -> none  [per_device(): rows.append((grads[b][block:] + after).astype(bf16))]
    pallas_call x1, Pallas kernels: 1.16 us -> 0.07 us  [join_call(): pl.pallas_call(functools.partial(join_body, len(parts)), in_specs=[VMEM]...]
  transfers between devices with their start and end apart: 27 -> 25, of which waited for: 10 -> 11; matrix products, arithmetic and copies ran while one was open for 4% -> 0% of each run, Pallas kernels for 14% -> 10%
where the time goes in v2:
time: 96.8 us; the launch traced here: 96.5 us
  starting transfers between devices  44.8 us (46%)
  waiting for transfers between devices  29.3 us (30%)
  Pallas kernels  21 us (22%)
  between operations  1.43 us (1%)
    ppermute x22, starting transfers between devices, swapped(): return lax.ppermute(array, axis, pairs)  35.7 us
    ppermute x22, waiting for transfers between devices, swapped(): return lax.ppermute(array, axis, pairs)  26.2 us
    ppermute x3, starting transfers between devices, shifted(): return lax.ppermute(array, axis, pairs)  9.1 us
    pallas_call x1, Pallas kernels, probs_call(): pl.pallas_call(probs_body, grid=(blocks, KH // 2), in_specs=[SMEM, pl.Blo...  8.35 us
    pallas_call x2, Pallas kernels, mix_call(): pl.pallas_call(mix_body, grid=(count, KH // 2), in_specs=[pl.BlockSpec((1...  5.63 us
    ppermute x3, waiting for transfers between devices, shifted(): return lax.ppermute(array, axis, pairs)  3.05 us
    pallas_call x1, Pallas kernels, cut_call(): pl.pallas_call(functools.partial(cut_body, quad), in_specs=[pl.BlockSpec(...  2.43 us
  transfers between devices with their start and end apart: 25, of which 11 were waited for; matrix products, arithmetic and copies ran while one was open for 0% of the time, Pallas kernels for 10%

profile of v2, /device:TPU:0, one launch (start us, length us, event | category | flops | bytes accessed | tf_op | source)
XLA Modules:
  0.0 96.5 jit_solution(5575167002250250393)
XLA Ops:
  0.6 4.9 %collective-permute-start = (bf16[256,256]{1,0:T(8,128)(2,1)}, bf16[256,256]{1,0:T(8,128)(2,1)S(1)}, u32[]{:S(2)}, u32[]{:S(2)}) collective-permute-start(bf16[256,256]{1,0:T(8,128)(2,1)} %bitcast.16), channel_id=1, source_target_pairs={{0,2},{2,4},{4,6},{6,8},{8,10},{10,12},{12,14},{14,16},{16,18},{18... | collective-permute-start | bytes 393224 | tf_op jit(solution)/shard_map/ppermute | solution.py:35
  5.5 3.0 %collective-permute-done.prev = bf16[256,256]{1,0:T(8,128)(2,1)S(1)} collective-permute-done((bf16[256,256]{1,0:T(8,128)(2,1)}, bf16[256,256]{1,0:T(8,128)(2,1)S(1)}, u32[]{:S(2)}, u32[]{:S(2)}) %collective-permute-start) | collective-permute-done | bytes 131104 | tf_op jit(solution)/shard_map/ppermute | solution.py:35
  8.6 8.4 %probs.1 = (bf16[2,32,256,128]{3,2,1,0:T(8,128)(2,1)}, f32[128,256]{1,0:T(8,128)S(1)}, f32[256,256]{1,0:T(8,128)S(1)}) custom-call(s32[32]{0:T(128)} %bands.1, s32[1,256]{1,0:T(1,128)} %pos.1, bf16[256,2048]{1,0:T(8,128)(2,1)} %bitcast.12, bf16[256,2048]{1,0:T(8,128)(2,1)} %bitcast.13, bf16[256,256]{1,0:T(8,128)(2,1)S(1)} %collective-permute-done.prev, ...), custom_call_target="tpu_custom_call" | custom-call | tf_op jit(solution)/shard_map/probs/pallas_call | solution.py:134
  16.9 1.3 %collective-permute-start.11 = (f32[128,256]{1,0:T(8,128)S(1)}, f32[128,256]{1,0:T(8,128)S(1)}, u32[]{:S(2)}, u32[]{:S(2)}) collective-permute-start(f32[128,256]{1,0:T(8,128)S(1)} %get-tuple-element.40), channel_id=1, source_target_pairs={{2,0},{4,2},{6,4},{8,6},{10,8},{12,10},{14,12},{16,14},{18,16},{20... | collective-permute-start | bytes 393224 | tf_op jit(solution)/shard_map/ppermute | solution.py:35
  18.2 2.4 %cut.1 = (bf16[4,180,256]{2,1,0:T(8,128)(2,1)S(1)}, bf16[4,180,256]{2,1,0:T(8,128)(2,1)S(1)}, bf16[4,180,256]{2,1,0:T(8,128)(2,1)S(1)}, bf16[4,180,256]{2,1,0:T(8,128)(2,1)S(1)}, bf16[180,256]{1,0:T(8,128)(2,1)S(1)}) custom-call(bf16[2880,256]{1,0:T(8,128)(2,1)} %bitcast.11, f32[180,1,256]{2,1,0:T(1,128)} %bitcast.14), custom_call_target="tpu_custom_call" | custom-call | tf_op jit(solution)/shard_map/cut/pallas_call | solution.py:232
  20.6 3.1 %collective-permute-start.1 = (bf16[4,180,256]{2,1,0:T(8,128)(2,1)S(1)}, bf16[4,180,256]{2,1,0:T(8,128)(2,1)S(1)}, u32[]{:S(2)}, u32[]{:S(2)}) collective-permute-start(bf16[4,180,256]{2,1,0:T(8,128)(2,1)S(1)} %get-tuple-element.29), channel_id=1, source_target_pairs={{0,2},{2,0},{4,6},{6,4},{8,10},{10,8},{12,14},{14,12},{16,18},{18,... | collective-permute-start | bytes 1105928 | tf_op jit(solution)/shard_map/ppermute | solution.py:29
  23.7 2.9 %collective-permute-start.2 = (bf16[4,180,256]{2,1,0:T(8,128)(2,1)S(1)}, bf16[4,180,256]{2,1,0:T(8,128)(2,1)S(1)}, u32[]{:S(2)}, u32[]{:S(2)}) collective-permute-start(bf16[4,180,256]{2,1,0:T(8,128)(2,1)S(1)} %get-tuple-element.30), channel_id=1, source_target_pairs={{0,4},{2,6},{4,0},{6,2},{8,12},{10,14},{12,8},{14,10},{16,20},{18,... | collective-permute-start | bytes 1105928 | tf_op jit(solution)/shard_map/ppermute | solution.py:29
  26.7 1.3 %pack.1.refs_2_ = f32[3,180,256]{2,1,0:T(8,128)S(1)} custom-call(f32[180,1,256]{2,1,0:T(1,128)} %bitcast.15, f32[180,1,256]{2,1,0:T(1,128)} %bitcast.19, f32[180,1,256]{2,1,0:T(1,128)} %bitcast.20), custom_call_target="tpu_custom_call" | custom-call | tf_op jit(solution)/shard_map/pack/pallas_call | solution.py:361
  27.9 0.1 collective-permute-start.24
  28.0 0.0 collective-permute-done.11
  28.1 1.5 %collective-permute-start.12 = (bf16[256,256]{1,0:T(8,128)(2,1)S(1)}, bf16[256,256]{1,0:T(8,128)(2,1)S(1)}, u32[]{:S(2)}, u32[]{:S(2)}) collective-permute-start(bf16[256,256]{1,0:T(8,128)(2,1)S(1)} %pad_maximum_fusion.refs_4_), channel_id=1, source_target_pairs={{0,2},{2,0},{4,6},{6,4},{8,10},{10,8},{12,14},{14,12},{16,18},{18,... | collective-permute-start | bytes 393224 | tf_op jit(solution)/shard_map/ppermute | solution.py:29
  29.6 4.1 %collective-permute-done.1.refs_1_ = bf16[4,180,256]{2,1,0:T(8,128)(2,1)S(1)} collective-permute-done((bf16[4,180,256]{2,1,0:T(8,128)(2,1)S(1)}, bf16[4,180,256]{2,1,0:T(8,128)(2,1)S(1)}, u32[]{:S(2)}, u32[]{:S(2)}) %collective-permute-start.1) | collective-permute-done | bytes 368672 | tf_op jit(solution)/shard_map/ppermute | solution.py:29
  33.7 3.1 %collective-permute-start.13 = (bf16[256,256]{1,0:T(8,128)(2,1)S(1)}, bf16[256,256]{1,0:T(8,128)(2,1)S(1)}, u32[]{:S(2)}, u32[]{:S(2)}) collective-permute-start(bf16[256,256]{1,0:T(8,128)(2,1)S(1)} %pad_maximum_fusion.refs_4_), channel_id=1, source_target_pairs={{0,4},{2,6},{4,0},{6,2},{8,12},{10,14},{12,8},{14,10},{16,20},{18,... | collective-permute-start | bytes 393224 | tf_op jit(solution)/shard_map/ppermute | solution.py:29
  36.8 7.4 %collective-permute-done.2.refs_2_ = bf16[4,180,256]{2,1,0:T(8,128)(2,1)S(1)} collective-permute-done((bf16[4,180,256]{2,1,0:T(8,128)(2,1)S(1)}, bf16[4,180,256]{2,1,0:T(8,128)(2,1)S(1)}, u32[]{:S(2)}, u32[]{:S(2)}) %collective-permute-start.2) | collective-permute-done | bytes 368672 | tf_op jit(solution)/shard_map/ppermute | solution.py:29
  44.2 1.6 %collective-permute-start.14 = (bf16[256,256]{1,0:T(8,128)(2,1)S(1)}, bf16[256,256]{1,0:T(8,128)(2,1)S(1)}, u32[]{:S(2)}, u32[]{:S(2)}) collective-permute-start(bf16[256,256]{1,0:T(8,128)(2,1)S(1)} %pad_maximum_fusion.refs_4_), channel_id=1, source_target_pairs={{0,6},{2,4},{4,2},{6,0},{8,14},{10,12},{12,10},{14,8},{16,22},{18,... | collective-permute-start | bytes 393224 | tf_op jit(solution)/shard_map/ppermute | solution.py:29
  45.8 0.0 collective-permute-done.3.refs_3_
  45.8 0.9 collective-permute-start.4
  46.7 2.8 %collective-permute-start.5 = (bf16[180,256]{1,0:T(8,128)(2,1)S(1)}, bf16[180,256]{1,0:T(8,128)(2,1)S(1)}, u32[]{:S(2)}, u32[]{:S(2)}) collective-permute-start(bf16[180,256]{1,0:T(8,128)(2,1)S(1)} %get-tuple-element.32.refs_4_), channel_id=1, source_target_pairs={{0,16},{2,18},{4,20},{6,22},{8,24},{10,26},{12,28},{14,30},{16,0},... | collective-permute-start | bytes 276488 | tf_op jit(solution)/shard_map/ppermute | solution.py:29
  49.5 1.6 %collective-permute-start.6 = (bf16[180,256]{1,0:T(8,128)(2,1)S(1)}, bf16[180,256]{1,0:T(8,128)(2,1)S(1)}, u32[]{:S(2)}, u32[]{:S(2)}) collective-permute-start(bf16[180,256]{1,0:T(8,128)(2,1)S(1)} %get-tuple-element.32.refs_4_), channel_id=1, source_target_pairs={{0,24},{2,26},{4,28},{6,30},{8,16},{10,18},{12,20},{14,22},{16,8},... | collective-permute-start | bytes 276488 | tf_op jit(solution)/shard_map/ppermute | solution.py:29
  51.0 0.0 collective-permute-done.14.refs_7_
  51.0 0.6 outer.1
  51.6 0.3 collective-permute-start.15
  51.9 2.6 %collective-permute-start.16 = (bf16[180,256]{1,0:T(8,128)(2,1)S(1)}, bf16[180,256]{1,0:T(8,128)(2,1)S(1)}, u32[]{:S(2)}, u32[]{:S(2)}) collective-permute-start(bf16[180,256]{1,0:T(8,128)(2,1)S(1)} %get-tuple-element.43), channel_id=1, source_target_pairs={{0,16},{2,18},{4,20},{6,22},{8,24},{10,26},{12,28},{14,30},{16,0},... | collective-permute-start | bytes 276488 | tf_op jit(solution)/shard_map/ppermute | solution.py:29
  54.5 2.0 %collective-permute-done.6.refs_7_ = bf16[180,256]{1,0:T(8,128)(2,1)S(1)} collective-permute-done((bf16[180,256]{1,0:T(8,128)(2,1)S(1)}, bf16[180,256]{1,0:T(8,128)(2,1)S(1)}, u32[]{:S(2)}, u32[]{:S(2)}) %collective-permute-start.6) | collective-permute-done | bytes 92192 | tf_op jit(solution)/shard_map/ppermute | solution.py:29
  56.5 0.8 value.1
  57.3 1.4 %collective-permute-start.7 = (f32[256,256]{1,0:T(8,128)S(1)}, f32[256,256]{1,0:T(8,128)S(1)}, u32[]{:S(2)}, u32[]{:S(2)}) collective-permute-start(f32[256,256]{1,0:T(8,128)S(1)} %get-tuple-element.34), channel_id=1, source_target_pairs={{0,2},{2,0},{4,6},{6,4},{8,10},{10,8},{12,14},{14,12},{16,18},{18,... | collective-permute-start | bytes 786440 | tf_op jit(solution)/shard_map/ppermute | solution.py:29
  58.7 1.0 %collective-permute-start.8 = (f32[256,256]{1,0:T(8,128)S(1)}, f32[256,256]{1,0:T(8,128)S(1)}, u32[]{:S(2)}, u32[]{:S(2)}) collective-permute-start(f32[256,256]{1,0:T(8,128)S(1)} %get-tuple-element.35), channel_id=1, source_target_pairs={{0,4},{2,6},{4,0},{6,2},{8,12},{10,14},{12,8},{14,10},{16,20},{18,... | collective-permute-start | bytes 786440 | tf_op jit(solution)/shard_map/ppermute | solution.py:29
  59.7 1.1 %collective-permute-start.9 = (f32[256,256]{1,0:T(8,128)S(1)}, f32[256,256]{1,0:T(8,128)S(1)}, u32[]{:S(2)}, u32[]{:S(2)}) collective-permute-start(f32[256,256]{1,0:T(8,128)S(1)} %get-tuple-element.36), channel_id=1, source_target_pairs={{0,6},{2,4},{4,2},{6,0},{8,14},{10,12},{12,10},{14,8},{16,22},{18,... | collective-permute-start | bytes 786440 | tf_op jit(solution)/shard_map/ppermute | solution.py:29
  60.8 4.0 %collective-permute-start.17 = (bf16[180,256]{1,0:T(8,128)(2,1)S(1)}, bf16[180,256]{1,0:T(8,128)(2,1)S(1)}, u32[]{:S(2)}, u32[]{:S(2)}) collective-permute-start(bf16[180,256]{1,0:T(8,128)(2,1)S(1)} %get-tuple-element.44), channel_id=1, source_target_pairs={{0,24},{2,26},{4,28},{6,30},{8,16},{10,18},{12,20},{14,22},{16,8},... | collective-permute-start | bytes 276488 | tf_op jit(solution)/shard_map/ppermute | solution.py:29
  64.9 2.5 %collective-permute-done.17.refs_2_ = bf16[180,256]{1,0:T(8,128)(2,1)S(1)} collective-permute-done((bf16[180,256]{1,0:T(8,128)(2,1)S(1)}, bf16[180,256]{1,0:T(8,128)(2,1)S(1)}, u32[]{:S(2)}, u32[]{:S(2)}) %collective-permute-start.17) | collective-permute-done | bytes 92192 | tf_op jit(solution)/shard_map/ppermute | solution.py:29
  67.4 0.2 reduce.1
  67.7 0.1 collective-permute-start.23
  67.8 0.6 collective-permute-done.8.refs_2_
  68.3 0.1 join.1
  68.4 2.9 %collective-permute-start.10 = (bf16[128,256]{1,0:T(8,128)(2,1)S(1)}, bf16[128,256]{1,0:T(8,128)(2,1)S(1)}, u32[]{:S(2)}, u32[]{:S(2)}) collective-permute-start(bf16[128,256]{1,0:T(8,128)(2,1)S(1)} %get-tuple-element.37), channel_id=1, source_target_pairs={{0,2},{2,4},{4,6},{6,8},{8,10},{10,12},{12,14},{14,16},{16,18},{18... | collective-permute-start | bytes 196616 | tf_op jit(solution)/shard_map/ppermute | solution.py:35
  71.4 0.2 collective-permute-start.18
  71.6 1.0 %collective-permute-done.18 = f32[1,128]{1,0:T(1,128)S(1)} collective-permute-done((f32[1,128]{1,0:T(1,128)S(1)}, f32[1,128]{1,0:T(1,128)S(1)}, u32[]{:S(2)}, u32[]{:S(2)}) %collective-permute-start.18) | collective-permute-done | bytes 544 | tf_op jit(solution)/shard_map/ppermute | solution.py:29
  72.6 4.4 %collective-permute-start.19 = (f32[1,128]{1,0:T(1,128)S(1)}, f32[1,128]{1,0:T(1,128)S(1)}, u32[]{:S(2)}, u32[]{:S(2)}) collective-permute-start(f32[1,128]{1,0:T(1,128)S(1)} %add.19), channel_id=1, source_target_pairs={{0,16},{2,18},{4,20},{6,22},{8,24},{10,26},{12,28},{14,30},{16,0},... | collective-permute-start | bytes 1544 | tf_op jit(solution)/shard_map/ppermute | solution.py:29
  77.0 1.5 %collective-permute-done.19 = f32[1,128]{1,0:T(1,128)S(1)} collective-permute-done((f32[1,128]{1,0:T(1,128)S(1)}, f32[1,128]{1,0:T(1,128)S(1)}, u32[]{:S(2)}, u32[]{:S(2)}) %collective-permute-start.19) | collective-permute-done | bytes 544 | tf_op jit(solution)/shard_map/ppermute | solution.py:29
  78.5 1.0 %collective-permute-start.20 = (f32[1,128]{1,0:T(1,128)S(1)}, f32[1,128]{1,0:T(1,128)S(1)}, u32[]{:S(2)}, u32[]{:S(2)}) collective-permute-start(f32[1,128]{1,0:T(1,128)S(1)} %add.20), channel_id=1, source_target_pairs={{0,8},{2,10},{4,12},{6,14},{8,0},{10,2},{12,4},{14,6},{16,24},{18,... | collective-permute-start | bytes 1544 | tf_op jit(solution)/shard_map/ppermute | solution.py:29
  79.5 2.6 %collective-permute-done.20 = f32[1,128]{1,0:T(1,128)S(1)} collective-permute-done((f32[1,128]{1,0:T(1,128)S(1)}, f32[1,128]{1,0:T(1,128)S(1)}, u32[]{:S(2)}, u32[]{:S(2)}) %collective-permute-start.20) | collective-permute-done | bytes 544 | tf_op jit(solution)/shard_map/ppermute | solution.py:29
  82.1 0.6 collective-permute-start.21
  82.7 3.0 %collective-permute-done.21 = f32[1,128]{1,0:T(1,128)S(1)} collective-permute-done((f32[1,128]{1,0:T(1,128)S(1)}, f32[1,128]{1,0:T(1,128)S(1)}, u32[]{:S(2)}, u32[]{:S(2)}) %collective-permute-start.21) | collective-permute-done | bytes 544 | tf_op jit(solution)/shard_map/ppermute | solution.py:29
  85.7 1.4 %collective-permute-start.22 = (f32[1,128]{1,0:T(1,128)S(1)}, f32[1,128]{1,0:T(1,128)S(1)}, u32[]{:S(2)}, u32[]{:S(2)}) collective-permute-start(f32[1,128]{1,0:T(1,128)S(1)} %add.22), channel_id=1, source_target_pairs={{0,2},{2,0},{4,6},{6,4},{8,10},{10,8},{12,14},{14,12},{16,18},{18,... | collective-permute-start | bytes 1544 | tf_op jit(solution)/shard_map/ppermute | solution.py:29
  87.7 1.5 %collective-permute-done.22 = f32[1,128]{1,0:T(1,128)S(1)} collective-permute-done((f32[1,128]{1,0:T(1,128)S(1)}, f32[1,128]{1,0:T(1,128)S(1)}, u32[]{:S(2)}, u32[]{:S(2)}) %collective-permute-start.22) | collective-permute-done | bytes 544 | tf_op jit(solution)/shard_map/ppermute | solution.py:29
  89.2 2.8 %shard_map.129.refs_0_ = bf16[256,2048]{1,0:T(8,128)(2,1)} custom-call(bf16[2,32,256,128]{3,2,1,0:T(8,128)(2,1)} %get-tuple-element.27.probs, bf16[256,256]{1,0:T(8,128)(2,1)S(1)} %get-tuple-element.38.vlo.vhi, bf16[256,256]{1,0:T(8,128)(2,1)S(1)} %get-tuple-element.38.vlo.vhi), custom_call_target="tpu_custom_call" | custom-call | tf_op jit(solution)/shard_map/pallas_call | solution.py:187
  92.1 1.6 %adam.1 = (f32[180,256]{1,0:T(8,128)}, f32[180,256]{1,0:T(8,128)}, f32[180,256]{1,0:T(8,128)}) custom-call(s32[1]{0:T(128)S(6)} %copy.16.step, f32[1,128]{1,0:T(1,128)S(1)} %add.23.squares, f32[180,256]{1,0:T(8,128)S(1)} %get-tuple-element.46.refs_0_, f32[180,256]{1,0:T(8,128)S(1)} %collective-permute-done.23.refs_1_, f32[3,180,256]{2,1,0:T(8,128)S(1)} %pack.1.refs_2_, ...), custom_call_target="tpu_custom_call" | custom-call | tf_op jit(solution)/shard_map/adam/pallas_call | solution.py:403
  93.7 2.8 %shard_map.130 = bf16[256,2048]{1,0:T(8,128)(2,1)} custom-call(bf16[2,32,256,128]{3,2,1,0:T(8,128)(2,1)} %get-tuple-element.27.probs, bf16[128,256]{1,0:T(8,128)(2,1)S(1)} %collective-permute-done.10.vlo, bf16[256,256]{1,0:T(8,128)(2,1)S(1)} %get-tuple-element.38.vlo.vhi, bf16[256,2048]{1,0:T(8,128)(2,1)} %shard_map.129.refs_0_), custom_call_target="tpu_custom_call", output_to_operand_aliasing={{}: (3, {})} | custom-call | tf_op jit(solution)/shard_map/pallas_call | solution.py:187
  (20 shorter events, 0.1 us)
Async XLA Ops:
  0.6 7.9 %collective-permute-start = (bf16[256,256]{1,0:T(8,128)(2,1)}, bf16[256,256]{1,0:T(8,128)(2,1)S(1)}, u32[]{:S(2)}, u32[]{:S(2)}) collective-permute-start(bf16[256,256]{1,0:T(8,128)(2,1)} %bitcast.16), channel_id=1, source_target_pairs={{0,2},{2,4},{4,6},{6,8},{8,10},{10,12},{12,14},{14,16},{16,18},{18... | collective-permute-start | bytes 393224 | tf_op jit(solution)/shard_map/ppermute | solution.py:35
  16.9 11.1 %collective-permute-start.11 = (f32[128,256]{1,0:T(8,128)S(1)}, f32[128,256]{1,0:T(8,128)S(1)}, u32[]{:S(2)}, u32[]{:S(2)}) collective-permute-start(f32[128,256]{1,0:T(8,128)S(1)} %get-tuple-element.40), channel_id=1, source_target_pairs={{2,0},{4,2},{6,4},{8,6},{10,8},{12,10},{14,12},{16,14},{18,16},{20... | collective-permute-start | bytes 393224 | tf_op jit(solution)/shard_map/ppermute | solution.py:35
  20.6 13.1 %collective-permute-start.1 = (bf16[4,180,256]{2,1,0:T(8,128)(2,1)S(1)}, bf16[4,180,256]{2,1,0:T(8,128)(2,1)S(1)}, u32[]{:S(2)}, u32[]{:S(2)}) collective-permute-start(bf16[4,180,256]{2,1,0:T(8,128)(2,1)S(1)} %get-tuple-element.29), channel_id=1, source_target_pairs={{0,2},{2,0},{4,6},{6,4},{8,10},{10,8},{12,14},{14,12},{16,18},{18,... | collective-permute-start | bytes 1105928 | tf_op jit(solution)/shard_map/ppermute | solution.py:29
  23.7 20.5 %collective-permute-start.2 = (bf16[4,180,256]{2,1,0:T(8,128)(2,1)S(1)}, bf16[4,180,256]{2,1,0:T(8,128)(2,1)S(1)}, u32[]{:S(2)}, u32[]{:S(2)}) collective-permute-start(bf16[4,180,256]{2,1,0:T(8,128)(2,1)S(1)} %get-tuple-element.30), channel_id=1, source_target_pairs={{0,4},{2,6},{4,0},{6,2},{8,12},{10,14},{12,8},{14,10},{16,20},{18,... | collective-permute-start | bytes 1105928 | tf_op jit(solution)/shard_map/ppermute | solution.py:29
  26.7 19.1 %collective-permute-start.3 = (bf16[4,180,256]{2,1,0:T(8,128)(2,1)S(1)}, bf16[4,180,256]{2,1,0:T(8,128)(2,1)S(1)}, u32[]{:S(2)}, u32[]{:S(2)}) collective-permute-start(bf16[4,180,256]{2,1,0:T(8,128)(2,1)S(1)} %get-tuple-element.31), channel_id=1, source_target_pairs={{0,6},{2,4},{4,2},{6,0},{8,14},{10,12},{12,10},{14,8},{16,22},{18,... | collective-permute-start | bytes 1105928 | tf_op jit(solution)/shard_map/ppermute | solution.py:29
  27.9 64.1 %collective-permute-start.24 = (f32[3,180,256]{2,1,0:T(8,128)S(1)}, f32[3,180,256]{2,1,0:T(8,128)S(1)}, u32[]{:S(2)}, u32[]{:S(2)}) collective-permute-start(f32[3,180,256]{2,1,0:T(8,128)S(1)} %pack.1.refs_2_), channel_id=1, source_target_pairs={{0,1},{1,0},{2,3},{3,2},{4,5},{5,4},{6,7},{7,6},{8,9},{9,8},{10,11... | collective-permute-start | bytes 1658888 | tf_op jit(solution)/shard_map/ppermute | solution.py:29
  28.1 18.6 %collective-permute-start.12 = (bf16[256,256]{1,0:T(8,128)(2,1)S(1)}, bf16[256,256]{1,0:T(8,128)(2,1)S(1)}, u32[]{:S(2)}, u32[]{:S(2)}) collective-permute-start(bf16[256,256]{1,0:T(8,128)(2,1)S(1)} %pad_maximum_fusion.refs_4_), channel_id=1, source_target_pairs={{0,2},{2,0},{4,6},{6,4},{8,10},{10,8},{12,14},{14,12},{16,18},{18,... | collective-permute-start | bytes 393224 | tf_op jit(solution)/shard_map/ppermute | solution.py:29
  33.7 15.8 %collective-permute-start.13 = (bf16[256,256]{1,0:T(8,128)(2,1)S(1)}, bf16[256,256]{1,0:T(8,128)(2,1)S(1)}, u32[]{:S(2)}, u32[]{:S(2)}) collective-permute-start(bf16[256,256]{1,0:T(8,128)(2,1)S(1)} %pad_maximum_fusion.refs_4_), channel_id=1, source_target_pairs={{0,4},{2,6},{4,0},{6,2},{8,12},{10,14},{12,8},{14,10},{16,20},{18,... | collective-permute-start | bytes 393224 | tf_op jit(solution)/shard_map/ppermute | solution.py:29
  44.2 6.8 %collective-permute-start.14 = (bf16[256,256]{1,0:T(8,128)(2,1)S(1)}, bf16[256,256]{1,0:T(8,128)(2,1)S(1)}, u32[]{:S(2)}, u32[]{:S(2)}) collective-permute-start(bf16[256,256]{1,0:T(8,128)(2,1)S(1)} %pad_maximum_fusion.refs_4_), channel_id=1, source_target_pairs={{0,6},{2,4},{4,2},{6,0},{8,14},{10,12},{12,10},{14,8},{16,22},{18,... | collective-permute-start | bytes 393224 | tf_op jit(solution)/shard_map/ppermute | solution.py:29
  45.8 6.1 %collective-permute-start.4 = (bf16[180,256]{1,0:T(8,128)(2,1)S(1)}, bf16[180,256]{1,0:T(8,128)(2,1)S(1)}, u32[]{:S(2)}, u32[]{:S(2)}) collective-permute-start(bf16[180,256]{1,0:T(8,128)(2,1)S(1)} %get-tuple-element.32.refs_4_), channel_id=1, source_target_pairs={{0,8},{2,10},{4,12},{6,14},{8,0},{10,2},{12,4},{14,6},{16,24},{18,... | collective-permute-start | bytes 276488 | tf_op jit(solution)/shard_map/ppermute | solution.py:29
  46.7 7.8 %collective-permute-start.5 = (bf16[180,256]{1,0:T(8,128)(2,1)S(1)}, bf16[180,256]{1,0:T(8,128)(2,1)S(1)}, u32[]{:S(2)}, u32[]{:S(2)}) collective-permute-start(bf16[180,256]{1,0:T(8,128)(2,1)S(1)} %get-tuple-element.32.refs_4_), channel_id=1, source_target_pairs={{0,16},{2,18},{4,20},{6,22},{8,24},{10,26},{12,28},{14,30},{16,0},... | collective-permute-start | bytes 276488 | tf_op jit(solution)/shard_map/ppermute | solution.py:29
  49.5 7.0 %collective-permute-start.6 = (bf16[180,256]{1,0:T(8,128)(2,1)S(1)}, bf16[180,256]{1,0:T(8,128)(2,1)S(1)}, u32[]{:S(2)}, u32[]{:S(2)}) collective-permute-start(bf16[180,256]{1,0:T(8,128)(2,1)S(1)} %get-tuple-element.32.refs_4_), channel_id=1, source_target_pairs={{0,24},{2,26},{4,28},{6,30},{8,16},{10,18},{12,20},{14,22},{16,8},... | collective-permute-start | bytes 276488 | tf_op jit(solution)/shard_map/ppermute | solution.py:29
  51.6 8.1 %collective-permute-start.15 = (bf16[180,256]{1,0:T(8,128)(2,1)S(1)}, bf16[180,256]{1,0:T(8,128)(2,1)S(1)}, u32[]{:S(2)}, u32[]{:S(2)}) collective-permute-start(bf16[180,256]{1,0:T(8,128)(2,1)S(1)} %get-tuple-element.42), channel_id=1, source_target_pairs={{0,8},{2,10},{4,12},{6,14},{8,0},{10,2},{12,4},{14,6},{16,24},{18,... | collective-permute-start | bytes 276488 | tf_op jit(solution)/shard_map/ppermute | solution.py:29
  51.9 9.0 %collective-permute-start.16 = (bf16[180,256]{1,0:T(8,128)(2,1)S(1)}, bf16[180,256]{1,0:T(8,128)(2,1)S(1)}, u32[]{:S(2)}, u32[]{:S(2)}) collective-permute-start(bf16[180,256]{1,0:T(8,128)(2,1)S(1)} %get-tuple-element.43), channel_id=1, source_target_pairs={{0,16},{2,18},{4,20},{6,22},{8,24},{10,26},{12,28},{14,30},{16,0},... | collective-permute-start | bytes 276488 | tf_op jit(solution)/shard_map/ppermute | solution.py:29
  57.3 10.5 %collective-permute-start.7 = (f32[256,256]{1,0:T(8,128)S(1)}, f32[256,256]{1,0:T(8,128)S(1)}, u32[]{:S(2)}, u32[]{:S(2)}) collective-permute-start(f32[256,256]{1,0:T(8,128)S(1)} %get-tuple-element.34), channel_id=1, source_target_pairs={{0,2},{2,0},{4,6},{6,4},{8,10},{10,8},{12,14},{14,12},{16,18},{18,... | collective-permute-start | bytes 786440 | tf_op jit(solution)/shard_map/ppermute | solution.py:29
  58.7 9.6 %collective-permute-start.8 = (f32[256,256]{1,0:T(8,128)S(1)}, f32[256,256]{1,0:T(8,128)S(1)}, u32[]{:S(2)}, u32[]{:S(2)}) collective-permute-start(f32[256,256]{1,0:T(8,128)S(1)} %get-tuple-element.35), channel_id=1, source_target_pairs={{0,4},{2,6},{4,0},{6,2},{8,12},{10,14},{12,8},{14,10},{16,20},{18,... | collective-permute-start | bytes 786440 | tf_op jit(solution)/shard_map/ppermute | solution.py:29
  59.7 8.7 %collective-permute-start.9 = (f32[256,256]{1,0:T(8,128)S(1)}, f32[256,256]{1,0:T(8,128)S(1)}, u32[]{:S(2)}, u32[]{:S(2)}) collective-permute-start(f32[256,256]{1,0:T(8,128)S(1)} %get-tuple-element.36), channel_id=1, source_target_pairs={{0,6},{2,4},{4,2},{6,0},{8,14},{10,12},{12,10},{14,8},{16,22},{18,... | collective-permute-start | bytes 786440 | tf_op jit(solution)/shard_map/ppermute | solution.py:29
  60.8 6.6 %collective-permute-start.17 = (bf16[180,256]{1,0:T(8,128)(2,1)S(1)}, bf16[180,256]{1,0:T(8,128)(2,1)S(1)}, u32[]{:S(2)}, u32[]{:S(2)}) collective-permute-start(bf16[180,256]{1,0:T(8,128)(2,1)S(1)} %get-tuple-element.44), channel_id=1, source_target_pairs={{0,24},{2,26},{4,28},{6,30},{8,16},{10,18},{12,20},{14,22},{16,8},... | collective-permute-start | bytes 276488 | tf_op jit(solution)/shard_map/ppermute | solution.py:29
  67.7 24.4 %collective-permute-start.23 = (f32[180,256]{1,0:T(8,128)S(1)}, f32[180,256]{1,0:T(8,128)S(1)}, u32[]{:S(2)}, u32[]{:S(2)}) collective-permute-start(f32[180,256]{1,0:T(8,128)S(1)} %get-tuple-element.46.refs_0_), channel_id=1, source_target_pairs={{0,1},{1,0},{2,3},{3,2},{4,5},{5,4},{6,7},{7,6},{8,9},{9,8},{10,11... | collective-permute-start | bytes 552968 | tf_op jit(solution)/shard_map/ppermute | solution.py:29
  68.4 25.3 %collective-permute-start.10 = (bf16[128,256]{1,0:T(8,128)(2,1)S(1)}, bf16[128,256]{1,0:T(8,128)(2,1)S(1)}, u32[]{:S(2)}, u32[]{:S(2)}) collective-permute-start(bf16[128,256]{1,0:T(8,128)(2,1)S(1)} %get-tuple-element.37), channel_id=1, source_target_pairs={{0,2},{2,4},{4,6},{6,8},{8,10},{10,12},{12,14},{14,16},{16,18},{18... | collective-permute-start | bytes 196616 | tf_op jit(solution)/shard_map/ppermute | solution.py:35
  71.4 1.2 %collective-permute-start.18 = (f32[1,128]{1,0:T(1,128)S(1)}, f32[1,128]{1,0:T(1,128)S(1)}, u32[]{:S(2)}, u32[]{:S(2)}) collective-permute-start(f32[1,128]{1,0:T(1,128)S(1)} %get-tuple-element.45), channel_id=1, source_target_pairs={{0,1},{1,0},{2,3},{3,2},{4,5},{5,4},{6,7},{7,6},{8,9},{9,8},{10,11... | collective-permute-start | bytes 1544 | tf_op jit(solution)/shard_map/ppermute | solution.py:29
  72.6 5.9 %collective-permute-start.19 = (f32[1,128]{1,0:T(1,128)S(1)}, f32[1,128]{1,0:T(1,128)S(1)}, u32[]{:S(2)}, u32[]{:S(2)}) collective-permute-start(f32[1,128]{1,0:T(1,128)S(1)} %add.19), channel_id=1, source_target_pairs={{0,16},{2,18},{4,20},{6,22},{8,24},{10,26},{12,28},{14,30},{16,0},... | collective-permute-start | bytes 1544 | tf_op jit(solution)/shard_map/ppermute | solution.py:29
  78.5 3.6 %collective-permute-start.20 = (f32[1,128]{1,0:T(1,128)S(1)}, f32[1,128]{1,0:T(1,128)S(1)}, u32[]{:S(2)}, u32[]{:S(2)}) collective-permute-start(f32[1,128]{1,0:T(1,128)S(1)} %add.20), channel_id=1, source_target_pairs={{0,8},{2,10},{4,12},{6,14},{8,0},{10,2},{12,4},{14,6},{16,24},{18,... | collective-permute-start | bytes 1544 | tf_op jit(solution)/shard_map/ppermute | solution.py:29
  82.1 3.6 %collective-permute-start.21 = (f32[1,128]{1,0:T(1,128)S(1)}, f32[1,128]{1,0:T(1,128)S(1)}, u32[]{:S(2)}, u32[]{:S(2)}) collective-permute-start(f32[1,128]{1,0:T(1,128)S(1)} %add.21), channel_id=1, source_target_pairs={{0,4},{2,6},{4,0},{6,2},{8,12},{10,14},{12,8},{14,10},{16,20},{18,... | collective-permute-start | bytes 1544 | tf_op jit(solution)/shard_map/ppermute | solution.py:29
  85.7 3.6 %collective-permute-start.22 = (f32[1,128]{1,0:T(1,128)S(1)}, f32[1,128]{1,0:T(1,128)S(1)}, u32[]{:S(2)}, u32[]{:S(2)}) collective-permute-start(f32[1,128]{1,0:T(1,128)S(1)} %add.22), channel_id=1, source_target_pairs={{0,2},{2,0},{4,6},{6,4},{8,10},{10,8},{12,14},{14,12},{16,18},{18,... | collective-permute-start | bytes 1544 | tf_op jit(solution)/shard_map/ppermute | solution.py:29

commit v3 on v2

v3 whole, which is shorter than its diff:
```python
import functools

import jax
import jax.numpy as jnp
from jax import lax
from jax.experimental import pallas as pl
from jax.experimental.pallas import tpu as pltpu
from jax.sharding import PartitionSpec as P


HD = 64
QH = 32
KH = 4
LOOKBACK_SPAN = 128
LANES = 128
SUBLANES = 8

beta_one = 0.9
beta_two = 0.95
adam_eps = 1e-08
learn_rate = 0.01
clip_norm = 0.5

bf16 = jnp.bfloat16
f32 = jnp.float32


def swapped(array, axis, mask):
    pairs = [(i, i ^ mask) for i in range(lax.axis_size(axis))]
    return lax.ppermute(array, axis, pairs)


def shifted(array, axis, by):
    devices = lax.axis_size(axis)
    pairs = [(i, i + by) for i in range(devices) if 0 <= i + by < devices]
    return lax.ppermute(array, axis, pairs)


VMEM = pl.BlockSpec(memory_space=pltpu.VMEM)
SMEM = pl.BlockSpec(memory_space=pltpu.SMEM)


def in_hbm(*arrays):
    return [pltpu.with_memory_space_constraint(a, pltpu.HBM) for a in arrays]


def in_vmem(*arrays):
    return [pltpu.with_memory_space_constraint(a, pltpu.VMEM) for a in arrays]


def vmem(shape, dtype):
    return pltpu.VMEM(shape, dtype)


def params(mib):
    return pltpu.CompilerParams(vmem_limit_bytes=mib << 20)


def full(shape, dtype):
    return jax.ShapeDtypeStruct(shape, dtype)


def probs_body(first, lower_from, bands, pos, query, cotan, prev, keys, probs_out, *grads_out):
    block = LOOKBACK_SPAN
    group = QH // KH
    pairs = group // 2
    turn, step = pl.program_id(0), pl.program_id(1)
    index = turn + first
    at = pl.ds(pl.multiple_of(index * block, block), block)
    above = pl.ds(pl.multiple_of(turn * block, block), block)
    lanes = pl.ds(pl.multiple_of(step * LANES, LANES), LANES)
    left = lax.broadcasted_iota(jnp.int32, (2 * block, LANES), 1) < HD
    before = pl.ds(pl.multiple_of(turn * block, block) + lower_from, block)
    lower = prev[before, lanes].astype(f32)
    keyed = jnp.concatenate([lower, keys[at, lanes].astype(f32)], 0) * HD ** (-0.5)
    rolled = pltpu.roll(keyed, HD, 1)
    gap = lax.broadcasted_iota(jnp.int32, (block, block), 1) - lax.broadcasted_iota(
        jnp.int32, (block, block), 0
    )
    own = gap >= 0
    same = gap == 0
    dist = jnp.where(own, gap, gap + block)
    row = pos[index]
    sums = []
    for half in range(2):
        one, two = (keyed, rolled) if half == 0 else (rolled, keyed)
        sides = (
            jnp.where(left, one, 0.0).astype(bf16),
            jnp.where(left, 0.0, two).astype(bf16),
        )
        base = (step * 2 + half) * group * HD
        cols = [
            pl.ds(pl.multiple_of(base + p * LANES, LANES), LANES) for p in range(pairs)
        ]
        queries = jnp.concatenate([query[at, c] for c in cols], 0)
        cotans = jnp.concatenate([cotan[at, c] for c in cols], 0)
        for odd, side in enumerate(sides):
            scores = lax.dot_general(
                side, queries, (((1,), (1,)), ((), ())), preferred_element_type=f32
            )
            rows = []
            for p in range(pairs):
                head = half * group + 2 * p + odd
                limit = jnp.minimum(row, bands[step * 2 * group + head])
                before = scores[:block, p * block : (p + 1) * block]
                here = scores[block:, p * block : (p + 1) * block]
                seen = jnp.where(dist <= limit, jnp.where(own, here, before), -1e30)
                far = jnp.sum(jnp.where(same, before, 0.0), axis=0, keepdims=True)
                far = jnp.where(limit >= block, far, -1e30)
                top = jnp.maximum(jnp.max(seen, axis=0, keepdims=True), far)
                expo = jnp.exp(seen - top)
                far = jnp.exp(far - top)
                scale = 1.0 / (jnp.sum(expo, axis=0, keepdims=True) + far)
                prob = expo * scale
                prob = jnp.concatenate(
                    [
                        jnp.where(own, jnp.where(same, far * scale, 0.0), prob).astype(bf16),
                        jnp.where(own, prob, 0.0).astype(bf16),
                    ],
                    0,
                )
                probs_out[turn, step * 2 * group + head] = prob
                rows.append(prob)
            sums.append(
                lax.dot_general(
                    jnp.concatenate(rows, 1),
                    cotans,
                    (((1,), (0,)), ((), ())),
                    preferred_element_type=f32,
                )
            )
    grad = jnp.where(
        left,
        sums[0] + pltpu.roll(sums[1], HD, 1),
        sums[3] + pltpu.roll(sums[2], HD, 1),
    )
    low, high = grad[:block], grad[block:]
    if first == 0:
        grads_out[0][:, lanes] = low
        grads_out[1][:, lanes] = high
    else:
        rows, = grads_out

        @pl.when(turn == 0)
        def _():
            rows[above, lanes] = low

        @pl.when(turn > 0)
        def _():
            rows[above, lanes] = rows[above, lanes] + low

        rows[at, lanes] = high


def probs_call(bands, positions, queries, out_grad, lower, keys, first, count):
    block = LOOKBACK_SPAN
    tokens = queries.shape[0]
    wide = KH * HD
    return pl.pallas_call(
        functools.partial(probs_body, first, 0 if first else lower.shape[0] - block),
        grid=(count, KH // 2),
        in_specs=[SMEM] + [VMEM] * 5,
        out_specs=[VMEM] * (2 if first else 3),
        out_shape=[vmem((count, QH, 2 * block, block), bf16)]
        + ([vmem((tokens, wide), f32)] if first else [vmem((block, wide), f32)] * 2),
        compiler_params=params(8),
    )(bands, *in_vmem(positions, queries, out_grad, lower, keys))


def mix_body(first, probs, lower, values, *refs):
    out = refs[-1]
    group = QH // KH
    pairs = group // 2
    block = LOOKBACK_SPAN
    index, step = pl.program_id(0), pl.program_id(1)
    at = pl.ds(pl.multiple_of((index + first) * block, block), block)
    above = pl.ds(pl.multiple_of(index * block, block), block)
    lanes = pl.ds(pl.multiple_of(step * LANES, LANES), LANES)
    valued = jnp.concatenate([lower[above, lanes], values[at, lanes]], 0).astype(f32)
    turned = valued.T.astype(bf16)
    for half in range(2):
        left = turned[half * HD : (half + 1) * HD]
        for p in range(pairs):
            head = step * 2 * group + half * group + 2 * p
            both = jnp.concatenate(
                [probs[index, head], probs[index, head + 1]], 1
            )
            res = lax.dot_general(
                left, both, (((1,), (0,)), ((), ())), preferred_element_type=f32
            )
            stacked = jnp.concatenate([res[:, :block], res[:, block:]], 0)
            base = half * group * HD + p * LANES
            out[:, base : base + LANES] = stacked.astype(bf16).T


def mix_call(probs, lower, values, first, count, into):
    block = LOOKBACK_SPAN
    tokens = values.shape[0]
    wide = 2 * (QH // KH) * HD
    extra = [] if into is None else [into]
    return pl.pallas_call(
        functools.partial(mix_body, first),
        grid=(count, KH // 2),
        in_specs=[VMEM] * 3 + [pl.BlockSpec(memory_space=pltpu.HBM)] * len(extra),
        out_specs=pl.BlockSpec((block, wide), lambda b, s: (b + first, s)),
        out_shape=pltpu.HBM((tokens, QH * HD), bf16),
        input_output_aliases={3: 0} if extra else {},
        compiler_params=params(8),
    )(*in_vmem(probs, lower, values), *extra)


def window_size(rows):
    return -(-(rows + max(rows * j % SUBLANES for j in range(SUBLANES))) // SUBLANES) * SUBLANES


def window_of(index, rows, width):
    start = jnp.minimum(index * rows // SUBLANES * SUBLANES, width - window_size(rows))
    return pl.multiple_of(start, SUBLANES), index * rows - start


def cut_body(quad, acts, weight, *refs):
    outs, (narrow, wide_weight, sems) = refs[:quad], refs[quad:]
    width = acts.shape[0]
    far_size, size = outs[0].shape[:2]
    rows, _, wide = weight.shape
    mine = lax.axis_index("ctx")
    copies = []
    for m in range(quad):
        for z in range(far_size):
            start, _ = window_of(z * quad + ((mine & (quad - 1)) ^ m), rows, width)
            copy = pltpu.make_async_copy(
                acts.at[pl.ds(start, size), :], outs[m].at[z], sems.at[m * far_size + z]
            )
            copy.start()
            copies.append(copy)
    fetch = pltpu.make_async_copy(weight, wide_weight, sems.at[quad * far_size])
    fetch.start()
    fetch.wait()
    _, offset = window_of(mine, rows, width)
    padded = jnp.concatenate(
        [wide_weight[...].reshape(rows, wide), jnp.zeros((size - rows, wide), f32)], 0
    )
    narrow[...] = pltpu.roll(padded, offset, 0).astype(bf16)
    for copy in copies:
        copy.wait()


def cut_call(turned, weight, devices, quad):
    _, tokens = turned.shape
    rows, _, wide = weight.shape
    size = window_size(rows)
    res = pl.pallas_call(
        functools.partial(cut_body, quad),
        in_specs=[pl.BlockSpec(memory_space=pltpu.HBM)] * 2,
        out_specs=[VMEM] * (quad + 1),
        out_shape=[vmem((devices // quad, size, tokens), bf16)] * quad
        + [vmem((size, wide), bf16)],
        scratch_shapes=[
            pltpu.VMEM(weight.shape, f32),
            pltpu.SemaphoreType.DMA((devices + 1,)),
        ],
        compiler_params=params(8),
        name="cut",
    )(*in_hbm(turned, weight))
    return res[:quad], res[quad]


def load_body(count, *refs):
    sources, targets, sems = refs[:count], refs[count : 2 * count], refs[2 * count]
    copies = [
        pltpu.make_async_copy(source, target, sems.at[n])
        for n, (source, target) in enumerate(zip(sources, targets))
    ]
    for copy in copies:
        copy.start()
    for copy in copies:
        copy.wait()


def load_call(*arrays):
    count = len(arrays)
    return pl.pallas_call(
        functools.partial(load_body, count),
        in_specs=[pl.BlockSpec(memory_space=pltpu.HBM)] * count,
        out_specs=[VMEM] * count,
        out_shape=[vmem(a.shape, a.dtype) for a in arrays],
        scratch_shapes=[pltpu.SemaphoreType.DMA((count,))],
        compiler_params=params(2),
        name="load",
    )(*in_hbm(*arrays))


def far_index(quad):
    return lax.axis_index("ctx") >> (quad.bit_length() - 1)


def outer_body(quad, far_size, *refs):
    turned, grads, outs = refs[:quad], refs[quad : 2 * quad], refs[2 * quad :]
    mine = far_index(quad)
    near = lax.axis_index("ctx") & (quad - 1)
    rows = outs[0].shape[0]
    size = turned[0].shape[1]
    for k in range(far_size):
        z = mine ^ k
        total = None
        for m in range(quad):
            term = lax.dot_general(
                turned[m][z], grads[m][...], (((1,), (0,)), ((), ())), preferred_element_type=f32
            )
            total = term if total is None else total + term
        _, offset = window_of(z * quad + near, rows, rows * quad * far_size)
        total = pltpu.roll(total, (size - offset) % size, 0)
        outs[k][...] = total[:rows].astype(outs[k].dtype)


def outer_call(turned, grads, rows):
    quad = len(turned)
    far_size = turned[0].shape[0]
    wide = grads[0].shape[1]
    return pl.pallas_call(
        functools.partial(outer_body, quad, far_size),
        in_specs=[VMEM] * (2 * quad),
        out_specs=[VMEM] * far_size,
        out_shape=[full((rows, wide), f32 if k == 0 else bf16) for k in range(far_size)],
        compiler_params=params(8),
        name="outer",
    )(*turned, *grads)


def value_body(quad, far_size, *refs):
    turned, weights, outs = refs[:quad], refs[quad : quad + far_size], refs[quad + far_size :]
    mine = far_index(quad)
    for m in range(quad):
        total = None
        for k in range(far_size):
            term = lax.dot_general(
                turned[m][mine ^ k],
                weights[k][...],
                (((0,), (0,)), ((), ())),
                preferred_element_type=f32,
            )
            total = term if total is None else total + term
        outs[m][...] = total


def value_call(turned, weights):
    quad = len(turned)
    far_size, _, tokens = turned[0].shape
    wide = weights[0].shape[1]
    return pl.pallas_call(
        functools.partial(value_body, quad, far_size),
        in_specs=[VMEM] * (quad + far_size),
        out_specs=[VMEM] * quad,
        out_shape=[full((tokens, wide), f32)] * quad,
        compiler_params=params(8),
        name="value",
    )(*turned, *weights)


def join_body(count, *refs):
    parts, whole, tail = refs[:count], refs[count], refs[count + 1]
    total = parts[0][...]
    for part in parts[1:]:
        total = total + part[...]
    value = total.astype(bf16)
    whole[...] = value
    tail[...] = value[whole.shape[0] - tail.shape[0] :]


def join_call(parts):
    tokens, wide = parts[0].shape
    return pl.pallas_call(
        functools.partial(join_body, len(parts)),
        in_specs=[VMEM] * len(parts),
        out_specs=[VMEM] * 2,
        out_shape=[full((tokens, wide), bf16), full((LOOKBACK_SPAN, wide), bf16)],
        compiler_params=params(4),
        name="join",
    )(*parts)


def reduce_body(scale, own, *refs):
    others, total, square = refs[:-2], refs[-2], refs[-1]
    grad = own[...]
    for other in others:
        grad = grad + other[...].astype(f32)
    grad = grad * scale
    total[...] = grad
    lane = lax.broadcasted_iota(jnp.int32, square.shape, 1)
    square[...] = jnp.where(lane == lax.axis_index("work"), jnp.sum(grad * grad), 0.0)


def reduce_call(own, others, scale):
    return pl.pallas_call(
        functools.partial(reduce_body, scale),
        in_specs=[VMEM] * (1 + len(others)),
        out_specs=[VMEM] * 2,
        out_shape=[full(own.shape, f32), full((1, LANES), f32)],
        compiler_params=params(4),
        name="reduce",
    )(own, *others)


def pack_body(step, weight, first, second, out, fixes):
    for n, ref in enumerate((weight, first, second)):
        out[n] = ref[...].reshape(out.shape[1:])
    row = lax.broadcasted_iota(jnp.int32, fixes.shape, 0)
    base = jnp.where(row == 0, f32(beta_one), f32(beta_two))
    fixes[...] = 1.0 - jnp.power(base, step[0].astype(f32))


def pack_call(step, weight, first, second):
    rows, _, wide = weight.shape
    return pl.pallas_call(
        pack_body,
        in_specs=[SMEM] + [VMEM] * 3,
        out_specs=[VMEM] * 2,
        out_shape=[vmem((3, rows, wide), f32), vmem((8, wide), f32)],
        compiler_params=params(4),
        name="pack",
    )(step, *in_hbm(weight, first, second))


def tree_sum(values):
    while len(values) > 1:
        values = [a + b for a, b in zip(values[::2], values[1::2])]
    return values[0]


def adam_body(workers, fixes, squares, *refs):
    grads, states, outs = refs[:workers], refs[workers : 2 * workers], refs[2 * workers :]
    fix_one, fix_two = fixes[0:1, :], fixes[1:2, :]
    slot = lax.axis_index("work")
    lane = lax.broadcasted_iota(jnp.int32, squares.shape, 1)
    results = []
    for w in range(workers):
        square = jnp.sum(
            jnp.where(lane == (slot ^ w), squares[...], 0.0), axis=1, keepdims=True
        )
        factor = jnp.minimum(1.0, clip_norm / (jnp.sqrt(square) + 1e-06))
        grad = grads[w][...] * factor
        weight, first, second = states[w][0], states[w][1], states[w][2]
        first = beta_one * first + (1.0 - beta_one) * grad
        second = beta_two * second + (1.0 - beta_two) * grad * grad
        weight = weight - learn_rate * (first / fix_one) / (
            jnp.sqrt(second / fix_two) + adam_eps
        )
        results.append((weight, first, second))
    for out, values in zip(outs, zip(*results)):
        out[...] = tree_sum(list(values)) / workers


def adam_call(fixes, squares, grads, states):
    workers = len(states)
    shape = grads[0].shape
    return pl.pallas_call(
        functools.partial(adam_body, workers),
        in_specs=[VMEM] * (2 + 2 * workers),
        out_specs=[VMEM] * 3,
        out_shape=[full(shape, f32)] * 3,
        compiler_params=params(8),
        name="adam",
    )(*in_vmem(fixes, squares, *grads, *states))


def per_device(
    inputs, queries, keys, out_grad, positions, bands, step, value_weight, moment_one, moment_two
):
    tokens = inputs.shape[1]
    block = LOOKBACK_SPAN
    devices = lax.axis_size("ctx")
    workers = lax.axis_size("work")
    quad = min(4, devices)
    far_size = devices // quad
    weight, first, second = (
        jnp.transpose(a, (1, 0, 2)) for a in (value_weight, moment_one, moment_two)
    )

    blocks = tokens // block
    prev_keys = shifted(keys[0], "ctx", 1)
    turned, narrow = cut_call(inputs[0].T, weight, devices, quad)
    keyed, query, cotan, pos = load_call(
        keys[0], queries[0], out_grad[0], positions.reshape(blocks, 1, block)
    )
    turned = [turned[0]] + [swapped(turned[m], "ctx", m) for m in range(1, quad)]
    column = [narrow] + [swapped(narrow, "ctx", k * quad) for k in range(1, far_size)]

    probs_prev, send, head = probs_call(bands, pos, query, cotan, prev_keys, keyed, 0, 1)
    returned = shifted(send, "ctx", -1)
    probs_own, rest = probs_call(bands, pos, query, cotan, keyed, keyed, 1, blocks - 1)
    last = tokens - block
    value_grad = jnp.concatenate(
        [head + rest[:block], rest[block:last], rest[last:] + returned], 0
    ).astype(bf16)
    value_grads = [value_grad] + [swapped(value_grad, "ctx", m) for m in range(1, quad)]

    pieces = value_call(turned, column)
    parts = outer_call(turned, value_grads, weight.shape[0])
    others = [swapped(parts[k], "ctx", k * quad) for k in range(1, far_size)]

    pieces = [pieces[0]] + [swapped(pieces[m], "ctx", m) for m in range(1, quad)]
    values, tail = join_call(pieces)
    prev_values = shifted(tail, "ctx", 1)
    out = mix_call(probs_own, values, values, 1, blocks - 1, None)
    out = mix_call(probs_prev, prev_values, values, 0, 1, out)

    state, fixes = pack_call(step, weight, first, second)
    states = [state] + [swapped(state, "work", w) for w in range(1, workers)]
    grad, squares = reduce_call(parts[0], others, 1.0 / (tokens * devices))
    grads = [grad] + [swapped(grad, "work", w) for w in range(1, workers)]
    for axis, size in (("work", workers), ("ctx", devices)):
        bit = size // 2
        while bit:
            squares = squares + swapped(squares, axis, bit)
            bit //= 2
    mean_weight, mean_one, mean_two = adam_call(fixes, squares, grads, states)
    return (out[None], mean_weight, mean_one, mean_two)


def solution(mesh):
    in_specs = (
        P("work", "ctx", None),
        P("work", "ctx", None),
        P("work", "ctx", None),
        P("work", "ctx", None),
        P("work", "ctx"),
        P(),
        P(),
        P("work", "ctx", None),
        P("work", "ctx", None),
        P("work", "ctx", None),
    )
    out_specs = (P("work", "ctx", None), P("ctx", None), P("ctx", None), P("ctx", None))
    return jax.shard_map(
        per_device, mesh=mesh, in_specs=in_specs, out_specs=out_specs, check_vma=False
    )
```

time: 96.8 us -> 90 us (0.930)
  Pallas kernels: 21 us -> 17.9 us
  waiting for transfers between devices: 29.3 us -> 26.3 us
    pallas_call x5 -> x7, Pallas kernels: 16.9 us -> 14.3 us  [the longest x2 7.01 us: probs_call(): pl.pallas_call(functools.partial(probs_body, first, 0 if first else lower...]
    ppermute x3, waiting for transfers between devices: 3.05 us -> 1.39 us  [shifted(): return lax.ppermute(array, axis, pairs)]
    ppermute x22, waiting for transfers between devices: 26.2 us -> 24.9 us  [swapped(): return lax.ppermute(array, axis, pairs)]
  transfers between devices with their start and end apart: 25 -> 25, of which waited for: 11 -> 11; matrix products, arithmetic and copies ran while one was open for 0% -> 0% of each run, Pallas kernels for 10% -> 14%
where the time goes in v3:
time: 90 us; the launch traced here: 89.7 us
  starting transfers between devices  44 us (49%)
  waiting for transfers between devices  26.3 us (29%)
  Pallas kernels  17.9 us (20%)
  between operations  1.45 us (2%)
    ppermute x22, starting transfers between devices, swapped(): return lax.ppermute(array, axis, pairs)  35.1 us
    ppermute x22, waiting for transfers between devices, swapped(): return lax.ppermute(array, axis, pairs)  24.9 us
    ppermute x3, starting transfers between devices, shifted(): return lax.ppermute(array, axis, pairs)  8.91 us
    pallas_call x2, Pallas kernels, probs_call(): pl.pallas_call(functools.partial(probs_body, first, 0 if first else lower...  7.01 us
    pallas_call x2, Pallas kernels, mix_call(): pl.pallas_call(functools.partial(mix_body, first), grid=(count, KH // 2),...  3.09 us
    pallas_call x1, Pallas kernels, cut_call(): pl.pallas_call(functools.partial(cut_body, quad), in_specs=[pl.BlockSpec(...  1.81 us
  transfers between devices with their start and end apart: 25, of which 11 were waited for; matrix products, arithmetic and copies ran while one was open for 0% of the time, Pallas kernels for 14%

profile of v3, /device:TPU:0, one launch (start us, length us, event | category | flops | bytes accessed | tf_op | source)
XLA Modules:
  0.0 89.7 jit_solution(7830411656324154975)
XLA Ops:
  0.6 4.9 %collective-permute-start = (bf16[256,256]{1,0:T(8,128)(2,1)}, bf16[256,256]{1,0:T(8,128)(2,1)S(1)}, u32[]{:S(2)}, u32[]{:S(2)}) collective-permute-start(bf16[256,256]{1,0:T(8,128)(2,1)} %bitcast.19), channel_id=1, source_target_pairs={{0,2},{2,4},{4,6},{6,8},{8,10},{10,12},{12,14},{14,16},{16,18},{18... | collective-permute-start | bytes 393224 | tf_op jit(solution)/shard_map/ppermute | solution.py:36
  5.5 1.7 %load.1 = (bf16[256,256]{1,0:T(8,128)(2,1)S(1)}, bf16[256,2048]{1,0:T(8,128)(2,1)S(1)}, bf16[256,2048]{1,0:T(8,128)(2,1)S(1)}, s32[2,1,128]{2,1,0:T(1,128)S(1)}) custom-call(bf16[256,256]{1,0:T(8,128)(2,1)} %bitcast.20, bf16[256,2048]{1,0:T(8,128)(2,1)} %bitcast.13, bf16[256,2048]{1,0:T(8,128)(2,1)} %bitcast.14, s32[2,1,128]{2,1,0:T(1,128)} %bitcast.21), custom_call_target="tpu_custom_call" | custom-call | tf_op jit(solution)/shard_map/load/pallas_call | solution.py:282
  7.2 1.4 %collective-permute-done.prev = bf16[256,256]{1,0:T(8,128)(2,1)S(1)} collective-permute-done((bf16[256,256]{1,0:T(8,128)(2,1)}, bf16[256,256]{1,0:T(8,128)(2,1)S(1)}, u32[]{:S(2)}, u32[]{:S(2)}) %collective-permute-start) | collective-permute-done | bytes 131104 | tf_op jit(solution)/shard_map/ppermute | solution.py:36
  8.6 3.5 %shard_map.129 = (bf16[1,32,256,128]{3,2,1,0:T(8,128)(2,1)S(1)}, f32[128,256]{1,0:T(8,128)S(1)}, f32[128,256]{1,0:T(8,128)S(1)}) custom-call(s32[32]{0:T(128)S(1)} %copy-done, s32[2,1,128]{2,1,0:T(1,128)S(1)} %get-tuple-element.35.pos, bf16[256,2048]{1,0:T(8,128)(2,1)S(1)} %get-tuple-element.36.query, bf16[256,2048]{1,0:T(8,128)(2,1)S(1)} %get-tuple-element.37.cotan, ...), custom_call_target="tpu_custom_call" | custom-call | tf_op jit(solution)/shard_map/pallas_call | solution.py:159
  12.1 1.3 %collective-permute-start.11 = (f32[128,256]{1,0:T(8,128)S(1)}, f32[128,256]{1,0:T(8,128)S(1)}, u32[]{:S(2)}, u32[]{:S(2)}) collective-permute-start(f32[128,256]{1,0:T(8,128)S(1)} %get-tuple-element.55), channel_id=1, source_target_pairs={{2,0},{4,2},{6,4},{8,6},{10,8},{12,10},{14,12},{16,14},{18,16},{20... | collective-permute-start | bytes 393224 | tf_op jit(solution)/shard_map/ppermute | solution.py:36
  13.4 1.8 %cut.1 = (bf16[4,184,256]{2,1,0:T(8,128)(2,1)S(1)}, bf16[4,184,256]{2,1,0:T(8,128)(2,1)S(1)}, bf16[4,184,256]{2,1,0:T(8,128)(2,1)S(1)}, bf16[4,184,256]{2,1,0:T(8,128)(2,1)S(1)}, bf16[184,256]{1,0:T(8,128)(2,1)S(1)}) custom-call(bf16[2880,256]{1,0:T(8,128)(2,1)} %bitcast.12, f32[180,1,256]{2,1,0:T(1,128)} %bitcast.15), custom_call_target="tpu_custom_call" | custom-call | tf_op jit(solution)/shard_map/cut/pallas_call | solution.py:252
  15.2 3.1 %collective-permute-start.1 = (bf16[4,184,256]{2,1,0:T(8,128)(2,1)S(1)}, bf16[4,184,256]{2,1,0:T(8,128)(2,1)S(1)}, u32[]{:S(2)}, u32[]{:S(2)}) collective-permute-start(bf16[4,184,256]{2,1,0:T(8,128)(2,1)S(1)} %get-tuple-element.41), channel_id=1, source_target_pairs={{0,2},{2,0},{4,6},{6,4},{8,10},{10,8},{12,14},{14,12},{16,18},{18,... | collective-permute-start | bytes 1130504 | tf_op jit(solution)/shard_map/ppermute | solution.py:30
  18.3 2.9 %collective-permute-start.2 = (bf16[4,184,256]{2,1,0:T(8,128)(2,1)S(1)}, bf16[4,184,256]{2,1,0:T(8,128)(2,1)S(1)}, u32[]{:S(2)}, u32[]{:S(2)}) collective-permute-start(bf16[4,184,256]{2,1,0:T(8,128)(2,1)S(1)} %get-tuple-element.42), channel_id=1, source_target_pairs={{0,4},{2,6},{4,0},{6,2},{8,12},{10,14},{12,8},{14,10},{16,20},{18,... | collective-permute-start | bytes 1130504 | tf_op jit(solution)/shard_map/ppermute | solution.py:30
  21.2 3.5 %shard_map.130 = (bf16[1,32,256,128]{3,2,1,0:T(8,128)(2,1)S(1)}, f32[256,256]{1,0:T(8,128)S(1)}) custom-call(s32[32]{0:T(128)S(1)} %copy-done, s32[2,1,128]{2,1,0:T(1,128)S(1)} %get-tuple-element.35.pos, bf16[256,2048]{1,0:T(8,128)(2,1)S(1)} %get-tuple-element.36.query, bf16[256,2048]{1,0:T(8,128)(2,1)S(1)} %get-tuple-element.37.cotan, ...), custom_call_target="tpu_custom_call" | custom-call | tf_op jit(solution)/shard_map/pallas_call | solution.py:159
  24.8 1.5 %collective-permute-start.12 = (bf16[256,256]{1,0:T(8,128)(2,1)S(1)}, bf16[256,256]{1,0:T(8,128)(2,1)S(1)}, u32[]{:S(2)}, u32[]{:S(2)}) collective-permute-start(bf16[256,256]{1,0:T(8,128)(2,1)S(1)} %pad_maximum_fusion.refs_4_), channel_id=1, source_target_pairs={{0,2},{2,0},{4,6},{6,4},{8,10},{10,8},{12,14},{14,12},{16,18},{18,... | collective-permute-start | bytes 393224 | tf_op jit(solution)/shard_map/ppermute | solution.py:30
  26.3 2.0 %collective-permute-start.13 = (bf16[256,256]{1,0:T(8,128)(2,1)S(1)}, bf16[256,256]{1,0:T(8,128)(2,1)S(1)}, u32[]{:S(2)}, u32[]{:S(2)}) collective-permute-start(bf16[256,256]{1,0:T(8,128)(2,1)S(1)} %pad_maximum_fusion.refs_4_), channel_id=1, source_target_pairs={{0,4},{2,6},{4,0},{6,2},{8,12},{10,14},{12,8},{14,10},{16,20},{18,... | collective-permute-start | bytes 393224 | tf_op jit(solution)/shard_map/ppermute | solution.py:30
  29.0 1.3 %pack.1 = (f32[3,180,256]{2,1,0:T(8,128)S(1)}, f32[8,256]{1,0:T(8,128)S(1)}) custom-call(s32[1]{0:T(128)S(6)} %copy.16.step, f32[180,1,256]{2,1,0:T(1,128)} %bitcast.16, f32[180,1,256]{2,1,0:T(1,128)} %bitcast.17, f32[180,1,256]{2,1,0:T(1,128)} %bitcast.18), custom_call_target="tpu_custom_call" | custom-call | tf_op jit(solution)/shard_map/pack/pallas_call | solution.py:414
  30.3 0.0 collective-permute-done.1.refs_1_
  30.3 0.1 collective-permute-start.24
  30.4 8.0 %collective-permute-done.2.refs_2_ = bf16[4,184,256]{2,1,0:T(8,128)(2,1)S(1)} collective-permute-done((bf16[4,184,256]{2,1,0:T(8,128)(2,1)S(1)}, bf16[4,184,256]{2,1,0:T(8,128)(2,1)S(1)}, u32[]{:S(2)}, u32[]{:S(2)}) %collective-permute-start.2) | collective-permute-done | bytes 376864 | tf_op jit(solution)/shard_map/ppermute | solution.py:30
  38.4 2.5 %collective-permute-start.14 = (bf16[256,256]{1,0:T(8,128)(2,1)S(1)}, bf16[256,256]{1,0:T(8,128)(2,1)S(1)}, u32[]{:S(2)}, u32[]{:S(2)}) collective-permute-start(bf16[256,256]{1,0:T(8,128)(2,1)S(1)} %pad_maximum_fusion.refs_4_), channel_id=1, source_target_pairs={{0,6},{2,4},{4,2},{6,0},{8,14},{10,12},{12,10},{14,8},{16,22},{18,... | collective-permute-start | bytes 393224 | tf_op jit(solution)/shard_map/ppermute | solution.py:30
  40.9 1.2 %collective-permute-start.4 = (bf16[184,256]{1,0:T(8,128)(2,1)S(1)}, bf16[184,256]{1,0:T(8,128)(2,1)S(1)}, u32[]{:S(2)}, u32[]{:S(2)}) collective-permute-start(bf16[184,256]{1,0:T(8,128)(2,1)S(1)} %get-tuple-element.44.refs_4_), channel_id=1, source_target_pairs={{0,8},{2,10},{4,12},{6,14},{8,0},{10,2},{12,4},{14,6},{16,24},{18,... | collective-permute-start | bytes 282632 | tf_op jit(solution)/shard_map/ppermute | solution.py:30
  42.1 2.4 %collective-permute-start.5 = (bf16[184,256]{1,0:T(8,128)(2,1)S(1)}, bf16[184,256]{1,0:T(8,128)(2,1)S(1)}, u32[]{:S(2)}, u32[]{:S(2)}) collective-permute-start(bf16[184,256]{1,0:T(8,128)(2,1)S(1)} %get-tuple-element.44.refs_4_), channel_id=1, source_target_pairs={{0,16},{2,18},{4,20},{6,22},{8,24},{10,26},{12,28},{14,30},{16,0},... | collective-permute-start | bytes 282632 | tf_op jit(solution)/shard_map/ppermute | solution.py:30
  44.5 1.3 %collective-permute-start.6 = (bf16[184,256]{1,0:T(8,128)(2,1)S(1)}, bf16[184,256]{1,0:T(8,128)(2,1)S(1)}, u32[]{:S(2)}, u32[]{:S(2)}) collective-permute-start(bf16[184,256]{1,0:T(8,128)(2,1)S(1)} %get-tuple-element.44.refs_4_), channel_id=1, source_target_pairs={{0,24},{2,26},{4,28},{6,30},{8,16},{10,18},{12,20},{14,22},{16,8},... | collective-permute-start | bytes 282632 | tf_op jit(solution)/shard_map/ppermute | solution.py:30
  45.8 0.7 outer.1
  46.5 0.8 collective-permute-start.15
  47.4 2.6 %collective-permute-start.16 = (bf16[180,256]{1,0:T(8,128)(2,1)S(1)}, bf16[180,256]{1,0:T(8,128)(2,1)S(1)}, u32[]{:S(2)}, u32[]{:S(2)}) collective-permute-start(bf16[180,256]{1,0:T(8,128)(2,1)S(1)} %get-tuple-element.58), channel_id=1, source_target_pairs={{0,16},{2,18},{4,20},{6,22},{8,24},{10,26},{12,28},{14,30},{16,0},... | collective-permute-start | bytes 276488 | tf_op jit(solution)/shard_map/ppermute | solution.py:30
  49.9 0.1 collective-permute-done.5.refs_6_
  50.1 2.0 %collective-permute-done.6.refs_7_ = bf16[184,256]{1,0:T(8,128)(2,1)S(1)} collective-permute-done((bf16[184,256]{1,0:T(8,128)(2,1)S(1)}, bf16[184,256]{1,0:T(8,128)(2,1)S(1)}, u32[]{:S(2)}, u32[]{:S(2)}) %collective-permute-start.6) | collective-permute-done | bytes 94240 | tf_op jit(solution)/shard_map/ppermute | solution.py:30
  52.1 0.8 value.1
  52.9 1.5 %collective-permute-start.7 = (f32[256,256]{1,0:T(8,128)S(1)}, f32[256,256]{1,0:T(8,128)S(1)}, u32[]{:S(2)}, u32[]{:S(2)}) collective-permute-start(f32[256,256]{1,0:T(8,128)S(1)} %get-tuple-element.46), channel_id=1, source_target_pairs={{0,2},{2,0},{4,6},{6,4},{8,10},{10,8},{12,14},{14,12},{16,18},{18,... | collective-permute-start | bytes 786440 | tf_op jit(solution)/shard_map/ppermute | solution.py:30
  54.3 0.0 collective-permute-start.8
  54.4 2.0 %collective-permute-start.9 = (f32[256,256]{1,0:T(8,128)S(1)}, f32[256,256]{1,0:T(8,128)S(1)}, u32[]{:S(2)}, u32[]{:S(2)}) collective-permute-start(f32[256,256]{1,0:T(8,128)S(1)} %get-tuple-element.48), channel_id=1, source_target_pairs={{0,6},{2,4},{4,2},{6,0},{8,14},{10,12},{12,10},{14,8},{16,22},{18,... | collective-permute-start | bytes 786440 | tf_op jit(solution)/shard_map/ppermute | solution.py:30
  56.4 2.8 %collective-permute-start.17 = (bf16[180,256]{1,0:T(8,128)(2,1)S(1)}, bf16[180,256]{1,0:T(8,128)(2,1)S(1)}, u32[]{:S(2)}, u32[]{:S(2)}) collective-permute-start(bf16[180,256]{1,0:T(8,128)(2,1)S(1)} %get-tuple-element.59), channel_id=1, source_target_pairs={{0,24},{2,26},{4,28},{6,30},{8,16},{10,18},{12,20},{14,22},{16,8},... | collective-permute-start | bytes 276488 | tf_op jit(solution)/shard_map/ppermute | solution.py:30
  59.3 3.6 %collective-permute-done.17.refs_2_ = bf16[180,256]{1,0:T(8,128)(2,1)S(1)} collective-permute-done((bf16[180,256]{1,0:T(8,128)(2,1)S(1)}, bf16[180,256]{1,0:T(8,128)(2,1)S(1)}, u32[]{:S(2)}, u32[]{:S(2)}) %collective-permute-start.17) | collective-permute-done | bytes 92192 | tf_op jit(solution)/shard_map/ppermute | solution.py:30
  62.8 0.2 reduce.1
  63.1 0.1 collective-permute-start.23
  63.2 0.6 collective-permute-done.8.refs_2_
  63.8 0.1 join.1
  63.8 2.7 %collective-permute-start.10 = (bf16[128,256]{1,0:T(8,128)(2,1)S(1)}, bf16[128,256]{1,0:T(8,128)(2,1)S(1)}, u32[]{:S(2)}, u32[]{:S(2)}) collective-permute-start(bf16[128,256]{1,0:T(8,128)(2,1)S(1)} %get-tuple-element.49), channel_id=1, source_target_pairs={{0,2},{2,4},{4,6},{6,8},{8,10},{10,12},{12,14},{14,16},{16,18},{18... | collective-permute-start | bytes 196616 | tf_op jit(solution)/shard_map/ppermute | solution.py:36
  66.6 0.3 collective-permute-start.18
  66.8 1.0 %collective-permute-done.18 = f32[1,128]{1,0:T(1,128)S(1)} collective-permute-done((f32[1,128]{1,0:T(1,128)S(1)}, f32[1,128]{1,0:T(1,128)S(1)}, u32[]{:S(2)}, u32[]{:S(2)}) %collective-permute-start.18) | collective-permute-done | bytes 544 | tf_op jit(solution)/shard_map/ppermute | solution.py:30
  67.8 5.3 %collective-permute-start.19 = (f32[1,128]{1,0:T(1,128)S(1)}, f32[1,128]{1,0:T(1,128)S(1)}, u32[]{:S(2)}, u32[]{:S(2)}) collective-permute-start(f32[1,128]{1,0:T(1,128)S(1)} %add.23), channel_id=1, source_target_pairs={{0,16},{2,18},{4,20},{6,22},{8,24},{10,26},{12,28},{14,30},{16,0},... | collective-permute-start | bytes 1544 | tf_op jit(solution)/shard_map/ppermute | solution.py:30
  73.1 1.5 %collective-permute-done.19 = f32[1,128]{1,0:T(1,128)S(1)} collective-permute-done((f32[1,128]{1,0:T(1,128)S(1)}, f32[1,128]{1,0:T(1,128)S(1)}, u32[]{:S(2)}, u32[]{:S(2)}) %collective-permute-start.19) | collective-permute-done | bytes 544 | tf_op jit(solution)/shard_map/ppermute | solution.py:30
  74.6 0.9 collective-permute-start.20
  75.5 2.7 %collective-permute-done.20 = f32[1,128]{1,0:T(1,128)S(1)} collective-permute-done((f32[1,128]{1,0:T(1,128)S(1)}, f32[1,128]{1,0:T(1,128)S(1)}, u32[]{:S(2)}, u32[]{:S(2)}) %collective-permute-start.20) | collective-permute-done | bytes 544 | tf_op jit(solution)/shard_map/ppermute | solution.py:30
  78.2 0.6 collective-permute-start.21
  78.8 3.0 %collective-permute-done.21 = f32[1,128]{1,0:T(1,128)S(1)} collective-permute-done((f32[1,128]{1,0:T(1,128)S(1)}, f32[1,128]{1,0:T(1,128)S(1)}, u32[]{:S(2)}, u32[]{:S(2)}) %collective-permute-start.21) | collective-permute-done | bytes 544 | tf_op jit(solution)/shard_map/ppermute | solution.py:30
  81.8 1.2 %collective-permute-start.22 = (f32[1,128]{1,0:T(1,128)S(1)}, f32[1,128]{1,0:T(1,128)S(1)}, u32[]{:S(2)}, u32[]{:S(2)}) collective-permute-start(f32[1,128]{1,0:T(1,128)S(1)} %add.26), channel_id=1, source_target_pairs={{0,2},{2,0},{4,6},{6,4},{8,10},{10,8},{12,14},{14,12},{16,18},{18,... | collective-permute-start | bytes 1544 | tf_op jit(solution)/shard_map/ppermute | solution.py:30
  82.9 2.4 %collective-permute-done.22 = f32[1,128]{1,0:T(1,128)S(1)} collective-permute-done((f32[1,128]{1,0:T(1,128)S(1)}, f32[1,128]{1,0:T(1,128)S(1)}, u32[]{:S(2)}, u32[]{:S(2)}) %collective-permute-start.22) | collective-permute-done | bytes 544 | tf_op jit(solution)/shard_map/ppermute | solution.py:30
  85.3 1.5 %shard_map.131.refs_0_ = bf16[256,2048]{1,0:T(8,128)(2,1)} custom-call(bf16[1,32,256,128]{3,2,1,0:T(8,128)(2,1)S(1)} %get-tuple-element.51.probs, bf16[256,256]{1,0:T(8,128)(2,1)S(1)} %get-tuple-element.50.lower.values, bf16[256,256]{1,0:T(8,128)(2,1)S(1)} %get-tuple-element.50.lower.values), custom_call_target="tpu_custom_call" | custom-call | tf_op jit(solution)/shard_map/pallas_call | solution.py:201
  86.9 1.3 %adam.1 = (f32[180,256]{1,0:T(8,128)}, f32[180,256]{1,0:T(8,128)}, f32[180,256]{1,0:T(8,128)}) custom-call(f32[8,256]{1,0:T(8,128)S(1)} %get-tuple-element.52.fixes, f32[1,128]{1,0:T(1,128)S(1)} %add.27.squares, f32[180,256]{1,0:T(8,128)S(1)} %get-tuple-element.61.refs_0_, f32[180,256]{1,0:T(8,128)S(1)} %collective-permute-done.23.refs_1_, ...), custom_call_target="tpu_custom_call" | custom-call | tf_op jit(solution)/shard_map/adam/pallas_call | solution.py:456
  88.2 1.5 %shard_map.132 = bf16[256,2048]{1,0:T(8,128)(2,1)} custom-call(bf16[1,32,256,128]{3,2,1,0:T(8,128)(2,1)S(1)} %get-tuple-element.39.probs, bf16[128,256]{1,0:T(8,128)(2,1)S(1)} %collective-permute-done.10.lower, bf16[256,256]{1,0:T(8,128)(2,1)S(1)} %get-tuple-element.50.lower.values, bf16[256,2048]{1,0:T(8,128)(2,1)} %shard_map.131.refs_0_), custom_call_target="tpu_custom_call", output_to_operand_aliasing={{}: (3, {})} | custom-call | tf_op jit(solution)/shard_map/pallas_call | solution.py:201
  (23 shorter events, 0.1 us)
Async XLA Ops:
  0.6 7.9 %copy-start = (s32[32]{0:T(128)S(1)}, s32[32]{0:T(128)}, u32[]{:S(2)}) copy-start(s32[32]{0:T(128)} %bands.3) | copy-start | bytes 388
  0.6 7.9 %collective-permute-start = (bf16[256,256]{1,0:T(8,128)(2,1)}, bf16[256,256]{1,0:T(8,128)(2,1)S(1)}, u32[]{:S(2)}, u32[]{:S(2)}) collective-permute-start(bf16[256,256]{1,0:T(8,128)(2,1)} %bitcast.19), channel_id=1, source_target_pairs={{0,2},{2,4},{4,6},{6,8},{8,10},{10,12},{12,14},{14,16},{16,18},{18... | collective-permute-start | bytes 393224 | tf_op jit(solution)/shard_map/ppermute | solution.py:36
  12.1 12.6 %collective-permute-start.11 = (f32[128,256]{1,0:T(8,128)S(1)}, f32[128,256]{1,0:T(8,128)S(1)}, u32[]{:S(2)}, u32[]{:S(2)}) collective-permute-start(f32[128,256]{1,0:T(8,128)S(1)} %get-tuple-element.55), channel_id=1, source_target_pairs={{2,0},{4,2},{6,4},{8,6},{10,8},{12,10},{14,12},{16,14},{18,16},{20... | collective-permute-start | bytes 393224 | tf_op jit(solution)/shard_map/ppermute | solution.py:36
  15.2 15.1 %collective-permute-start.1 = (bf16[4,184,256]{2,1,0:T(8,128)(2,1)S(1)}, bf16[4,184,256]{2,1,0:T(8,128)(2,1)S(1)}, u32[]{:S(2)}, u32[]{:S(2)}) collective-permute-start(bf16[4,184,256]{2,1,0:T(8,128)(2,1)S(1)} %get-tuple-element.41), channel_id=1, source_target_pairs={{0,2},{2,0},{4,6},{6,4},{8,10},{10,8},{12,14},{14,12},{16,18},{18,... | collective-permute-start | bytes 1130504 | tf_op jit(solution)/shard_map/ppermute | solution.py:30
  18.3 20.1 %collective-permute-start.2 = (bf16[4,184,256]{2,1,0:T(8,128)(2,1)S(1)}, bf16[4,184,256]{2,1,0:T(8,128)(2,1)S(1)}, u32[]{:S(2)}, u32[]{:S(2)}) collective-permute-start(bf16[4,184,256]{2,1,0:T(8,128)(2,1)S(1)} %get-tuple-element.42), channel_id=1, source_target_pairs={{0,4},{2,6},{4,0},{6,2},{8,12},{10,14},{12,8},{14,10},{16,20},{18,... | collective-permute-start | bytes 1130504 | tf_op jit(solution)/shard_map/ppermute | solution.py:30
  21.2 19.7 %collective-permute-start.3 = (bf16[4,184,256]{2,1,0:T(8,128)(2,1)S(1)}, bf16[4,184,256]{2,1,0:T(8,128)(2,1)S(1)}, u32[]{:S(2)}, u32[]{:S(2)}) collective-permute-start(bf16[4,184,256]{2,1,0:T(8,128)(2,1)S(1)} %get-tuple-element.43), channel_id=1, source_target_pairs={{0,6},{2,4},{4,2},{6,0},{8,14},{10,12},{12,10},{14,8},{16,22},{18,... | collective-permute-start | bytes 1130504 | tf_op jit(solution)/shard_map/ppermute | solution.py:30
  24.8 17.3 %collective-permute-start.12 = (bf16[256,256]{1,0:T(8,128)(2,1)S(1)}, bf16[256,256]{1,0:T(8,128)(2,1)S(1)}, u32[]{:S(2)}, u32[]{:S(2)}) collective-permute-start(bf16[256,256]{1,0:T(8,128)(2,1)S(1)} %pad_maximum_fusion.refs_4_), channel_id=1, source_target_pairs={{0,2},{2,0},{4,6},{6,4},{8,10},{10,8},{12,14},{14,12},{16,18},{18,... | collective-permute-start | bytes 393224 | tf_op jit(solution)/shard_map/ppermute | solution.py:30
  26.3 18.1 %collective-permute-start.13 = (bf16[256,256]{1,0:T(8,128)(2,1)S(1)}, bf16[256,256]{1,0:T(8,128)(2,1)S(1)}, u32[]{:S(2)}, u32[]{:S(2)}) collective-permute-start(bf16[256,256]{1,0:T(8,128)(2,1)S(1)} %pad_maximum_fusion.refs_4_), channel_id=1, source_target_pairs={{0,4},{2,6},{4,0},{6,2},{8,12},{10,14},{12,8},{14,10},{16,20},{18,... | collective-permute-start | bytes 393224 | tf_op jit(solution)/shard_map/ppermute | solution.py:30
  30.3 56.6 %collective-permute-start.24 = (f32[3,180,256]{2,1,0:T(8,128)S(1)}, f32[3,180,256]{2,1,0:T(8,128)S(1)}, u32[]{:S(2)}, u32[]{:S(2)}) collective-permute-start(f32[3,180,256]{2,1,0:T(8,128)S(1)} %get-tuple-element.62.refs_2_), channel_id=1, source_target_pairs={{0,1},{1,0},{2,3},{3,2},{4,5},{5,4},{6,7},{7,6},{8,9},{9,8},{10,11... | collective-permute-start | bytes 1658888 | tf_op jit(solution)/shard_map/ppermute | solution.py:30
  38.4 7.5 %collective-permute-start.14 = (bf16[256,256]{1,0:T(8,128)(2,1)S(1)}, bf16[256,256]{1,0:T(8,128)(2,1)S(1)}, u32[]{:S(2)}, u32[]{:S(2)}) collective-permute-start(bf16[256,256]{1,0:T(8,128)(2,1)S(1)} %pad_maximum_fusion.refs_4_), channel_id=1, source_target_pairs={{0,6},{2,4},{4,2},{6,0},{8,14},{10,12},{12,10},{14,8},{16,22},{18,... | collective-permute-start | bytes 393224 | tf_op jit(solution)/shard_map/ppermute | solution.py:30
  40.9 6.5 %collective-permute-start.4 = (bf16[184,256]{1,0:T(8,128)(2,1)S(1)}, bf16[184,256]{1,0:T(8,128)(2,1)S(1)}, u32[]{:S(2)}, u32[]{:S(2)}) collective-permute-start(bf16[184,256]{1,0:T(8,128)(2,1)S(1)} %get-tuple-element.44.refs_4_), channel_id=1, source_target_pairs={{0,8},{2,10},{4,12},{6,14},{8,0},{10,2},{12,4},{14,6},{16,24},{18,... | collective-permute-start | bytes 282632 | tf_op jit(solution)/shard_map/ppermute | solution.py:30
  42.1 8.0 %collective-permute-start.5 = (bf16[184,256]{1,0:T(8,128)(2,1)S(1)}, bf16[184,256]{1,0:T(8,128)(2,1)S(1)}, u32[]{:S(2)}, u32[]{:S(2)}) collective-permute-start(bf16[184,256]{1,0:T(8,128)(2,1)S(1)} %get-tuple-element.44.refs_4_), channel_id=1, source_target_pairs={{0,16},{2,18},{4,20},{6,22},{8,24},{10,26},{12,28},{14,30},{16,0},... | collective-permute-start | bytes 282632 | tf_op jit(solution)/shard_map/ppermute | solution.py:30
  44.5 7.6 %collective-permute-start.6 = (bf16[184,256]{1,0:T(8,128)(2,1)S(1)}, bf16[184,256]{1,0:T(8,128)(2,1)S(1)}, u32[]{:S(2)}, u32[]{:S(2)}) collective-permute-start(bf16[184,256]{1,0:T(8,128)(2,1)S(1)} %get-tuple-element.44.refs_4_), channel_id=1, source_target_pairs={{0,24},{2,26},{4,28},{6,30},{8,16},{10,18},{12,20},{14,22},{16,8},... | collective-permute-start | bytes 282632 | tf_op jit(solution)/shard_map/ppermute | solution.py:30
  46.5 7.9 %collective-permute-start.15 = (bf16[180,256]{1,0:T(8,128)(2,1)S(1)}, bf16[180,256]{1,0:T(8,128)(2,1)S(1)}, u32[]{:S(2)}, u32[]{:S(2)}) collective-permute-start(bf16[180,256]{1,0:T(8,128)(2,1)S(1)} %get-tuple-element.57), channel_id=1, source_target_pairs={{0,8},{2,10},{4,12},{6,14},{8,0},{10,2},{12,4},{14,6},{16,24},{18,... | collective-permute-start | bytes 276488 | tf_op jit(solution)/shard_map/ppermute | solution.py:30
  47.4 9.1 %collective-permute-start.16 = (bf16[180,256]{1,0:T(8,128)(2,1)S(1)}, bf16[180,256]{1,0:T(8,128)(2,1)S(1)}, u32[]{:S(2)}, u32[]{:S(2)}) collective-permute-start(bf16[180,256]{1,0:T(8,128)(2,1)S(1)} %get-tuple-element.58), channel_id=1, source_target_pairs={{0,16},{2,18},{4,20},{6,22},{8,24},{10,26},{12,28},{14,30},{16,0},... | collective-permute-start | bytes 276488 | tf_op jit(solution)/shard_map/ppermute | solution.py:30
  52.9 10.3 %collective-permute-start.7 = (f32[256,256]{1,0:T(8,128)S(1)}, f32[256,256]{1,0:T(8,128)S(1)}, u32[]{:S(2)}, u32[]{:S(2)}) collective-permute-start(f32[256,256]{1,0:T(8,128)S(1)} %get-tuple-element.46), channel_id=1, source_target_pairs={{0,2},{2,0},{4,6},{6,4},{8,10},{10,8},{12,14},{14,12},{16,18},{18,... | collective-permute-start | bytes 786440 | tf_op jit(solution)/shard_map/ppermute | solution.py:30
  54.3 9.4 %collective-permute-start.8 = (f32[256,256]{1,0:T(8,128)S(1)}, f32[256,256]{1,0:T(8,128)S(1)}, u32[]{:S(2)}, u32[]{:S(2)}) collective-permute-start(f32[256,256]{1,0:T(8,128)S(1)} %get-tuple-element.47), channel_id=1, source_target_pairs={{0,4},{2,6},{4,0},{6,2},{8,12},{10,14},{12,8},{14,10},{16,20},{18,... | collective-permute-start | bytes 786440 | tf_op jit(solution)/shard_map/ppermute | solution.py:30
  54.4 9.4 %collective-permute-start.9 = (f32[256,256]{1,0:T(8,128)S(1)}, f32[256,256]{1,0:T(8,128)S(1)}, u32[]{:S(2)}, u32[]{:S(2)}) collective-permute-start(f32[256,256]{1,0:T(8,128)S(1)} %get-tuple-element.48), channel_id=1, source_target_pairs={{0,6},{2,4},{4,2},{6,0},{8,14},{10,12},{12,10},{14,8},{16,22},{18,... | collective-permute-start | bytes 786440 | tf_op jit(solution)/shard_map/ppermute | solution.py:30
  56.4 6.4 %collective-permute-start.17 = (bf16[180,256]{1,0:T(8,128)(2,1)S(1)}, bf16[180,256]{1,0:T(8,128)(2,1)S(1)}, u32[]{:S(2)}, u32[]{:S(2)}) collective-permute-start(bf16[180,256]{1,0:T(8,128)(2,1)S(1)} %get-tuple-element.59), channel_id=1, source_target_pairs={{0,24},{2,26},{4,28},{6,30},{8,16},{10,18},{12,20},{14,22},{16,8},... | collective-permute-start | bytes 276488 | tf_op jit(solution)/shard_map/ppermute | solution.py:30
  63.1 23.8 %collective-permute-start.23 = (f32[180,256]{1,0:T(8,128)S(1)}, f32[180,256]{1,0:T(8,128)S(1)}, u32[]{:S(2)}, u32[]{:S(2)}) collective-permute-start(f32[180,256]{1,0:T(8,128)S(1)} %get-tuple-element.61.refs_0_), channel_id=1, source_target_pairs={{0,1},{1,0},{2,3},{3,2},{4,5},{5,4},{6,7},{7,6},{8,9},{9,8},{10,11... | collective-permute-start | bytes 552968 | tf_op jit(solution)/shard_map/ppermute | solution.py:30
  63.8 24.3 %collective-permute-start.10 = (bf16[128,256]{1,0:T(8,128)(2,1)S(1)}, bf16[128,256]{1,0:T(8,128)(2,1)S(1)}, u32[]{:S(2)}, u32[]{:S(2)}) collective-permute-start(bf16[128,256]{1,0:T(8,128)(2,1)S(1)} %get-tuple-element.49), channel_id=1, source_target_pairs={{0,2},{2,4},{4,6},{6,8},{8,10},{10,12},{12,14},{14,16},{16,18},{18... | collective-permute-start | bytes 196616 | tf_op jit(solution)/shard_map/ppermute | solution.py:36
  66.6 1.2 %collective-permute-start.18 = (f32[1,128]{1,0:T(1,128)S(1)}, f32[1,128]{1,0:T(1,128)S(1)}, u32[]{:S(2)}, u32[]{:S(2)}) collective-permute-start(f32[1,128]{1,0:T(1,128)S(1)} %get-tuple-element.60), channel_id=1, source_target_pairs={{0,1},{1,0},{2,3},{3,2},{4,5},{5,4},{6,7},{7,6},{8,9},{9,8},{10,11... | collective-permute-start | bytes 1544 | tf_op jit(solution)/shard_map/ppermute | solution.py:30
  67.8 6.8 %collective-permute-start.19 = (f32[1,128]{1,0:T(1,128)S(1)}, f32[1,128]{1,0:T(1,128)S(1)}, u32[]{:S(2)}, u32[]{:S(2)}) collective-permute-start(f32[1,128]{1,0:T(1,128)S(1)} %add.23), channel_id=1, source_target_pairs={{0,16},{2,18},{4,20},{6,22},{8,24},{10,26},{12,28},{14,30},{16,0},... | collective-permute-start | bytes 1544 | tf_op jit(solution)/shard_map/ppermute | solution.py:30
  74.6 3.6 %collective-permute-start.20 = (f32[1,128]{1,0:T(1,128)S(1)}, f32[1,128]{1,0:T(1,128)S(1)}, u32[]{:S(2)}, u32[]{:S(2)}) collective-permute-start(f32[1,128]{1,0:T(1,128)S(1)} %add.24), channel_id=1, source_target_pairs={{0,8},{2,10},{4,12},{6,14},{8,0},{10,2},{12,4},{14,6},{16,24},{18,... | collective-permute-start | bytes 1544 | tf_op jit(solution)/shard_map/ppermute | solution.py:30
  78.2 3.6 %collective-permute-start.21 = (f32[1,128]{1,0:T(1,128)S(1)}, f32[1,128]{1,0:T(1,128)S(1)}, u32[]{:S(2)}, u32[]{:S(2)}) collective-permute-start(f32[1,128]{1,0:T(1,128)S(1)} %add.25), channel_id=1, source_target_pairs={{0,4},{2,6},{4,0},{6,2},{8,12},{10,14},{12,8},{14,10},{16,20},{18,... | collective-permute-start | bytes 1544 | tf_op jit(solution)/shard_map/ppermute | solution.py:30
  81.8 3.6 %collective-permute-start.22 = (f32[1,128]{1,0:T(1,128)S(1)}, f32[1,128]{1,0:T(1,128)S(1)}, u32[]{:S(2)}, u32[]{:S(2)}) collective-permute-start(f32[1,128]{1,0:T(1,128)S(1)} %add.26), channel_id=1, source_target_pairs={{0,2},{2,0},{4,6},{6,4},{8,10},{10,8},{12,14},{14,12},{16,18},{18,... | collective-permute-start | bytes 1544 | tf_op jit(solution)/shard_map/ppermute | solution.py:30

commit v4 on v3

--- a/solution.py
+++ b/solution.py
@@ -136,7 +136,7 @@
     )
     low, high = grad[:block], grad[block:]
     if first == 0:
-        grads_out[0][:, lanes] = low
+        grads_out[0][:, lanes] = low.astype(bf16)
         grads_out[1][:, lanes] = high
     else:
         rows, = grads_out
@@ -162,7 +162,7 @@
         in_specs=[SMEM] + [VMEM] * 5,
         out_specs=[VMEM] * (2 if first else 3),
         out_shape=[vmem((count, QH, 2 * block, block), bf16)]
-        + ([vmem((tokens, wide), f32)] if first else [vmem((block, wide), f32)] * 2),
+        + ([vmem((tokens, wide), f32)] if first else [vmem((block, wide), bf16), vmem((block, wide), f32)]),
         compiler_params=params(8),
     )(bands, *in_vmem(positions, queries, out_grad, lower, keys))
 
@@ -490,7 +490,7 @@
     probs_own, rest = probs_call(bands, pos, query, cotan, keyed, keyed, 1, blocks - 1)
     last = tokens - block
     value_grad = jnp.concatenate(
-        [head + rest[:block], rest[block:last], rest[last:] + returned], 0
+        [head + rest[:block], rest[block:last], rest[last:] + returned.astype(f32)], 0
     ).astype(bf16)
     value_grads = [value_grad] + [swapped(value_grad, "ctx", m) for m in range(1, quad)]
 

time: 90 us -> 94.8 us (1.053)
  starting transfers between devices: 44 us -> 48.2 us
    ppermute x22, starting transfers between devices: 35.1 us -> 39.3 us  [swapped(): return lax.ppermute(array, axis, pairs)]
  transfers between devices with their start and end apart: 25 -> 25, of which waited for: 11 -> 12; matrix products, arithmetic and copies ran while one was open for 0% -> 0% of each run, Pallas kernels for 14% -> 14%
where the time goes in v4:
time: 94.8 us; the launch traced here: 94.5 us
  starting transfers between devices  48.2 us (51%)
  waiting for transfers between devices  27 us (28%)
  Pallas kernels  17.9 us (19%)
  between operations  1.46 us (2%)
    ppermute x22, starting transfers between devices, swapped(): return lax.ppermute(array, axis, pairs)  39.3 us
    ppermute x22, waiting for transfers between devices, swapped(): return lax.ppermute(array, axis, pairs)  25.6 us
    ppermute x3, starting transfers between devices, shifted(): return lax.ppermute(array, axis, pairs)  8.91 us
    pallas_call x2, Pallas kernels, probs_call(): pl.pallas_call(functools.partial(probs_body, first, 0 if first else lower...  7.01 us
    pallas_call x2, Pallas kernels, mix_call(): pl.pallas_call(functools.partial(mix_body, first), grid=(count, KH // 2),...  3.1 us
  transfers between devices with their start and end apart: 25, of which 12 were waited for; matrix products, arithmetic and copies ran while one was open for 0% of the time, Pallas kernels for 14%

profile of v4, /device:TPU:0, one launch (start us, length us, event | category | flops | bytes accessed | tf_op | source)
XLA Modules:
  0.0 94.5 jit_solution(13695489385631109796)
XLA Ops:
  0.6 4.9 %collective-permute-start = (bf16[256,256]{1,0:T(8,128)(2,1)}, bf16[256,256]{1,0:T(8,128)(2,1)S(1)}, u32[]{:S(2)}, u32[]{:S(2)}) collective-permute-start(bf16[256,256]{1,0:T(8,128)(2,1)} %bitcast.19), channel_id=1, source_target_pairs={{0,2},{2,4},{4,6},{6,8},{8,10},{10,12},{12,14},{14,16},{16,18},{18... | collective-permute-start | bytes 393224 | tf_op jit(solution)/shard_map/ppermute | solution.py:36
  5.5 1.7 %load.1 = (bf16[256,256]{1,0:T(8,128)(2,1)S(1)}, bf16[256,2048]{1,0:T(8,128)(2,1)S(1)}, bf16[256,2048]{1,0:T(8,128)(2,1)S(1)}, s32[2,1,128]{2,1,0:T(1,128)S(1)}) custom-call(bf16[256,256]{1,0:T(8,128)(2,1)} %bitcast.20, bf16[256,2048]{1,0:T(8,128)(2,1)} %bitcast.13, bf16[256,2048]{1,0:T(8,128)(2,1)} %bitcast.14, s32[2,1,128]{2,1,0:T(1,128)} %bitcast.21), custom_call_target="tpu_custom_call" | custom-call | tf_op jit(solution)/shard_map/load/pallas_call | solution.py:282
  7.2 1.4 %collective-permute-done.prev = bf16[256,256]{1,0:T(8,128)(2,1)S(1)} collective-permute-done((bf16[256,256]{1,0:T(8,128)(2,1)}, bf16[256,256]{1,0:T(8,128)(2,1)S(1)}, u32[]{:S(2)}, u32[]{:S(2)}) %collective-permute-start) | collective-permute-done | bytes 131104 | tf_op jit(solution)/shard_map/ppermute | solution.py:36
  8.6 3.5 %shard_map.129 = (bf16[1,32,256,128]{3,2,1,0:T(8,128)(2,1)S(1)}, bf16[128,256]{1,0:T(8,128)(2,1)S(1)}, f32[128,256]{1,0:T(8,128)S(1)}) custom-call(s32[32]{0:T(128)S(1)} %copy-done, s32[2,1,128]{2,1,0:T(1,128)S(1)} %get-tuple-element.35.pos, bf16[256,2048]{1,0:T(8,128)(2,1)S(1)} %get-tuple-element.36.query, bf16[256,2048]{1,0:T(8,128)(2,1)S(1)} %get-tuple-element.37.cotan, ...), custom_call_target="tpu_custom_call" | custom-call | tf_op jit(solution)/shard_map/pallas_call | solution.py:159
  12.1 1.3 %collective-permute-start.11 = (bf16[128,256]{1,0:T(8,128)(2,1)S(1)}, bf16[128,256]{1,0:T(8,128)(2,1)S(1)}, u32[]{:S(2)}, u32[]{:S(2)}) collective-permute-start(bf16[128,256]{1,0:T(8,128)(2,1)S(1)} %get-tuple-element.55), channel_id=1, source_target_pairs={{2,0},{4,2},{6,4},{8,6},{10,8},{12,10},{14,12},{16,14},{18,16},{20... | collective-permute-start | bytes 196616 | tf_op jit(solution)/shard_map/ppermute | solution.py:36
  13.4 1.8 %cut.1 = (bf16[4,184,256]{2,1,0:T(8,128)(2,1)S(1)}, bf16[4,184,256]{2,1,0:T(8,128)(2,1)S(1)}, bf16[4,184,256]{2,1,0:T(8,128)(2,1)S(1)}, bf16[4,184,256]{2,1,0:T(8,128)(2,1)S(1)}, bf16[184,256]{1,0:T(8,128)(2,1)S(1)}) custom-call(bf16[2880,256]{1,0:T(8,128)(2,1)} %bitcast.12, f32[180,1,256]{2,1,0:T(1,128)} %bitcast.15), custom_call_target="tpu_custom_call" | custom-call | tf_op jit(solution)/shard_map/cut/pallas_call | solution.py:252
  15.2 3.1 %collective-permute-start.1 = (bf16[4,184,256]{2,1,0:T(8,128)(2,1)S(1)}, bf16[4,184,256]{2,1,0:T(8,128)(2,1)S(1)}, u32[]{:S(2)}, u32[]{:S(2)}) collective-permute-start(bf16[4,184,256]{2,1,0:T(8,128)(2,1)S(1)} %get-tuple-element.41), channel_id=1, source_target_pairs={{0,2},{2,0},{4,6},{6,4},{8,10},{10,8},{12,14},{14,12},{16,18},{18,... | collective-permute-start | bytes 1130504 | tf_op jit(solution)/shard_map/ppermute | solution.py:30
  18.3 2.9 %collective-permute-start.2 = (bf16[4,184,256]{2,1,0:T(8,128)(2,1)S(1)}, bf16[4,184,256]{2,1,0:T(8,128)(2,1)S(1)}, u32[]{:S(2)}, u32[]{:S(2)}) collective-permute-start(bf16[4,184,256]{2,1,0:T(8,128)(2,1)S(1)} %get-tuple-element.42), channel_id=1, source_target_pairs={{0,4},{2,6},{4,0},{6,2},{8,12},{10,14},{12,8},{14,10},{16,20},{18,... | collective-permute-start | bytes 1130504 | tf_op jit(solution)/shard_map/ppermute | solution.py:30
  21.2 3.5 %shard_map.130 = (bf16[1,32,256,128]{3,2,1,0:T(8,128)(2,1)S(1)}, f32[256,256]{1,0:T(8,128)S(1)}) custom-call(s32[32]{0:T(128)S(1)} %copy-done, s32[2,1,128]{2,1,0:T(1,128)S(1)} %get-tuple-element.35.pos, bf16[256,2048]{1,0:T(8,128)(2,1)S(1)} %get-tuple-element.36.query, bf16[256,2048]{1,0:T(8,128)(2,1)S(1)} %get-tuple-element.37.cotan, ...), custom_call_target="tpu_custom_call" | custom-call | tf_op jit(solution)/shard_map/pallas_call | solution.py:159
  24.7 0.0 collective-permute-done.11
  24.8 1.5 %collective-permute-start.12 = (bf16[256,256]{1,0:T(8,128)(2,1)S(1)}, bf16[256,256]{1,0:T(8,128)(2,1)S(1)}, u32[]{:S(2)}, u32[]{:S(2)}) collective-permute-start(bf16[256,256]{1,0:T(8,128)(2,1)S(1)} %pad_maximum_fusion.refs_4_), channel_id=1, source_target_pairs={{0,2},{2,0},{4,6},{6,4},{8,10},{10,8},{12,14},{14,12},{16,18},{18,... | collective-permute-start | bytes 393224 | tf_op jit(solution)/shard_map/ppermute | solution.py:30
  26.3 2.0 %collective-permute-start.13 = (bf16[256,256]{1,0:T(8,128)(2,1)S(1)}, bf16[256,256]{1,0:T(8,128)(2,1)S(1)}, u32[]{:S(2)}, u32[]{:S(2)}) collective-permute-start(bf16[256,256]{1,0:T(8,128)(2,1)S(1)} %pad_maximum_fusion.refs_4_), channel_id=1, source_target_pairs={{0,4},{2,6},{4,0},{6,2},{8,12},{10,14},{12,8},{14,10},{16,20},{18,... | collective-permute-start | bytes 393224 | tf_op jit(solution)/shard_map/ppermute | solution.py:30
  28.4 9.4 %collective-permute-done.12.refs_5_ = bf16[256,256]{1,0:T(8,128)(2,1)S(1)} collective-permute-done((bf16[256,256]{1,0:T(8,128)(2,1)S(1)}, bf16[256,256]{1,0:T(8,128)(2,1)S(1)}, u32[]{:S(2)}, u32[]{:S(2)}) %collective-permute-start.12) | collective-permute-done | bytes 131104 | tf_op jit(solution)/shard_map/ppermute | solution.py:30
  37.7 3.2 %collective-permute-start.14 = (bf16[256,256]{1,0:T(8,128)(2,1)S(1)}, bf16[256,256]{1,0:T(8,128)(2,1)S(1)}, u32[]{:S(2)}, u32[]{:S(2)}) collective-permute-start(bf16[256,256]{1,0:T(8,128)(2,1)S(1)} %pad_maximum_fusion.refs_4_), channel_id=1, source_target_pairs={{0,6},{2,4},{4,2},{6,0},{8,14},{10,12},{12,10},{14,8},{16,22},{18,... | collective-permute-start | bytes 393224 | tf_op jit(solution)/shard_map/ppermute | solution.py:30
  41.6 1.3 %pack.1 = (f32[3,180,256]{2,1,0:T(8,128)S(1)}, f32[8,256]{1,0:T(8,128)S(1)}) custom-call(s32[1]{0:T(128)S(6)} %copy.16.step, f32[180,1,256]{2,1,0:T(1,128)} %bitcast.16, f32[180,1,256]{2,1,0:T(1,128)} %bitcast.17, f32[180,1,256]{2,1,0:T(1,128)} %bitcast.18), custom_call_target="tpu_custom_call" | custom-call | tf_op jit(solution)/shard_map/pack/pallas_call | solution.py:414
  42.9 0.1 collective-permute-start.24
  43.0 0.9 collective-permute-done.14.refs_7_
  43.9 3.5 %collective-permute-start.4 = (bf16[184,256]{1,0:T(8,128)(2,1)S(1)}, bf16[184,256]{1,0:T(8,128)(2,1)S(1)}, u32[]{:S(2)}, u32[]{:S(2)}) collective-permute-start(bf16[184,256]{1,0:T(8,128)(2,1)S(1)} %get-tuple-element.44.refs_4_), channel_id=1, source_target_pairs={{0,8},{2,10},{4,12},{6,14},{8,0},{10,2},{12,4},{14,6},{16,24},{18,... | collective-permute-start | bytes 282632 | tf_op jit(solution)/shard_map/ppermute | solution.py:30
  47.4 2.6 %collective-permute-start.5 = (bf16[184,256]{1,0:T(8,128)(2,1)S(1)}, bf16[184,256]{1,0:T(8,128)(2,1)S(1)}, u32[]{:S(2)}, u32[]{:S(2)}) collective-permute-start(bf16[184,256]{1,0:T(8,128)(2,1)S(1)} %get-tuple-element.44.refs_4_), channel_id=1, source_target_pairs={{0,16},{2,18},{4,20},{6,22},{8,24},{10,26},{12,28},{14,30},{16,0},... | collective-permute-start | bytes 282632 | tf_op jit(solution)/shard_map/ppermute | solution.py:30
  50.0 0.7 outer.1
  50.7 0.9 %collective-permute-start.15 = (bf16[180,256]{1,0:T(8,128)(2,1)S(1)}, bf16[180,256]{1,0:T(8,128)(2,1)S(1)}, u32[]{:S(2)}, u32[]{:S(2)}) collective-permute-start(bf16[180,256]{1,0:T(8,128)(2,1)S(1)} %get-tuple-element.57), channel_id=1, source_target_pairs={{0,8},{2,10},{4,12},{6,14},{8,0},{10,2},{12,4},{14,6},{16,24},{18,... | collective-permute-start | bytes 276488 | tf_op jit(solution)/shard_map/ppermute | solution.py:30
  51.6 3.5 %collective-permute-start.16 = (bf16[180,256]{1,0:T(8,128)(2,1)S(1)}, bf16[180,256]{1,0:T(8,128)(2,1)S(1)}, u32[]{:S(2)}, u32[]{:S(2)}) collective-permute-start(bf16[180,256]{1,0:T(8,128)(2,1)S(1)} %get-tuple-element.58), channel_id=1, source_target_pairs={{0,16},{2,18},{4,20},{6,22},{8,24},{10,26},{12,28},{14,30},{16,0},... | collective-permute-start | bytes 276488 | tf_op jit(solution)/shard_map/ppermute | solution.py:30
  55.1 0.3 collective-permute-done.5.refs_6_
  55.5 1.9 %collective-permute-done.6.refs_7_ = bf16[184,256]{1,0:T(8,128)(2,1)S(1)} collective-permute-done((bf16[184,256]{1,0:T(8,128)(2,1)S(1)}, bf16[184,256]{1,0:T(8,128)(2,1)S(1)}, u32[]{:S(2)}, u32[]{:S(2)}) %collective-permute-start.6) | collective-permute-done | bytes 94240 | tf_op jit(solution)/shard_map/ppermute | solution.py:30
  57.4 0.8 value.1
  58.2 1.5 %collective-permute-start.7 = (f32[256,256]{1,0:T(8,128)S(1)}, f32[256,256]{1,0:T(8,128)S(1)}, u32[]{:S(2)}, u32[]{:S(2)}) collective-permute-start(f32[256,256]{1,0:T(8,128)S(1)} %get-tuple-element.46), channel_id=1, source_target_pairs={{0,2},{2,0},{4,6},{6,4},{8,10},{10,8},{12,14},{14,12},{16,18},{18,... | collective-permute-start | bytes 786440 | tf_op jit(solution)/shard_map/ppermute | solution.py:30
  59.6 0.7 collective-permute-start.8
  60.3 1.4 %collective-permute-start.9 = (f32[256,256]{1,0:T(8,128)S(1)}, f32[256,256]{1,0:T(8,128)S(1)}, u32[]{:S(2)}, u32[]{:S(2)}) collective-permute-start(f32[256,256]{1,0:T(8,128)S(1)} %get-tuple-element.48), channel_id=1, source_target_pairs={{0,6},{2,4},{4,2},{6,0},{8,14},{10,12},{12,10},{14,8},{16,22},{18,... | collective-permute-start | bytes 786440 | tf_op jit(solution)/shard_map/ppermute | solution.py:30
  61.7 2.4 %collective-permute-start.17 = (bf16[180,256]{1,0:T(8,128)(2,1)S(1)}, bf16[180,256]{1,0:T(8,128)(2,1)S(1)}, u32[]{:S(2)}, u32[]{:S(2)}) collective-permute-start(bf16[180,256]{1,0:T(8,128)(2,1)S(1)} %get-tuple-element.59), channel_id=1, source_target_pairs={{0,24},{2,26},{4,28},{6,30},{8,16},{10,18},{12,20},{14,22},{16,8},... | collective-permute-start | bytes 276488 | tf_op jit(solution)/shard_map/ppermute | solution.py:30
  64.1 4.0 %collective-permute-done.17.refs_2_ = bf16[180,256]{1,0:T(8,128)(2,1)S(1)} collective-permute-done((bf16[180,256]{1,0:T(8,128)(2,1)S(1)}, bf16[180,256]{1,0:T(8,128)(2,1)S(1)}, u32[]{:S(2)}, u32[]{:S(2)}) %collective-permute-start.17) | collective-permute-done | bytes 92192 | tf_op jit(solution)/shard_map/ppermute | solution.py:30
  68.1 0.2 reduce.1
  68.4 0.1 collective-permute-start.23
  68.4 1.0 %collective-permute-done.8.refs_2_ = f32[256,256]{1,0:T(8,128)S(1)} collective-permute-done((f32[256,256]{1,0:T(8,128)S(1)}, f32[256,256]{1,0:T(8,128)S(1)}, u32[]{:S(2)}, u32[]{:S(2)}) %collective-permute-start.8) | collective-permute-done | bytes 262176 | tf_op jit(solution)/shard_map/ppermute | solution.py:30
  69.4 0.1 join.1
  69.5 2.7 %collective-permute-start.10 = (bf16[128,256]{1,0:T(8,128)(2,1)S(1)}, bf16[128,256]{1,0:T(8,128)(2,1)S(1)}, u32[]{:S(2)}, u32[]{:S(2)}) collective-permute-start(bf16[128,256]{1,0:T(8,128)(2,1)S(1)} %get-tuple-element.49), channel_id=1, source_target_pairs={{0,2},{2,4},{4,6},{6,8},{8,10},{10,12},{12,14},{14,16},{16,18},{18... | collective-permute-start | bytes 196616 | tf_op jit(solution)/shard_map/ppermute | solution.py:36
  72.2 0.1 collective-permute-start.18
  72.3 1.1 %collective-permute-done.18 = f32[1,128]{1,0:T(1,128)S(1)} collective-permute-done((f32[1,128]{1,0:T(1,128)S(1)}, f32[1,128]{1,0:T(1,128)S(1)}, u32[]{:S(2)}, u32[]{:S(2)}) %collective-permute-start.18) | collective-permute-done | bytes 544 | tf_op jit(solution)/shard_map/ppermute | solution.py:30
  73.5 4.4 %collective-permute-start.19 = (f32[1,128]{1,0:T(1,128)S(1)}, f32[1,128]{1,0:T(1,128)S(1)}, u32[]{:S(2)}, u32[]{:S(2)}) collective-permute-start(f32[1,128]{1,0:T(1,128)S(1)} %add.23), channel_id=1, source_target_pairs={{0,16},{2,18},{4,20},{6,22},{8,24},{10,26},{12,28},{14,30},{16,0},... | collective-permute-start | bytes 1544 | tf_op jit(solution)/shard_map/ppermute | solution.py:30
  77.9 1.5 %collective-permute-done.19 = f32[1,128]{1,0:T(1,128)S(1)} collective-permute-done((f32[1,128]{1,0:T(1,128)S(1)}, f32[1,128]{1,0:T(1,128)S(1)}, u32[]{:S(2)}, u32[]{:S(2)}) %collective-permute-start.19) | collective-permute-done | bytes 544 | tf_op jit(solution)/shard_map/ppermute | solution.py:30
  79.5 1.6 %collective-permute-start.20 = (f32[1,128]{1,0:T(1,128)S(1)}, f32[1,128]{1,0:T(1,128)S(1)}, u32[]{:S(2)}, u32[]{:S(2)}) collective-permute-start(f32[1,128]{1,0:T(1,128)S(1)} %add.24), channel_id=1, source_target_pairs={{0,8},{2,10},{4,12},{6,14},{8,0},{10,2},{12,4},{14,6},{16,24},{18,... | collective-permute-start | bytes 1544 | tf_op jit(solution)/shard_map/ppermute | solution.py:30
  81.1 1.9 %collective-permute-done.20 = f32[1,128]{1,0:T(1,128)S(1)} collective-permute-done((f32[1,128]{1,0:T(1,128)S(1)}, f32[1,128]{1,0:T(1,128)S(1)}, u32[]{:S(2)}, u32[]{:S(2)}) %collective-permute-start.20) | collective-permute-done | bytes 544 | tf_op jit(solution)/shard_map/ppermute | solution.py:30
  83.0 1.7 %collective-permute-start.21 = (f32[1,128]{1,0:T(1,128)S(1)}, f32[1,128]{1,0:T(1,128)S(1)}, u32[]{:S(2)}, u32[]{:S(2)}) collective-permute-start(f32[1,128]{1,0:T(1,128)S(1)} %add.25), channel_id=1, source_target_pairs={{0,4},{2,6},{4,0},{6,2},{8,12},{10,14},{12,8},{14,10},{16,20},{18,... | collective-permute-start | bytes 1544 | tf_op jit(solution)/shard_map/ppermute | solution.py:30
  84.8 1.8 %collective-permute-done.21 = f32[1,128]{1,0:T(1,128)S(1)} collective-permute-done((f32[1,128]{1,0:T(1,128)S(1)}, f32[1,128]{1,0:T(1,128)S(1)}, u32[]{:S(2)}, u32[]{:S(2)}) %collective-permute-start.21) | collective-permute-done | bytes 544 | tf_op jit(solution)/shard_map/ppermute | solution.py:30
  86.6 2.0 %collective-permute-start.22 = (f32[1,128]{1,0:T(1,128)S(1)}, f32[1,128]{1,0:T(1,128)S(1)}, u32[]{:S(2)}, u32[]{:S(2)}) collective-permute-start(f32[1,128]{1,0:T(1,128)S(1)} %add.26), channel_id=1, source_target_pairs={{0,2},{2,0},{4,6},{6,4},{8,10},{10,8},{12,14},{14,12},{16,18},{18,... | collective-permute-start | bytes 1544 | tf_op jit(solution)/shard_map/ppermute | solution.py:30
  88.6 1.6 %collective-permute-done.22 = f32[1,128]{1,0:T(1,128)S(1)} collective-permute-done((f32[1,128]{1,0:T(1,128)S(1)}, f32[1,128]{1,0:T(1,128)S(1)}, u32[]{:S(2)}, u32[]{:S(2)}) %collective-permute-start.22) | collective-permute-done | bytes 544 | tf_op jit(solution)/shard_map/ppermute | solution.py:30
  90.2 1.5 %shard_map.131.refs_0_ = bf16[256,2048]{1,0:T(8,128)(2,1)} custom-call(bf16[1,32,256,128]{3,2,1,0:T(8,128)(2,1)S(1)} %get-tuple-element.51.probs, bf16[256,256]{1,0:T(8,128)(2,1)S(1)} %get-tuple-element.50.lower.values, bf16[256,256]{1,0:T(8,128)(2,1)S(1)} %get-tuple-element.50.lower.values), custom_call_target="tpu_custom_call" | custom-call | tf_op jit(solution)/shard_map/pallas_call | solution.py:201
  91.7 1.3 %adam.1 = (f32[180,256]{1,0:T(8,128)}, f32[180,256]{1,0:T(8,128)}, f32[180,256]{1,0:T(8,128)}) custom-call(f32[8,256]{1,0:T(8,128)S(1)} %get-tuple-element.52.fixes, f32[1,128]{1,0:T(1,128)S(1)} %add.27.squares, f32[180,256]{1,0:T(8,128)S(1)} %get-tuple-element.61.refs_0_, f32[180,256]{1,0:T(8,128)S(1)} %collective-permute-done.23.refs_1_, ...), custom_call_target="tpu_custom_call" | custom-call | tf_op jit(solution)/shard_map/adam/pallas_call | solution.py:456
  93.0 1.5 %shard_map.132 = bf16[256,2048]{1,0:T(8,128)(2,1)} custom-call(bf16[1,32,256,128]{3,2,1,0:T(8,128)(2,1)S(1)} %get-tuple-element.39.probs, bf16[128,256]{1,0:T(8,128)(2,1)S(1)} %collective-permute-done.10.lower, bf16[256,256]{1,0:T(8,128)(2,1)S(1)} %get-tuple-element.50.lower.values, bf16[256,2048]{1,0:T(8,128)(2,1)} %shard_map.131.refs_0_), custom_call_target="tpu_custom_call", output_to_operand_aliasing={{}: (3, {})} | custom-call | tf_op jit(solution)/shard_map/pallas_call | solution.py:201
  (23 shorter events, 0.1 us)
Async XLA Ops:
  0.6 7.9 %copy-start = (s32[32]{0:T(128)S(1)}, s32[32]{0:T(128)}, u32[]{:S(2)}) copy-start(s32[32]{0:T(128)} %bands.3) | copy-start | bytes 388
  0.6 7.9 %collective-permute-start = (bf16[256,256]{1,0:T(8,128)(2,1)}, bf16[256,256]{1,0:T(8,128)(2,1)S(1)}, u32[]{:S(2)}, u32[]{:S(2)}) collective-permute-start(bf16[256,256]{1,0:T(8,128)(2,1)} %bitcast.19), channel_id=1, source_target_pairs={{0,2},{2,4},{4,6},{6,8},{8,10},{10,12},{12,14},{14,16},{16,18},{18... | collective-permute-start | bytes 393224 | tf_op jit(solution)/shard_map/ppermute | solution.py:36
  12.1 12.6 %collective-permute-start.11 = (bf16[128,256]{1,0:T(8,128)(2,1)S(1)}, bf16[128,256]{1,0:T(8,128)(2,1)S(1)}, u32[]{:S(2)}, u32[]{:S(2)}) collective-permute-start(bf16[128,256]{1,0:T(8,128)(2,1)S(1)} %get-tuple-element.55), channel_id=1, source_target_pairs={{2,0},{4,2},{6,4},{8,6},{10,8},{12,10},{14,12},{16,14},{18,16},{20... | collective-permute-start | bytes 196616 | tf_op jit(solution)/shard_map/ppermute | solution.py:36
  15.2 32.2 %collective-permute-start.1 = (bf16[4,184,256]{2,1,0:T(8,128)(2,1)S(1)}, bf16[4,184,256]{2,1,0:T(8,128)(2,1)S(1)}, u32[]{:S(2)}, u32[]{:S(2)}) collective-permute-start(bf16[4,184,256]{2,1,0:T(8,128)(2,1)S(1)} %get-tuple-element.41), channel_id=1, source_target_pairs={{0,2},{2,0},{4,6},{6,4},{8,10},{10,8},{12,14},{14,12},{16,18},{18,... | collective-permute-start | bytes 1130504 | tf_op jit(solution)/shard_map/ppermute | solution.py:30
  18.3 31.7 %collective-permute-start.2 = (bf16[4,184,256]{2,1,0:T(8,128)(2,1)S(1)}, bf16[4,184,256]{2,1,0:T(8,128)(2,1)S(1)}, u32[]{:S(2)}, u32[]{:S(2)}) collective-permute-start(bf16[4,184,256]{2,1,0:T(8,128)(2,1)S(1)} %get-tuple-element.42), channel_id=1, source_target_pairs={{0,4},{2,6},{4,0},{6,2},{8,12},{10,14},{12,8},{14,10},{16,20},{18,... | collective-permute-start | bytes 1130504 | tf_op jit(solution)/shard_map/ppermute | solution.py:30
  21.2 28.8 %collective-permute-start.3 = (bf16[4,184,256]{2,1,0:T(8,128)(2,1)S(1)}, bf16[4,184,256]{2,1,0:T(8,128)(2,1)S(1)}, u32[]{:S(2)}, u32[]{:S(2)}) collective-permute-start(bf16[4,184,256]{2,1,0:T(8,128)(2,1)S(1)} %get-tuple-element.43), channel_id=1, source_target_pairs={{0,6},{2,4},{4,2},{6,0},{8,14},{10,12},{12,10},{14,8},{16,22},{18,... | collective-permute-start | bytes 1130504 | tf_op jit(solution)/shard_map/ppermute | solution.py:30
  24.8 12.9 %collective-permute-start.12 = (bf16[256,256]{1,0:T(8,128)(2,1)S(1)}, bf16[256,256]{1,0:T(8,128)(2,1)S(1)}, u32[]{:S(2)}, u32[]{:S(2)}) collective-permute-start(bf16[256,256]{1,0:T(8,128)(2,1)S(1)} %pad_maximum_fusion.refs_4_), channel_id=1, source_target_pairs={{0,2},{2,0},{4,6},{6,4},{8,10},{10,8},{12,14},{14,12},{16,18},{18,... | collective-permute-start | bytes 393224 | tf_op jit(solution)/shard_map/ppermute | solution.py:30
  26.3 16.6 %collective-permute-start.13 = (bf16[256,256]{1,0:T(8,128)(2,1)S(1)}, bf16[256,256]{1,0:T(8,128)(2,1)S(1)}, u32[]{:S(2)}, u32[]{:S(2)}) collective-permute-start(bf16[256,256]{1,0:T(8,128)(2,1)S(1)} %pad_maximum_fusion.refs_4_), channel_id=1, source_target_pairs={{0,4},{2,6},{4,0},{6,2},{8,12},{10,14},{12,8},{14,10},{16,20},{18,... | collective-permute-start | bytes 393224 | tf_op jit(solution)/shard_map/ppermute | solution.py:30
  37.7 6.2 %collective-permute-start.14 = (bf16[256,256]{1,0:T(8,128)(2,1)S(1)}, bf16[256,256]{1,0:T(8,128)(2,1)S(1)}, u32[]{:S(2)}, u32[]{:S(2)}) collective-permute-start(bf16[256,256]{1,0:T(8,128)(2,1)S(1)} %pad_maximum_fusion.refs_4_), channel_id=1, source_target_pairs={{0,6},{2,4},{4,2},{6,0},{8,14},{10,12},{12,10},{14,8},{16,22},{18,... | collective-permute-start | bytes 393224 | tf_op jit(solution)/shard_map/ppermute | solution.py:30
  42.9 48.8 %collective-permute-start.24 = (f32[3,180,256]{2,1,0:T(8,128)S(1)}, f32[3,180,256]{2,1,0:T(8,128)S(1)}, u32[]{:S(2)}, u32[]{:S(2)}) collective-permute-start(f32[3,180,256]{2,1,0:T(8,128)S(1)} %get-tuple-element.62.refs_2_), channel_id=1, source_target_pairs={{0,1},{1,0},{2,3},{3,2},{4,5},{5,4},{6,7},{7,6},{8,9},{9,8},{10,11... | collective-permute-start | bytes 1658888 | tf_op jit(solution)/shard_map/ppermute | solution.py:30
  43.9 7.7 %collective-permute-start.4 = (bf16[184,256]{1,0:T(8,128)(2,1)S(1)}, bf16[184,256]{1,0:T(8,128)(2,1)S(1)}, u32[]{:S(2)}, u32[]{:S(2)}) collective-permute-start(bf16[184,256]{1,0:T(8,128)(2,1)S(1)} %get-tuple-element.44.refs_4_), channel_id=1, source_target_pairs={{0,8},{2,10},{4,12},{6,14},{8,0},{10,2},{12,4},{14,6},{16,24},{18,... | collective-permute-start | bytes 282632 | tf_op jit(solution)/shard_map/ppermute | solution.py:30
  47.4 8.1 %collective-permute-start.5 = (bf16[184,256]{1,0:T(8,128)(2,1)S(1)}, bf16[184,256]{1,0:T(8,128)(2,1)S(1)}, u32[]{:S(2)}, u32[]{:S(2)}) collective-permute-start(bf16[184,256]{1,0:T(8,128)(2,1)S(1)} %get-tuple-element.44.refs_4_), channel_id=1, source_target_pairs={{0,16},{2,18},{4,20},{6,22},{8,24},{10,26},{12,28},{14,30},{16,0},... | collective-permute-start | bytes 282632 | tf_op jit(solution)/shard_map/ppermute | solution.py:30
  50.0 7.4 %collective-permute-start.6 = (bf16[184,256]{1,0:T(8,128)(2,1)S(1)}, bf16[184,256]{1,0:T(8,128)(2,1)S(1)}, u32[]{:S(2)}, u32[]{:S(2)}) collective-permute-start(bf16[184,256]{1,0:T(8,128)(2,1)S(1)} %get-tuple-element.44.refs_4_), channel_id=1, source_target_pairs={{0,24},{2,26},{4,28},{6,30},{8,16},{10,18},{12,20},{14,22},{16,8},... | collective-permute-start | bytes 282632 | tf_op jit(solution)/shard_map/ppermute | solution.py:30
  50.7 9.7 %collective-permute-start.15 = (bf16[180,256]{1,0:T(8,128)(2,1)S(1)}, bf16[180,256]{1,0:T(8,128)(2,1)S(1)}, u32[]{:S(2)}, u32[]{:S(2)}) collective-permute-start(bf16[180,256]{1,0:T(8,128)(2,1)S(1)} %get-tuple-element.57), channel_id=1, source_target_pairs={{0,8},{2,10},{4,12},{6,14},{8,0},{10,2},{12,4},{14,6},{16,24},{18,... | collective-permute-start | bytes 276488 | tf_op jit(solution)/shard_map/ppermute | solution.py:30
  51.6 10.1 %collective-permute-start.16 = (bf16[180,256]{1,0:T(8,128)(2,1)S(1)}, bf16[180,256]{1,0:T(8,128)(2,1)S(1)}, u32[]{:S(2)}, u32[]{:S(2)}) collective-permute-start(bf16[180,256]{1,0:T(8,128)(2,1)S(1)} %get-tuple-element.58), channel_id=1, source_target_pairs={{0,16},{2,18},{4,20},{6,22},{8,24},{10,26},{12,28},{14,30},{16,0},... | collective-permute-start | bytes 276488 | tf_op jit(solution)/shard_map/ppermute | solution.py:30
  58.2 10.3 %collective-permute-start.7 = (f32[256,256]{1,0:T(8,128)S(1)}, f32[256,256]{1,0:T(8,128)S(1)}, u32[]{:S(2)}, u32[]{:S(2)}) collective-permute-start(f32[256,256]{1,0:T(8,128)S(1)} %get-tuple-element.46), channel_id=1, source_target_pairs={{0,2},{2,0},{4,6},{6,4},{8,10},{10,8},{12,14},{14,12},{16,18},{18,... | collective-permute-start | bytes 786440 | tf_op jit(solution)/shard_map/ppermute | solution.py:30
  59.6 9.8 %collective-permute-start.8 = (f32[256,256]{1,0:T(8,128)S(1)}, f32[256,256]{1,0:T(8,128)S(1)}, u32[]{:S(2)}, u32[]{:S(2)}) collective-permute-start(f32[256,256]{1,0:T(8,128)S(1)} %get-tuple-element.47), channel_id=1, source_target_pairs={{0,4},{2,6},{4,0},{6,2},{8,12},{10,14},{12,8},{14,10},{16,20},{18,... | collective-permute-start | bytes 786440 | tf_op jit(solution)/shard_map/ppermute | solution.py:30
  60.3 9.1 %collective-permute-start.9 = (f32[256,256]{1,0:T(8,128)S(1)}, f32[256,256]{1,0:T(8,128)S(1)}, u32[]{:S(2)}, u32[]{:S(2)}) collective-permute-start(f32[256,256]{1,0:T(8,128)S(1)} %get-tuple-element.48), channel_id=1, source_target_pairs={{0,6},{2,4},{4,2},{6,0},{8,14},{10,12},{12,10},{14,8},{16,22},{18,... | collective-permute-start | bytes 786440 | tf_op jit(solution)/shard_map/ppermute | solution.py:30
  61.7 6.4 %collective-permute-start.17 = (bf16[180,256]{1,0:T(8,128)(2,1)S(1)}, bf16[180,256]{1,0:T(8,128)(2,1)S(1)}, u32[]{:S(2)}, u32[]{:S(2)}) collective-permute-start(bf16[180,256]{1,0:T(8,128)(2,1)S(1)} %get-tuple-element.59), channel_id=1, source_target_pairs={{0,24},{2,26},{4,28},{6,30},{8,16},{10,18},{12,20},{14,22},{16,8},... | collective-permute-start | bytes 276488 | tf_op jit(solution)/shard_map/ppermute | solution.py:30
  68.4 23.4 %collective-permute-start.23 = (f32[180,256]{1,0:T(8,128)S(1)}, f32[180,256]{1,0:T(8,128)S(1)}, u32[]{:S(2)}, u32[]{:S(2)}) collective-permute-start(f32[180,256]{1,0:T(8,128)S(1)} %get-tuple-element.61.refs_0_), channel_id=1, source_target_pairs={{0,1},{1,0},{2,3},{3,2},{4,5},{5,4},{6,7},{7,6},{8,9},{9,8},{10,11... | collective-permute-start | bytes 552968 | tf_op jit(solution)/shard_map/ppermute | solution.py:30
  69.5 23.5 %collective-permute-start.10 = (bf16[128,256]{1,0:T(8,128)(2,1)S(1)}, bf16[128,256]{1,0:T(8,128)(2,1)S(1)}, u32[]{:S(2)}, u32[]{:S(2)}) collective-permute-start(bf16[128,256]{1,0:T(8,128)(2,1)S(1)} %get-tuple-element.49), channel_id=1, source_target_pairs={{0,2},{2,4},{4,6},{6,8},{8,10},{10,12},{12,14},{14,16},{16,18},{18... | collective-permute-start | bytes 196616 | tf_op jit(solution)/shard_map/ppermute | solution.py:36
  72.2 1.2 %collective-permute-start.18 = (f32[1,128]{1,0:T(1,128)S(1)}, f32[1,128]{1,0:T(1,128)S(1)}, u32[]{:S(2)}, u32[]{:S(2)}) collective-permute-start(f32[1,128]{1,0:T(1,128)S(1)} %get-tuple-element.60), channel_id=1, source_target_pairs={{0,1},{1,0},{2,3},{3,2},{4,5},{5,4},{6,7},{7,6},{8,9},{9,8},{10,11... | collective-permute-start | bytes 1544 | tf_op jit(solution)/shard_map/ppermute | solution.py:30
  73.5 6.0 %collective-permute-start.19 = (f32[1,128]{1,0:T(1,128)S(1)}, f32[1,128]{1,0:T(1,128)S(1)}, u32[]{:S(2)}, u32[]{:S(2)}) collective-permute-start(f32[1,128]{1,0:T(1,128)S(1)} %add.23), channel_id=1, source_target_pairs={{0,16},{2,18},{4,20},{6,22},{8,24},{10,26},{12,28},{14,30},{16,0},... | collective-permute-start | bytes 1544 | tf_op jit(solution)/shard_map/ppermute | solution.py:30
  79.5 3.6 %collective-permute-start.20 = (f32[1,128]{1,0:T(1,128)S(1)}, f32[1,128]{1,0:T(1,128)S(1)}, u32[]{:S(2)}, u32[]{:S(2)}) collective-permute-start(f32[1,128]{1,0:T(1,128)S(1)} %add.24), channel_id=1, source_target_pairs={{0,8},{2,10},{4,12},{6,14},{8,0},{10,2},{12,4},{14,6},{16,24},{18,... | collective-permute-start | bytes 1544 | tf_op jit(solution)/shard_map/ppermute | solution.py:30
  83.0 3.6 %collective-permute-start.21 = (f32[1,128]{1,0:T(1,128)S(1)}, f32[1,128]{1,0:T(1,128)S(1)}, u32[]{:S(2)}, u32[]{:S(2)}) collective-permute-start(f32[1,128]{1,0:T(1,128)S(1)} %add.25), channel_id=1, source_target_pairs={{0,4},{2,6},{4,0},{6,2},{8,12},{10,14},{12,8},{14,10},{16,20},{18,... | collective-permute-start | bytes 1544 | tf_op jit(solution)/shard_map/ppermute | solution.py:30
  86.6 3.6 %collective-permute-start.22 = (f32[1,128]{1,0:T(1,128)S(1)}, f32[1,128]{1,0:T(1,128)S(1)}, u32[]{:S(2)}, u32[]{:S(2)}) collective-permute-start(f32[1,128]{1,0:T(1,128)S(1)} %add.26), channel_id=1, source_target_pairs={{0,2},{2,0},{4,6},{6,4},{8,10},{10,8},{12,14},{14,12},{16,18},{18,... | collective-permute-start | bytes 1544 | tf_op jit(solution)/shard_map/ppermute | solution.py:30
